TPU v7x, 32 devices: a whole 2x2x4 slice. The times are simulated.
32 devices in a mesh: groups: 2 (over y), tiles: 8 (over z, x), subwin: 2 (over core).
Axes of the slice: x: 2, y: 2, z: 4, core: 2. Of those that a mesh axis runs over, the one named last changes fastest.
Arguments:
- increment: float32 [64, 8, 16, 16], P(('groups', 'tiles'), 'subwin'), parts along dimension 0, may hold values from -6 to 6
- dual_vector: float32 [64, 8, 16, 16], P(('groups', 'tiles'), 'subwin'), parts along dimension 0, may hold values from -6 to 6
- wind_u: float32 [32, 16, 16], P('tiles'), may hold values from -0.3 to 0.3
- wind_v: float32 [32, 16, 16], P('tiles'), may hold values from -0.3 to 0.3
- land_sea: int32 [32, 16], P('tiles'), may hold values from 0 to 1
- length_sq: float32 [8, 16], P('subwin', 'tiles'), may hold values from 1 to 300
- spread: float32 [8, 16], P('subwin'), may hold values from 0.5 to 3
Outputs:
- model_side: float32 [64, 8, 16, 16], P(('groups', 'tiles'), 'subwin'), parts along dimension 0
- dual_side: float32 [64, 8, 16, 16], P(('groups', 'tiles'), 'subwin'), parts along dimension 0
There are 2 independent parts, one for each index of `groups`. A program takes and returns all parts, laid end to end along the dimension named above; an argument that names none is the same for every part. Nothing has to cross between parts.
All inputs are finite; a program needn't handle non-finite values.
Results may differ from a plain program's by a relative error of at most 0.000098.
Values sent between devices are 32-bit elements; how exact they have to be, the bound alone decides.
No kernel may reach another device: no remote copies, remote signals or barrier semaphores. Data moves between devices by JAX's collectives and lax.ppermute only.
A program may use at most 192 MiB of HBM per device.

v0:
```python
import math

import jax
import jax.numpy as jnp
from jax import lax
from jax.sharding import PartitionSpec as P

STEPS = 8
SWEEPS = 4
LON_DEV = 4


def extended(x, sides, width):
    for axis, dim in sides:
        devices, length = (lax.axis_size(axis), x.shape[dim])
        up = [(i, (i + 1) % devices) for i in range(devices)]
        down = [(j, i) for i, j in up]
        last = lax.slice_in_dim(x, length - width, length, axis=dim)
        leading = lax.slice_in_dim(x, 0, width, axis=dim)
        before = lax.ppermute(last, axis, up)
        after = lax.ppermute(leading, axis, down)
        x = jnp.concatenate([before, x, after], axis=dim)
    return x


def passed_along(x, axis, by):
    devices = lax.axis_size(axis)
    pairs = [(i, i + by) for i in range(devices) if 0 <= i + by < devices]
    return lax.ppermute(x, axis, pairs)


def from_north(values):
    return jnp.concatenate([values[..., 1:], jnp.zeros_like(values[..., :1])], axis=-1)


def from_south(values):
    return jnp.concatenate([jnp.zeros_like(values[..., :1]), values[..., :-1]], axis=-1)


def coefficients(wind_u, wind_v, mixing):
    return (
        1.0 - 4.0 * mixing,
        mixing - 0.5 * wind_u,
        mixing + 0.5 * wind_u,
        mixing - 0.5 * wind_v,
        mixing + 0.5 * wind_v,
    )


def tangent_step(fields, coeffs, offset):
    extent = fields.shape[0]
    centre, eastward, westward, northward, southward = [
        coeff[offset + 1 : offset + extent - 1][:, None] for coeff in coeffs
    ]
    middle = fields[1:-1]
    return (
        centre * middle
        + eastward * fields[2:]
        + westward * fields[:-2]
        + northward * from_north(middle)
        + southward * from_south(middle)
    )


def adjoint_step(fields, coeffs, offset):
    extent = fields.shape[0]
    centre = coeffs[0][offset + 1 : offset + extent - 1][:, None]
    northward = coeffs[3][offset + 1 : offset + extent - 1][:, None]
    southward = coeffs[4][offset + 1 : offset + extent - 1][:, None]
    eastward = coeffs[1][offset : offset + extent][:, None]
    westward = coeffs[2][offset : offset + extent][:, None]
    middle = fields[1:-1]
    return (
        centre * middle
        + (eastward * fields)[:-2]
        + (westward * fields)[2:]
        + from_south(northward * middle)
        + from_north(southward * middle)
    )


def run_tangent(fields, coeffs, margin):
    for repeat in range(STEPS // margin):
        grown = extended(fields, (("tiles", 0),), margin)
        for inner_step in range(margin):
            offset = (coeffs[0].shape[0] - grown.shape[0]) // 2
            grown = tangent_step(grown, coeffs, offset)
        fields = grown
    return fields


def run_adjoint(fields, coeffs, margin):
    for repeat in range(STEPS // margin):
        grown = extended(fields, (("tiles", 0),), margin)
        for inner_step in range(margin):
            offset = (coeffs[0].shape[0] - grown.shape[0]) // 2
            grown = adjoint_step(grown, coeffs, offset)
        fields = grown
    return fields


def square_tables(extent):
    index = jnp.arange(extent, dtype=jnp.int32)
    phases = index[:, None] * index[None, :] % extent
    angles = phases.astype(jnp.float32) * (2.0 * math.pi / extent)
    return (jnp.cos(angles), jnp.sin(angles))


def contract(form, first, second):
    return jnp.einsum(form, first, second, precision=lax.Precision.HIGHEST)


def smooth_bands(bands, length_sq):
    count = bands.shape[0]
    inner = LON_DEV
    outer = count // inner
    columns = bands.reshape(outer, inner, -1)
    cos_outer, sin_outer = square_tables(outer)
    cos_inner, sin_inner = square_tables(inner)
    outer_index = jnp.arange(outer, dtype=jnp.int32)
    inner_index = jnp.arange(inner, dtype=jnp.int32)
    twist = (outer_index[:, None] * inner_index[None, :] % count).astype(jnp.float32) * (
        2.0 * math.pi / count
    )
    twist_cos = jnp.cos(twist)[:, :, None]
    twist_sin = jnp.sin(twist)[:, :, None]
    first_real = contract("ab,bqc->aqc", cos_outer, columns)
    first_imag = -contract("ab,bqc->aqc", sin_outer, columns)
    turned_real = first_real * twist_cos + first_imag * twist_sin
    turned_imag = first_imag * twist_cos - first_real * twist_sin
    modes_real = contract("aqc,kq->akc", turned_real, cos_inner) + contract(
        "aqc,kq->akc", turned_imag, sin_inner
    )
    modes_imag = contract("aqc,kq->akc", turned_imag, cos_inner) - contract(
        "aqc,kq->akc", turned_real, sin_inner
    )
    wave = (outer_index[:, None] + outer * inner_index[None, :]).astype(jnp.float32)
    basic = 1.0 - jnp.cos(wave * (2.0 * math.pi / count))
    damping = (1.0 + 2.0 * length_sq[None, None, :, None, :] * basic[:, :, None, None, None]) ** (
        -SWEEPS
    )
    damping = jnp.broadcast_to(damping, (outer, inner) + bands.shape[1:]).reshape(outer, inner, -1)
    modes_real = modes_real * damping
    modes_imag = modes_imag * damping
    back_real = contract("akc,kq->aqc", modes_real, cos_inner) - contract(
        "akc,kq->aqc", modes_imag, sin_inner
    )
    back_imag = contract("akc,kq->aqc", modes_imag, cos_inner) + contract(
        "akc,kq->aqc", modes_real, sin_inner
    )
    final_real = back_real * twist_cos - back_imag * twist_sin
    final_imag = back_imag * twist_cos + back_real * twist_sin
    smoothed = contract("ab,bqc->aqc", cos_outer, final_real) - contract(
        "ab,bqc->aqc", sin_outer, final_imag
    )
    return (smoothed / count).reshape(bands.shape)


def body(increment, dual_vector, wind_u, wind_v, land_sea, length_sq, spread):
    margin = 4
    mixing = 0.15 + 0.09 * land_sea.astype(jnp.float32)
    grown_u, grown_v, grown_mix = (
        extended(wind_u, (("tiles", 0),), margin),
        extended(wind_v, (("tiles", 0),), margin),
        extended(mixing, (("tiles", 0),), margin),
    )
    coeffs = coefficients(grown_u, grown_v, grown_mix[:, None, :])
    carried = passed_along(increment[:, -1:], "subwin", 1)
    previous = jnp.concatenate([carried, increment[:, :-1]], axis=1)
    later = passed_along(dual_vector[:, :1], "subwin", -1)
    following = jnp.concatenate([dual_vector[:, 1:], later], axis=1)
    weighted = dual_vector * spread[None, :, :, None]
    bands = lax.all_to_all(weighted, "tiles", split_axis=3, concat_axis=0, tiled=True)
    smoothed = smooth_bands(bands, length_sq)
    forward = run_tangent(previous, coeffs, margin)
    backward = run_adjoint(following, coeffs, margin)
    returned = lax.all_to_all(smoothed, "tiles", split_axis=0, concat_axis=3, tiled=True)
    covar = returned * spread[None, :, :, None]
    return (covar + increment - forward, dual_vector - backward)


def solution(mesh):
    placed = (
        P(("groups", "tiles"), "subwin", None, None),
        P(("groups", "tiles"), "subwin", None, None),
        P("tiles", None, None),
        P("tiles", None, None),
        P("tiles", None),
        P("subwin", "tiles"),
        P("subwin", None),
    )
    return jax.shard_map(
        body,
        mesh=mesh,
        in_specs=placed,
        out_specs=(
            P(("groups", "tiles"), "subwin", None, None),
            P(("groups", "tiles"), "subwin", None, None),
        ),
        check_vma=False,
    )
```

profile of v0, /device:TPU:0, one launch (start us, length us, event | category | flops | bytes accessed | tf_op | source)
XLA Modules:
  0.0 88.9 jit_solution(5874913392847764511)
XLA Ops:
  0.6 0.7 fusion.186
  1.3 3.0 %collective-permute-start = (f32[4,16]{1,0:T(4,128)S(1)}, f32[4,16]{1,0:T(4,128)S(1)}, u32[]{:S(2)}, u32[]{:S(2)}) collective-permute-start(f32[4,16]{1,0:T(4,128)S(1)} %get-tuple-element.69), channel_id=1, source_target_pairs={{0,2},{2,4},{4,6},{6,8},{8,10},{10,12},{12,14},{14,0},{1,3},{3,5},... | collective-permute-start | bytes 776 | tf_op jit(solution)/shard_map/ppermute | solution.py:20
  4.3 3.0 %collective-permute-start.1 = (f32[4,16]{1,0:T(4,128)S(1)}, f32[4,16]{1,0:T(4,128)S(1)}, u32[]{:S(2)}, u32[]{:S(2)}) collective-permute-start(f32[4,16]{1,0:T(4,128)S(1)} %get-tuple-element.69), channel_id=1, source_target_pairs={{2,0},{4,2},{6,4},{8,6},{10,8},{12,10},{14,12},{0,14},{3,1},{5,3},... | collective-permute-start | bytes 776 | tf_op jit(solution)/shard_map/ppermute | solution.py:21
  7.3 4.7 %collective-permute-start.6 = (f32[4,16,16]{2,1,0:T(8,128)}, f32[4,16,16]{2,1,0:T(8,128)S(1)}, u32[]{:S(2)}, u32[]{:S(2)}) collective-permute-start(f32[4,16,16]{2,1,0:T(8,128)} %param.9), channel_id=1, source_target_pairs={{2,0},{4,2},{6,4},{8,6},{10,8},{12,10},{14,12},{0,14},{3,1},{5,3},... | collective-permute-start | bytes 12296 | tf_op jit(solution)/shard_map/ppermute | solution.py:21
  12.1 1.0 %copy.123 = f32[4,4,16,16]{2,3,1,0:T(8,128)S(1)} copy(f32[4,4,16,16]{3,2,1,0:T(8,128)} %param.8) | data formatting | bytes 32768 | tf_op args[1]
  13.1 0.7 copy-done.6
  13.8 0.1 cosine_subtract_fusion
  14.2 0.6 copy-done.4
  14.8 4.7 %collective-permute-start.8 = (f32[4,16,16]{2,1,0:T(8,128)S(1)}, f32[4,16,16]{2,1,0:T(8,128)S(1)}, u32[]{:S(2)}, u32[]{:S(2)}) collective-permute-start(f32[4,16,16]{2,1,0:T(8,128)S(1)} %copy-done.4), channel_id=1, source_target_pairs={{2,0},{4,2},{6,4},{8,6},{10,8},{12,10},{14,12},{0,14},{3,1},{5,3},... | collective-permute-start | bytes 12296 | tf_op jit(solution)/shard_map/ppermute | solution.py:21
  19.6 1.3 %collective-permute-start.11 = (f32[4,1,16,16]{2,3,1,0:T(8,128)S(1)}, f32[4,1,16,16]{2,3,1,0:T(8,128)S(1)}, u32[]{:S(2)}, u32[]{:S(2)}) collective-permute-start(f32[4,1,16,16]{2,3,1,0:T(8,128)S(1)} %slice.551), channel_id=1, source_target_pairs={{1,0},{3,2},{5,4},{7,6},{9,8},{11,10},{13,12},{15,14},{17,16},{19,... | collective-permute-start | bytes 12296 | tf_op jit(solution)/shard_map/ppermute | solution.py:29
  20.9 1.7 %collective-permute-done.11 = f32[4,1,16,16]{2,3,1,0:T(8,128)S(1)} collective-permute-done((f32[4,1,16,16]{2,3,1,0:T(8,128)S(1)}, f32[4,1,16,16]{2,3,1,0:T(8,128)S(1)}, u32[]{:S(2)}, u32[]{:S(2)}) %collective-permute-start.11) | collective-permute-done | bytes 4128 | tf_op jit(solution)/shard_map/ppermute | solution.py:29
  22.6 2.1 %collective-permute-start.2 = (f32[4,1,16,16]{2,3,1,0:T(8,128)S(1)}, f32[4,1,16,16]{2,3,1,0:T(8,128)S(1)}, u32[]{:S(2)}, u32[]{:S(2)}) collective-permute-start(f32[4,1,16,16]{2,3,1,0:T(8,128)S(1)} %slice.492), channel_id=1, source_target_pairs={{0,1},{2,3},{4,5},{6,7},{8,9},{10,11},{12,13},{14,15},{16,17},{18,... | collective-permute-start | bytes 12296 | tf_op jit(solution)/shard_map/ppermute | solution.py:29
  24.7 0.8 collective-permute-done.2
  25.6 4.8 %collective-permute-start.13 = (f32[4,4,16,16]{2,3,1,0:T(8,128)S(1)}, f32[4,4,16,16]{2,3,1,0:T(8,128)S(1)}, u32[]{:S(2)}, u32[]{:S(2)}) collective-permute-start(f32[4,4,16,16]{2,3,1,0:T(8,128)S(1)} %pad_maximum_fusion.5), channel_id=1, source_target_pairs={{2,0},{4,2},{6,4},{8,6},{10,8},{12,10},{14,12},{0,14},{3,1},{5,3},... | collective-permute-start | bytes 49160 | tf_op jit(solution)/shard_map/ppermute | solution.py:21
  30.4 4.7 %collective-permute-start.4 = (f32[4,4,16,16]{2,3,1,0:T(8,128)S(1)}, f32[4,4,16,16]{2,3,1,0:T(8,128)S(1)}, u32[]{:S(2)}, u32[]{:S(2)}) collective-permute-start(f32[4,4,16,16]{2,3,1,0:T(8,128)S(1)} %pad_maximum_fusion.4), channel_id=1, source_target_pairs={{2,0},{4,2},{6,4},{8,6},{10,8},{12,10},{14,12},{0,14},{3,1},{5,3},... | collective-permute-start | bytes 49160 | tf_op jit(solution)/shard_map/ppermute | solution.py:21
  37.0 0.8 copy-done
  37.7 0.6 collective-permute-done.3
  38.3 1.5 %collective-permute-done.4 = f32[4,4,16,16]{2,3,1,0:T(8,128)S(1)} collective-permute-done((f32[4,4,16,16]{2,3,1,0:T(8,128)S(1)}, f32[4,4,16,16]{2,3,1,0:T(8,128)S(1)}, u32[]{:S(2)}, u32[]{:S(2)}) %collective-permute-start.4) | collective-permute-done | bytes 16416 | tf_op jit(solution)/shard_map/ppermute | solution.py:21
  39.9 0.9 %slice-done = f32[10,4,16,16]{2,3,1,0:T(8,128)S(1)} async-done(((f32[12,4,16,16]{2,3,1,0:T(8,128)}), f32[10,4,16,16]{2,3,1,0:T(8,128)S(1)}, s32[]{:S(2)}) %slice-start) | async-done | bytes 40984 | tf_op jit(solution)/shard_map/slice | solution.py:72
  40.9 0.9 %copy-done.1 = f32[12,4,16,16]{2,3,1,0:T(8,128)S(1)} copy-done((f32[12,4,16,16]{2,3,1,0:T(8,128)S(1)}, f32[12,4,16,16]{2,3,1,0:T(8,128)}, u32[]{:S(2)}) %copy-start.1) | copy-done | bytes 49176
  41.8 0.5 fusion.11
  42.5 0.4 fusion.27
  43.0 0.3 fusion.43
  43.3 0.2 fusion.60
  43.5 3.0 %collective-permute-start.10 = (f32[4,4,16,16]{2,3,1,0:T(8,128)S(1)}, f32[4,4,16,16]{2,3,1,0:T(8,128)S(1)}, u32[]{:S(2)}, u32[]{:S(2)}) collective-permute-start(f32[4,4,16,16]{2,3,1,0:T(8,128)S(1)} %get-tuple-element.67), channel_id=1, source_target_pairs={{2,0},{4,2},{6,4},{8,6},{10,8},{12,10},{14,12},{0,14},{3,1},{5,3},... | collective-permute-start | bytes 49160 | tf_op jit(solution)/shard_map/ppermute | solution.py:21
  46.7 4.8 %collective-permute-start.15 = (f32[4,4,16,16]{2,3,1,0:T(8,128)S(1)}, f32[4,4,16,16]{2,3,1,0:T(8,128)S(1)}, u32[]{:S(2)}, u32[]{:S(2)}) collective-permute-start(f32[4,4,16,16]{2,3,1,0:T(8,128)S(1)} %get-tuple-element.66), channel_id=1, source_target_pairs={{2,0},{4,2},{6,4},{8,6},{10,8},{12,10},{14,12},{0,14},{3,1},{5,3},... | collective-permute-start | bytes 49160 | tf_op jit(solution)/shard_map/ppermute | solution.py:21
  51.4 2.7 %collective-permute-done.9 = f32[4,4,16,16]{2,3,1,0:T(8,128)S(1)} collective-permute-done((f32[4,4,16,16]{2,3,1,0:T(8,128)S(1)}, f32[4,4,16,16]{2,3,1,0:T(8,128)S(1)}, u32[]{:S(2)}, u32[]{:S(2)}) %collective-permute-start.9) | collective-permute-done | bytes 16416 | tf_op jit(solution)/shard_map/ppermute | solution.py:20
  54.3 1.3 %collective-permute-done.14 = f32[4,4,16,16]{2,3,1,0:T(8,128)S(1)} collective-permute-done((f32[4,4,16,16]{2,3,1,0:T(8,128)S(1)}, f32[4,4,16,16]{2,3,1,0:T(8,128)S(1)}, u32[]{:S(2)}, u32[]{:S(2)}) %collective-permute-start.14) | collective-permute-done | bytes 16416 | tf_op jit(solution)/shard_map/ppermute | solution.py:20
  55.6 1.8 %collective-permute-done.15 = f32[4,4,16,16]{2,3,1,0:T(8,128)S(1)} collective-permute-done((f32[4,4,16,16]{2,3,1,0:T(8,128)S(1)}, f32[4,4,16,16]{2,3,1,0:T(8,128)S(1)}, u32[]{:S(2)}, u32[]{:S(2)}) %collective-permute-start.15) | collective-permute-done | bytes 16416 | tf_op jit(solution)/shard_map/ppermute | solution.py:21
  57.5 0.5 fusion.7
  58.2 0.4 fusion.23
  58.7 0.3 fusion.39
  59.0 0.7 copy-done.5
  59.7 0.1 fusion.56
  59.9 0.7 reshape.210
  60.6 3.8 %all-to-all-start = ((f32[8,1,512]{2,1,0:T(1,128)}), f32[8,1,512]{2,1,0:T(1,128)S(1)}, u32[]{:S(2)}, u32[]{:S(2)}) async-start(f32[8,1,512]{2,1,0:T(1,128)} %reshape.210), calls=%async_computation | async-start | bytes 32768 | tf_op jit(solution)/shard_map/all_to_all | solution.py:173
  64.7 6.3 %all-to-all-done = f32[8,1,512]{2,1,0:T(1,128)S(1)} async-done(((f32[8,1,512]{2,1,0:T(1,128)}), f32[8,1,512]{2,1,0:T(1,128)S(1)}, u32[]{:S(2)}, u32[]{:S(2)}) %all-to-all-start) | async-done | bytes 16416 | tf_op jit(solution)/shard_map/all_to_all | solution.py:173
  71.0 0.6 broadcast.355
  71.6 0.7 reduce
  72.3 0.1 reshape.211
  72.5 0.2 copy.126
  72.6 0.3 fusion.97
  73.0 0.4 multiply_add_fusion
  73.4 0.3 fusion.84
  73.7 0.3 fusion.4
  74.0 0.2 fusion.109
  74.2 0.2 fusion.118
  74.4 0.3 fusion.80
  74.7 0.3 fusion.2
  75.0 0.2 fusion.111
  75.2 0.2 fusion.116
  75.4 0.2 fusion.76
  75.6 0.2 fusion
  75.8 0.3 copy.144
  76.1 0.2 reshape.201
  76.4 0.1 copy.145
  76.5 0.7 reshape.212
  77.2 3.3 %all-to-all-start.1 = ((f32[8,1,512]{2,1,0:T(1,128)}), f32[8,1,512]{2,1,0:T(1,128)S(1)}, u32[]{:S(2)}, u32[]{:S(2)}) async-start(f32[8,1,512]{2,1,0:T(1,128)} %reshape.212), calls=%async_computation.1 | async-start | bytes 32768 | tf_op jit(solution)/shard_map/all_to_all | solution.py:177
  80.6 0.8 copy.173
  81.4 5.7 %all-to-all-done.1 = f32[8,1,512]{2,1,0:T(1,128)S(1)} async-done(((f32[8,1,512]{2,1,0:T(1,128)}), f32[8,1,512]{2,1,0:T(1,128)S(1)}, u32[]{:S(2)}, u32[]{:S(2)}) %all-to-all-start.1) | async-done | bytes 16416 | tf_op jit(solution)/shard_map/all_to_all | solution.py:177
  87.1 0.7 reduce.1
  87.8 0.1 reshape.213
  87.9 0.1 copy.147
  88.2 0.8 copy.172
  (120 shorter events, 3.4 us)
Async XLA Ops:
  1.3 12.9 %collective-permute-start = (f32[4,16]{1,0:T(4,128)S(1)}, f32[4,16]{1,0:T(4,128)S(1)}, u32[]{:S(2)}, u32[]{:S(2)}) collective-permute-start(f32[4,16]{1,0:T(4,128)S(1)} %get-tuple-element.69), channel_id=1, source_target_pairs={{0,2},{2,4},{4,6},{6,8},{8,10},{10,12},{12,14},{14,0},{1,3},{3,5},... | collective-permute-start | bytes 776 | tf_op jit(solution)/shard_map/ppermute | solution.py:20
  4.3 15.3 %collective-permute-start.1 = (f32[4,16]{1,0:T(4,128)S(1)}, f32[4,16]{1,0:T(4,128)S(1)}, u32[]{:S(2)}, u32[]{:S(2)}) collective-permute-start(f32[4,16]{1,0:T(4,128)S(1)} %get-tuple-element.69), channel_id=1, source_target_pairs={{2,0},{4,2},{6,4},{8,6},{10,8},{12,10},{14,12},{0,14},{3,1},{5,3},... | collective-permute-start | bytes 776 | tf_op jit(solution)/shard_map/ppermute | solution.py:21
  7.3 18.2 %collective-permute-start.5 = (f32[4,16,16]{2,1,0:T(8,128)}, f32[4,16,16]{2,1,0:T(8,128)S(1)}, u32[]{:S(2)}, u32[]{:S(2)}) collective-permute-start(f32[4,16,16]{2,1,0:T(8,128)} %param.9), channel_id=1, source_target_pairs={{0,2},{2,4},{4,6},{6,8},{8,10},{10,12},{12,14},{14,0},{1,3},{3,5},... | collective-permute-start | bytes 12296 | tf_op jit(solution)/shard_map/ppermute | solution.py:20
  7.3 23.0 %collective-permute-start.6 = (f32[4,16,16]{2,1,0:T(8,128)}, f32[4,16,16]{2,1,0:T(8,128)S(1)}, u32[]{:S(2)}, u32[]{:S(2)}) collective-permute-start(f32[4,16,16]{2,1,0:T(8,128)} %param.9), channel_id=1, source_target_pairs={{2,0},{4,2},{6,4},{8,6},{10,8},{12,10},{14,12},{0,14},{3,1},{5,3},... | collective-permute-start | bytes 12296 | tf_op jit(solution)/shard_map/ppermute | solution.py:21
  12.0 18.3 %collective-permute-start.7 = (f32[4,16,16]{2,1,0:T(8,128)}, f32[4,16,16]{2,1,0:T(8,128)S(1)}, u32[]{:S(2)}, u32[]{:S(2)}) collective-permute-start(f32[4,16,16]{2,1,0:T(8,128)} %param.10), channel_id=1, source_target_pairs={{0,2},{2,4},{4,6},{6,8},{8,10},{10,12},{12,14},{14,0},{1,3},{3,5},... | collective-permute-start | bytes 12296 | tf_op jit(solution)/shard_map/ppermute | solution.py:20
  13.1 0.9 %copy-start.2 = (f32[4,4,16,16]{3,2,1,0:T(8,128)S(1)}, f32[4,4,16,16]{3,2,1,0:T(8,128)}, u32[]{:S(2)}) copy-start(f32[4,4,16,16]{3,2,1,0:T(8,128)} %param.7) | copy-start | bytes 49156
  13.1 0.7 copy-start.6
  14.1 0.8 copy-start.4
  14.8 20.3 %collective-permute-start.8 = (f32[4,16,16]{2,1,0:T(8,128)S(1)}, f32[4,16,16]{2,1,0:T(8,128)S(1)}, u32[]{:S(2)}, u32[]{:S(2)}) collective-permute-start(f32[4,16,16]{2,1,0:T(8,128)S(1)} %copy-done.4), channel_id=1, source_target_pairs={{2,0},{4,2},{6,4},{8,6},{10,8},{12,10},{14,12},{0,14},{3,1},{5,3},... | collective-permute-start | bytes 12296 | tf_op jit(solution)/shard_map/ppermute | solution.py:21
  19.6 3.1 %collective-permute-start.11 = (f32[4,1,16,16]{2,3,1,0:T(8,128)S(1)}, f32[4,1,16,16]{2,3,1,0:T(8,128)S(1)}, u32[]{:S(2)}, u32[]{:S(2)}) collective-permute-start(f32[4,1,16,16]{2,3,1,0:T(8,128)S(1)} %slice.551), channel_id=1, source_target_pairs={{1,0},{3,2},{5,4},{7,6},{9,8},{11,10},{13,12},{15,14},{17,16},{19,... | collective-permute-start | bytes 12296 | tf_op jit(solution)/shard_map/ppermute | solution.py:29
  22.6 2.9 %collective-permute-start.2 = (f32[4,1,16,16]{2,3,1,0:T(8,128)S(1)}, f32[4,1,16,16]{2,3,1,0:T(8,128)S(1)}, u32[]{:S(2)}, u32[]{:S(2)}) collective-permute-start(f32[4,1,16,16]{2,3,1,0:T(8,128)S(1)} %slice.492), channel_id=1, source_target_pairs={{0,1},{2,3},{4,5},{6,7},{8,9},{10,11},{12,13},{14,15},{16,17},{18,... | collective-permute-start | bytes 12296 | tf_op jit(solution)/shard_map/ppermute | solution.py:29
  24.7 10.4 %copy-start.3 = (f32[4,16,16]{2,1,0:T(8,128)S(1)}, f32[4,16,16]{2,1,0:T(8,128)}, u32[]{:S(2)}) copy-start(f32[4,16,16]{2,1,0:T(8,128)} %param.9) | copy-start | bytes 12292
  25.6 11.4 %collective-permute-start.12 = (f32[4,4,16,16]{2,3,1,0:T(8,128)S(1)}, f32[4,4,16,16]{2,3,1,0:T(8,128)S(1)}, u32[]{:S(2)}, u32[]{:S(2)}) collective-permute-start(f32[4,4,16,16]{2,3,1,0:T(8,128)S(1)} %pad_maximum_fusion.5), channel_id=1, source_target_pairs={{0,2},{2,4},{4,6},{6,8},{8,10},{10,12},{12,14},{14,0},{1,3},{3,5},... | collective-permute-start | bytes 49160 | tf_op jit(solution)/shard_map/ppermute | solution.py:20
  25.6 11.3 %collective-permute-start.13 = (f32[4,4,16,16]{2,3,1,0:T(8,128)S(1)}, f32[4,4,16,16]{2,3,1,0:T(8,128)S(1)}, u32[]{:S(2)}, u32[]{:S(2)}) collective-permute-start(f32[4,4,16,16]{2,3,1,0:T(8,128)S(1)} %pad_maximum_fusion.5), channel_id=1, source_target_pairs={{2,0},{4,2},{6,4},{8,6},{10,8},{12,10},{14,12},{0,14},{3,1},{5,3},... | collective-permute-start | bytes 49160 | tf_op jit(solution)/shard_map/ppermute | solution.py:21
  30.4 8.0 %collective-permute-start.3 = (f32[4,4,16,16]{2,3,1,0:T(8,128)S(1)}, f32[4,4,16,16]{2,3,1,0:T(8,128)S(1)}, u32[]{:S(2)}, u32[]{:S(2)}) collective-permute-start(f32[4,4,16,16]{2,3,1,0:T(8,128)S(1)} %pad_maximum_fusion.4), channel_id=1, source_target_pairs={{0,2},{2,4},{4,6},{6,8},{8,10},{10,12},{12,14},{14,0},{1,3},{3,5},... | collective-permute-start | bytes 49160 | tf_op jit(solution)/shard_map/ppermute | solution.py:20
  30.4 9.4 %collective-permute-start.4 = (f32[4,4,16,16]{2,3,1,0:T(8,128)S(1)}, f32[4,4,16,16]{2,3,1,0:T(8,128)S(1)}, u32[]{:S(2)}, u32[]{:S(2)}) collective-permute-start(f32[4,4,16,16]{2,3,1,0:T(8,128)S(1)} %pad_maximum_fusion.4), channel_id=1, source_target_pairs={{2,0},{4,2},{6,4},{8,6},{10,8},{12,10},{14,12},{0,14},{3,1},{5,3},... | collective-permute-start | bytes 49160 | tf_op jit(solution)/shard_map/ppermute | solution.py:21
  37.0 0.8 copy-start
  39.9 1.0 %slice-start = ((f32[12,4,16,16]{2,3,1,0:T(8,128)}), f32[10,4,16,16]{2,3,1,0:T(8,128)S(1)}, s32[]{:S(2)}) async-start(f32[12,4,16,16]{2,3,1,0:T(8,128)} %copy-done), calls=%async_computation.2 | async-start | bytes 655360 | tf_op jit(solution)/shard_map/slice | solution.py:72
  40.8 1.0 %copy-start.1 = (f32[12,4,16,16]{2,3,1,0:T(8,128)S(1)}, f32[12,4,16,16]{2,3,1,0:T(8,128)}, u32[]{:S(2)}) copy-start(f32[12,4,16,16]{2,3,1,0:T(8,128)} %copy-done) | copy-start | bytes 147460
  43.5 7.9 %collective-permute-start.10 = (f32[4,4,16,16]{2,3,1,0:T(8,128)S(1)}, f32[4,4,16,16]{2,3,1,0:T(8,128)S(1)}, u32[]{:S(2)}, u32[]{:S(2)}) collective-permute-start(f32[4,4,16,16]{2,3,1,0:T(8,128)S(1)} %get-tuple-element.67), channel_id=1, source_target_pairs={{2,0},{4,2},{6,4},{8,6},{10,8},{12,10},{14,12},{0,14},{3,1},{5,3},... | collective-permute-start | bytes 49160 | tf_op jit(solution)/shard_map/ppermute | solution.py:21
  46.5 7.7 %collective-permute-start.9 = (f32[4,4,16,16]{2,3,1,0:T(8,128)S(1)}, f32[4,4,16,16]{2,3,1,0:T(8,128)S(1)}, u32[]{:S(2)}, u32[]{:S(2)}) collective-permute-start(f32[4,4,16,16]{2,3,1,0:T(8,128)S(1)} %get-tuple-element.67), channel_id=1, source_target_pairs={{0,2},{2,4},{4,6},{6,8},{8,10},{10,12},{12,14},{14,0},{1,3},{3,5},... | collective-permute-start | bytes 49160 | tf_op jit(solution)/shard_map/ppermute | solution.py:20
  46.6 9.0 %collective-permute-start.14 = (f32[4,4,16,16]{2,3,1,0:T(8,128)S(1)}, f32[4,4,16,16]{2,3,1,0:T(8,128)S(1)}, u32[]{:S(2)}, u32[]{:S(2)}) collective-permute-start(f32[4,4,16,16]{2,3,1,0:T(8,128)S(1)} %get-tuple-element.66), channel_id=1, source_target_pairs={{0,2},{2,4},{4,6},{6,8},{8,10},{10,12},{12,14},{14,0},{1,3},{3,5},... | collective-permute-start | bytes 49160 | tf_op jit(solution)/shard_map/ppermute | solution.py:20
  46.7 10.7 %collective-permute-start.15 = (f32[4,4,16,16]{2,3,1,0:T(8,128)S(1)}, f32[4,4,16,16]{2,3,1,0:T(8,128)S(1)}, u32[]{:S(2)}, u32[]{:S(2)}) collective-permute-start(f32[4,4,16,16]{2,3,1,0:T(8,128)S(1)} %get-tuple-element.66), channel_id=1, source_target_pairs={{2,0},{4,2},{6,4},{8,6},{10,8},{12,10},{14,12},{0,14},{3,1},{5,3},... | collective-permute-start | bytes 49160 | tf_op jit(solution)/shard_map/ppermute | solution.py:21
  59.0 0.7 copy-start.5
  60.6 10.4 %all-to-all-start = ((f32[8,1,512]{2,1,0:T(1,128)}), f32[8,1,512]{2,1,0:T(1,128)S(1)}, u32[]{:S(2)}, u32[]{:S(2)}) async-start(f32[8,1,512]{2,1,0:T(1,128)} %reshape.210), calls=%async_computation | async-start | bytes 32768 | tf_op jit(solution)/shard_map/all_to_all | solution.py:173
  77.2 9.9 %all-to-all-start.1 = ((f32[8,1,512]{2,1,0:T(1,128)}), f32[8,1,512]{2,1,0:T(1,128)S(1)}, u32[]{:S(2)}, u32[]{:S(2)}) async-start(f32[8,1,512]{2,1,0:T(1,128)} %reshape.212), calls=%async_computation.1 | async-start | bytes 32768 | tf_op jit(solution)/shard_map/all_to_all | solution.py:177
where the time goes:
time: 89.4 us; the launch traced here: 88.9 us
  starting transfers between devices  43.3 us (48%)
  waiting for transfers between devices  22.6 us (25%)
  local copies, waits for them, and re-layouts  12.8 us (14%)
  other arithmetic  5.55 us (6%)
  matrix products  3.17 us (4%)
  between operations  1.5 us (2%)
    ppermute x7, starting transfers between devices, extended(): after = lax.ppermute(leading, axis, down)  29.7 us
    unnamed x24, local copies, waits for them, and re-layouts  8.26 us
    all_to_all x1, waiting for transfers between devices, body(): lax.all_to_all(weighted, 'tiles', split_axis=3, concat_axis=0, tiled=True)  6.35 us
    all_to_all x1, waiting for transfers between devices, body(): lax.all_to_all(smoothed, 'tiles', split_axis=0, concat_axis=3, tiled=True)  5.73 us
    ppermute x7, waiting for transfers between devices, extended(): before = lax.ppermute(last, axis, up)  4.68 us
    all_to_all x1, starting transfers between devices, body(): lax.all_to_all(weighted, 'tiles', split_axis=3, concat_axis=0, tiled=True)  3.83 us
    ppermute x2, starting transfers between devices, passed_along(): return lax.ppermute(x, axis, pairs)  3.34 us
    all_to_all x1, starting transfers between devices, body(): lax.all_to_all(smoothed, 'tiles', split_axis=0, concat_axis=3, tiled=True)  3.34 us
  transfers between devices with their start and end apart: 18, of which 9 were waited for; matrix products, arithmetic and copies ran while one was open for 5% of the time, Pallas kernels for 0%

commit v1 on v0

--- a/solution.py
+++ b/solution.py
@@ -1,8 +1,11 @@
+import functools
 import math
 
 import jax
 import jax.numpy as jnp
 from jax import lax
+from jax.experimental import pallas as pl
+from jax.experimental.pallas import tpu as pltpu
 from jax.sharding import PartitionSpec as P
 
 STEPS = 8
@@ -179,6 +182,271 @@
     return (covar + increment - forward, dual_vector - backward)
 
 
+SUB = 8
+LANES = 128
+
+
+def dense_fits(mesh, shape, lats):
+    lons, wins, levels, _ = shape
+    tiles = mesh.shape["tiles"]
+    halves = levels // SUB
+    return (
+        levels % SUB == 0
+        and wins * halves * lats == LANES
+        and lons * halves * lats == LANES
+        and lats % tiles == 0
+        and lons * lats + wins * (lats // tiles) <= LANES
+        and mesh.shape["subwin"] == 2
+        and tiles % 2 == 0
+        and tiles // 2 >= 3
+        and STEPS <= 2 * lons
+    )
+
+
+def lane_index():
+    return lax.broadcasted_iota(jnp.int32, (SUB, LANES), 1)
+
+
+def picked(values, index):
+    return jnp.take_along_axis(values, index, axis=1)
+
+
+def pack_kernel(inc_ref, dual_ref, u_ref, v_ref, land_ref, len_ref, main_ref, extra_ref):
+    lons, wins, levels, lats = inc_ref.shape
+    halves = levels // SUB
+    own_lats = len_ref.shape[1]
+    lane = lane_index()
+    first = lax.axis_index("subwin") == 0
+
+    def put(ref, row, slot, value):
+        ref[row * SUB : (row + 1) * SUB, slot * lats : (slot + 1) * lats] = value
+
+    for i in range(lons):
+        for half in range(halves):
+            rows = slice(half * SUB, (half + 1) * SUB)
+            for s in range(wins):
+                put(main_ref, i, s * halves + half, dual_ref[i, s, rows, :])
+                put(main_ref, lons + i, s * halves + half, inc_ref[i, s, rows, :])
+            put(main_ref, 2 * lons, i * halves + half, u_ref[i, rows, :])
+            put(main_ref, 2 * lons + 1, i * halves + half, v_ref[i, rows, :])
+            edge = jnp.where(first, inc_ref[i, wins - 1, rows, :], dual_ref[i, 0, rows, :])
+            put(extra_ref, 0, i * halves + half, edge)
+    base = (2 * lons + 2) * SUB
+    main_ref[base : base + SUB, :] = jnp.zeros((SUB, LANES), jnp.float32)
+    for i in range(lons):
+        mixing = 0.15 + 0.09 * land_ref[i : i + 1, :].astype(jnp.float32)
+        main_ref[base : base + SUB, i * lats : (i + 1) * lats] = jnp.broadcast_to(mixing, (SUB, lats))
+    for s in range(wins):
+        at = lons * lats + s * own_lats
+        main_ref[base : base + SUB, at : at + own_lats] = jnp.broadcast_to(
+            len_ref[s : s + 1, :], (SUB, own_lats)
+        )
+
+
+def apply_kernel(geometry, *refs):
+    lons, wins, levels, lats, tiles = geometry
+    halves = levels // SUB
+    group = halves * lats
+    rings = tiles // 2
+    own_lats = lats // tiles
+    count = lons * tiles
+    main_ref, extra_ref, pmain_ref, pextra_ref, left_ref, right_ref = refs[:6]
+    far_refs = refs[6 : 6 + rings - 3]
+    spread_ref, model_ref, dual_out_ref, coeff_ref, field_ref, dual_ref = refs[6 + rings - 3 :]
+    lane = lane_index()
+    tile = lax.axis_index("tiles")
+    even = tile % 2 == 0
+    first = lax.axis_index("subwin") == 0
+    main_rows = (2 * lons + 3) * SUB
+    block_rows = main_rows + SUB
+    far_rows = (lons + 1) * SUB
+
+    def block(ring, peer, row):
+        ring = (ring + rings // 2 - 1) % rings - (rings // 2 - 1)
+        if ring == 0:
+            if row == 2 * lons + 3:
+                ref, at = (pextra_ref if peer else extra_ref), 0
+            else:
+                ref, at = (pmain_ref if peer else main_ref), row * SUB
+        elif ring in (-1, 1):
+            ref, at = (right_ref if ring == 1 else left_ref), row * SUB + (block_rows if peer else 0)
+        else:
+            if row >= lons:
+                row = lons
+            ref, at = far_refs[ring % rings - 2], row * SUB + (far_rows if peer else 0)
+        return ref[at : at + SUB, :]
+
+    def at_tile(offset, row):
+        if offset % 2 == 0:
+            return block(offset // 2, False, row)
+        return jnp.where(even, block((offset - 1) // 2, True, row), block((offset + 1) // 2, True, row))
+
+    misc_row = 2 * lons + 2
+
+    length = jnp.zeros((SUB, LANES), jnp.float32)
+    index = lons * lats + own_lats * (lane // group) + lane % own_lats
+    owner = lane % lats // own_lats
+    low = -(tiles // 2) + 1
+    for offset in range(low, low + tiles):
+        here = picked(at_tile(offset, misc_row), index)
+        length = jnp.where(owner == (tile + offset + tiles) % tiles, here, length)
+    damped = []
+    for wave in range(count // 2 + 1):
+        basic = 1.0 - math.cos(2.0 * math.pi * wave / count)
+        inverse = 1.0 / (1.0 + (2.0 * basic) * length)
+        squared = inverse * inverse
+        weight = (1.0 if wave in (0, count // 2) else 2.0) / count
+        damped.append(squared * squared * weight)
+    weights = []
+    for gap in range(count // 2 + 1):
+        total = None
+        for wave in range(count // 2 + 1):
+            term = damped[wave] * math.cos(2.0 * math.pi * (wave * gap % count) / count)
+            total = term if total is None else total + term
+        weights.append(total)
+
+    smooth = [None] * lons
+    for offset in range(low, low + tiles):
+        for j in range(lons):
+            value = at_tile(offset, j)
+            for i in range(lons):
+                gap = (i - (offset * lons + j)) % count
+                term = weights[min(gap, count - gap)] * value
+                smooth[i] = term if smooth[i] is None else smooth[i] + term
+
+    lat = lane % lats
+    span = lons + 2 * STEPS
+    for r in range(span):
+        offset, i = (r - STEPS) // lons, (r - STEPS) % lons
+        spot = i * group + lane % group
+        wind_u = 0.5 * picked(at_tile(offset, 2 * lons), spot)
+        wind_v = 0.5 * picked(at_tile(offset, 2 * lons + 1), spot)
+        mixing = picked(at_tile(offset, misc_row), i * lats + lat)
+        coeff_ref[r, 0] = 1.0 - 4.0 * mixing
+        coeff_ref[r, 1] = mixing - wind_u
+        coeff_ref[r, 2] = mixing + wind_u
+        coeff_ref[r, 3] = jnp.where(lat == lats - 1, 0.0, mixing - wind_v)
+        coeff_ref[r, 4] = jnp.where(lat == 0, 0.0, mixing + wind_v)
+        edge = at_tile(offset, 2 * lons + 3)
+        early = pltpu.roll(edge, (LANES - i * group) % LANES, 1)
+        late = pltpu.roll(edge, (2 * LANES - (i + 1) * group) % LANES, 1)
+        inside = pltpu.roll(at_tile(offset, lons + i), group, 1)
+        field_ref[r] = jnp.where(lane < group, jnp.where(first, 0.0, early), inside)
+        inside = pltpu.roll(at_tile(offset, i), LANES - group, 1)
+        dual_ref[r] = jnp.where(lane >= LANES - group, jnp.where(first, late, 0.0), inside)
+
+    def north(values):
+        return pltpu.roll(values, LANES - 1, 1)
+
+    def south(values):
+        return pltpu.roll(values, 1, 1)
+
+    forward = [field_ref[r] for r in range(span)]
+    for step in range(STEPS):
+        following = []
+        for p in range(1, len(forward) - 1):
+            r = p + step
+            middle = forward[p]
+            following.append(
+                coeff_ref[r, 0] * middle
+                + coeff_ref[r, 1] * forward[p + 1]
+                + coeff_ref[r, 2] * forward[p - 1]
+                + coeff_ref[r, 3] * north(middle)
+                + coeff_ref[r, 4] * south(middle)
+            )
+        forward = following
+    backward = [dual_ref[r] for r in range(span)]
+    for step in range(STEPS):
+        following = []
+        for p in range(1, len(backward) - 1):
+            r = p + step
+            middle = backward[p]
+            following.append(
+                coeff_ref[r, 0] * middle
+                + coeff_ref[r - 1, 1] * backward[p - 1]
+                + coeff_ref[r + 1, 2] * backward[p + 1]
+                + south(coeff_ref[r, 3] * middle)
+                + north(coeff_ref[r, 4] * middle)
+            )
+        backward = following
+
+    level = lax.broadcasted_iota(jnp.int32, (SUB, LANES), 0) + SUB * (lane % group // lats)
+    scale = jnp.zeros((SUB, LANES), jnp.float32)
+    for s in range(wins):
+        row = jnp.concatenate(
+            [jnp.broadcast_to(spread_ref[s : s + 1, :], (SUB, levels))] * (LANES // levels), axis=1
+        )
+        scale = jnp.where(lane // group == s, picked(row, level), scale)
+    square = scale * scale
+
+    for i in range(lons):
+        model = square * smooth[i] + block(0, False, lons + i) - forward[i]
+        other = block(0, False, i) - backward[i]
+        for s in range(wins):
+            for half in range(halves):
+                at = (s * halves + half) * lats
+                rows = slice(half * SUB, (half + 1) * SUB)
+                model_ref[i, s, rows, :] = model[:, at : at + lats]
+                dual_out_ref[i, s, rows, :] = other[:, at : at + lats]
+
+
+def dense_body(increment, dual_vector, wind_u, wind_v, land_sea, length_sq, spread):
+    lons, wins, levels, lats = increment.shape
+    tiles = lax.axis_size("tiles")
+    cores = lax.axis_size("subwin")
+    rings = tiles // 2
+    main_rows = (2 * lons + 3) * SUB
+    vmem = pl.BlockSpec(memory_space=pltpu.VMEM)
+    main, extra = pl.pallas_call(
+        pack_kernel,
+        out_shape=(
+            jax.ShapeDtypeStruct((main_rows, LANES), jnp.float32),
+            jax.ShapeDtypeStruct((SUB, LANES), jnp.float32),
+        ),
+        in_specs=[vmem] * 6,
+        out_specs=(vmem, vmem),
+        name="pack",
+    )(increment, dual_vector, wind_u, wind_v, land_sea, length_sq)
+
+    other = [(w, cores - 1 - w) for w in range(cores)]
+    peer = [(t, t ^ 1) for t in range(tiles)]
+    across = [
+        (t * cores + w, (t ^ 1) * cores + cores - 1 - w) for t in range(tiles) for w in range(cores)
+    ]
+    swapped = lax.ppermute(extra, "subwin", other)
+    peer_main = lax.ppermute(main, "tiles", peer)
+    peer_extra = lax.ppermute(extra, ("tiles", "subwin"), across)
+
+    def ring(x, by):
+        return lax.ppermute(
+            x, "tiles", [(t, (t // 2 + by) % rings * 2 + t % 2) for t in range(tiles)]
+        )
+
+    pair = jnp.concatenate([main, swapped, peer_main, peer_extra])
+    held, misc = lons * SUB, (2 * lons + 2) * SUB
+    short = jnp.concatenate(
+        [main[:held], main[misc:], peer_main[:held], peer_main[misc:]]
+    )
+    left = ring(pair, 1)
+    right = ring(pair, -1)
+    far = [ring(short, -d) for d in range(2, rings - 1)]
+    span = lons + 2 * STEPS
+    shape = jax.ShapeDtypeStruct(increment.shape, jnp.float32)
+    inputs = [main, swapped, peer_main, peer_extra, left, right, *far, spread]
+    return pl.pallas_call(
+        functools.partial(apply_kernel, (lons, wins, levels, lats, tiles)),
+        out_shape=(shape, shape),
+        in_specs=[vmem] * len(inputs),
+        out_specs=(vmem, vmem),
+        scratch_shapes=[
+            pltpu.VMEM((span, 5, SUB, LANES), jnp.float32),
+            pltpu.VMEM((span, SUB, LANES), jnp.float32),
+            pltpu.VMEM((span, SUB, LANES), jnp.float32),
+        ],
+        name="apply",
+    )(*inputs)
+
+
 def solution(mesh):
     placed = (
         P(("groups", "tiles"), "subwin", None, None),
@@ -189,8 +457,15 @@
         P("subwin", "tiles"),
         P("subwin", None),
     )
+
+    def local(*arrays):
+        increment = arrays[0]
+        lats = increment.shape[3]
+        chosen = dense_body if dense_fits(mesh, increment.shape, lats) else body
+        return chosen(*arrays)
+
     return jax.shard_map(
-        body,
+        local,
         mesh=mesh,
         in_specs=placed,
         out_specs=(

time: 89.4 us -> 25.7 us (0.29)
  starting transfers between devices: 43.3 us -> 7.75 us
  waiting for transfers between devices: 22.6 us -> 6.75 us
  local copies, waits for them, and re-layouts: 12.8 us -> 5.38 us
  other arithmetic: 5.55 us -> 0.01 us
  Pallas kernels: 0 us -> 4.85 us
  matrix products: 3.17 us -> 0 us
    ppermute x16 -> x6, starting transfers between devices: 36.1 us -> 7.75 us  [the longest x3 4.67 us: ring(): lax.ppermute(x, 'tiles', [(t, (t // 2 + by) % rings * 2 + t % 2) for t in...]
    all_to_all x2 -> x0, waiting for transfers between devices: 12.1 us -> none  [the longest x1 6.35 us: body(): lax.all_to_all(weighted, 'tiles', split_axis=3, concat_axis=0, tiled=True)]
    all_to_all x2 -> x0, starting transfers between devices: 7.17 us -> none  [the longest x1 3.83 us: body(): lax.all_to_all(weighted, 'tiles', split_axis=3, concat_axis=0, tiled=True)]
    pallas_call x0 -> x2, Pallas kernels: none -> 4.85 us  [the longest x1 3.08 us: dense_body(): pl.pallas_call(functools.partial(apply_kernel, (lons, wins, levels, lats,...]
    unnamed x24 -> x16, local copies, waits for them, and re-layouts: 8.26 us -> 3.97 us
    ppermute x16 -> x6, waiting for transfers between devices: 10.5 us -> 6.75 us  [the longest x3 5.32 us: ring(): lax.ppermute(x, 'tiles', [(t, (t // 2 + by) % rings * 2 + t % 2) for t in...]
    dot_general x12 -> x0, matrix products: 3.17 us -> none  [contract(): return jnp.einsum(form, first, second, precision=lax.Precision.HIGHEST)]
    add x7 -> x0, other arithmetic: 2.53 us -> none  [adjoint_step(): centre * middle + (eastward * fields)[:-2] + (westward * fields)[2:]]
  transfers between devices with their start and end apart: 18 -> 6, of which waited for: 9 -> 3; matrix products, arithmetic and copies ran while one was open for 5% -> 9% of each run, Pallas kernels for 0% -> 0%
where the time goes in v1:
time: 25.7 us; the launch traced here: 25.4 us
  starting transfers between devices  7.75 us (30%)
  waiting for transfers between devices  6.75 us (26%)
  local copies, waits for them, and re-layouts  5.38 us (21%)
  Pallas kernels  4.85 us (19%)
  between operations  0.68 us (3%)
    ppermute x3, waiting for transfers between devices, ring(): lax.ppermute(x, 'tiles', [(t, (t // 2 + by) % rings * 2 + t % 2) for t in...  5.32 us
    ppermute x3, starting transfers between devices, ring(): lax.ppermute(x, 'tiles', [(t, (t // 2 + by) % rings * 2 + t % 2) for t in...  4.67 us
    unnamed x16, local copies, waits for them, and re-layouts  3.97 us
    pallas_call x1, Pallas kernels, dense_body(): pl.pallas_call(functools.partial(apply_kernel, (lons, wins, levels, lats,...  3.08 us
    ppermute x1, starting transfers between devices, dense_body(): peer_extra = lax.ppermute(extra, ('tiles', 'subwin'), across)  2.41 us
    pallas_call x1, Pallas kernels, dense_body(): pl.pallas_call(pack_kernel, out_shape=(jax.ShapeDtypeStruct((main_rows, L...  1.77 us
    ppermute x1, waiting for transfers between devices, dense_body(): peer_main = lax.ppermute(main, 'tiles', peer)  1.43 us
    slice x1, local copies, waits for them, and re-layouts, dense_body(): main[:held]  0.72 us
  transfers between devices with their start and end apart: 6, of which 3 were waited for; matrix products, arithmetic and copies ran while one was open for 9% of the time, Pallas kernels for 0%

profile of v1, /device:TPU:0, one launch (start us, length us, event | category | flops | bytes accessed | tf_op | source)
XLA Modules:
  0.0 25.4 jit_solution(996374163673981842)
XLA Ops:
  0.6 1.3 %copy.9.len_ref = f32[4,2]{1,0:T(4,128)} copy(f32[4,2]{0,1:T(2,128)} %param.12) | data formatting | bytes 64 | tf_op args[5]
  2.0 1.8 %pack.1 = (f32[88,128]{1,0:T(8,128)}, f32[8,128]{1,0:T(8,128)}) custom-call(f32[4,4,16,16]{3,2,1,0:T(8,128)} %inc_ref.1, f32[4,4,16,16]{3,2,1,0:T(8,128)} %dual_ref.1, f32[4,16,16]{2,1,0:T(8,128)} %u_ref.1, f32[4,16,16]{2,1,0:T(8,128)} %v_ref.1, s32[4,16]{1,0:T(4,128)} %land_ref.1, f32[4,2]{1,0:T(4,128)} %copy.9.len_ref), custom_call_target="tpu_custom_call" | custom-call | tf_op jit(solution)/shard_map/pack/pallas_call | solution.py:400
  3.7 2.4 %collective-permute-start.2 = (f32[8,128]{1,0:T(8,128)}, f32[8,128]{1,0:T(8,128)S(1)}, u32[]{:S(2)}, u32[]{:S(2)}) collective-permute-start(f32[8,128]{1,0:T(8,128)} %get-tuple-element.5), channel_id=1, source_target_pairs={{0,3},{1,2},{2,1},{3,0},{4,7},{5,6},{6,5},{7,4},{8,11},{9,10},{10,... | collective-permute-start | bytes 12296 | tf_op jit(solution)/shard_map/ppermute | solution.py:418
  6.1 0.7 %collective-permute-start = (f32[8,128]{1,0:T(8,128)}, f32[8,128]{1,0:T(8,128)S(1)}, u32[]{:S(2)}, u32[]{:S(2)}) collective-permute-start(f32[8,128]{1,0:T(8,128)} %get-tuple-element.5), channel_id=1, source_target_pairs={{0,1},{1,0},{2,3},{3,2},{4,5},{5,4},{6,7},{7,6},{8,9},{9,8},{10,11... | collective-permute-start | bytes 12296 | tf_op jit(solution)/shard_map/ppermute | solution.py:416
  6.8 0.0 collective-permute-start.1
  6.8 0.8 %constant_dynamic-update-slice_fusion.3 = f32[192,128]{1,0:T(8,128)S(1)} fusion(f32[88,128]{1,0:T(8,128)} %get-tuple-element.4.refs_0_), kind=kLoop, calls=%fused_computation.4 | loop fusion | bytes 90112
  7.7 0.7 %slice.13 = f32[8,128]{1,0:T(8,128)S(1)} slice(f32[88,128]{1,0:T(8,128)} %get-tuple-element.4.refs_0_), slice={[80:88], [0:128]} | slice | bytes 8192 | tf_op jit(solution)/shard_map/slice | solution.py:428
  8.3 0.7 %slice.12 = f32[32,128]{1,0:T(8,128)S(1)} slice(f32[88,128]{1,0:T(8,128)} %get-tuple-element.4.refs_0_), slice={[0:32], [0:128]} | slice | bytes 32768 | tf_op jit(solution)/shard_map/slice | solution.py:428
  9.1 0.0 collective-permute-done.refs_1_
  9.1 0.0 copy-start.5
  9.1 0.6 %copy-done.5 = f32[8,128]{1,0:T(8,128)} copy-done((f32[8,128]{1,0:T(8,128)}, f32[8,128]{1,0:T(8,128)S(1)}, u32[]{:S(2)}) %copy-start.5) | copy-done | bytes 4120
  9.6 1.4 %collective-permute-done.1.refs_2_ = f32[88,128]{1,0:T(8,128)S(1)} collective-permute-done((f32[88,128]{1,0:T(8,128)}, f32[88,128]{1,0:T(8,128)S(1)}, u32[]{:S(2)}, u32[]{:S(2)}) %collective-permute-start.1) | collective-permute-done | bytes 45088 | tf_op jit(solution)/shard_map/ppermute | solution.py:417
  11.1 0.0 copy-start
  11.1 0.0 collective-permute-done.2.refs_3_
  11.1 0.0 copy-start.4
  11.1 0.6 %copy-done.4 = f32[8,128]{1,0:T(8,128)} copy-done((f32[8,128]{1,0:T(8,128)}, f32[8,128]{1,0:T(8,128)S(1)}, u32[]{:S(2)}) %copy-start.4) | copy-done | bytes 4120
  11.7 3.6 %collective-permute-start.4 = (f32[192,128]{1,0:T(8,128)S(1)}, f32[192,128]{1,0:T(8,128)S(1)}, u32[]{:S(2)}, u32[]{:S(2)}) collective-permute-start(f32[192,128]{1,0:T(8,128)S(1)} %constant_dynamic-update-slice_fusion), channel_id=1, source_target_pairs={{0,12},{2,14},{4,0},{6,2},{8,4},{10,6},{12,8},{14,10},{1,13},{3,15... | collective-permute-start | bytes 294920 | tf_op jit(solution)/shard_map/ppermute | solution.py:421
  15.3 0.0 collective-permute-start.3
  15.3 0.0 copy-done
  15.3 1.1 %collective-permute-start.5 = (f32[80,128]{1,0:T(8,128)S(1)}, f32[80,128]{1,0:T(8,128)S(1)}, u32[]{:S(2)}, u32[]{:S(2)}) collective-permute-start(f32[80,128]{1,0:T(8,128)S(1)} %pad_maximum_fusion), channel_id=1, source_target_pairs={{0,8},{2,10},{4,12},{6,14},{8,0},{10,2},{12,4},{14,6},{1,9},{3,11}... | collective-permute-start | bytes 122888 | tf_op jit(solution)/shard_map/ppermute | solution.py:421
  16.4 3.9 %collective-permute-done.5.refs_6_ = f32[80,128]{1,0:T(8,128)S(1)} collective-permute-done((f32[80,128]{1,0:T(8,128)S(1)}, f32[80,128]{1,0:T(8,128)S(1)}, u32[]{:S(2)}, u32[]{:S(2)}) %collective-permute-start.5) | collective-permute-done | bytes 40992 | tf_op jit(solution)/shard_map/ppermute | solution.py:421
  20.3 0.0 copy-start.3
  20.3 0.0 collective-permute-done.4.refs_5_
  20.3 0.0 copy-start.1
  20.3 1.4 %collective-permute-done.3.refs_4_ = f32[192,128]{1,0:T(8,128)S(1)} collective-permute-done((f32[192,128]{1,0:T(8,128)S(1)}, f32[192,128]{1,0:T(8,128)S(1)}, u32[]{:S(2)}, u32[]{:S(2)}) %collective-permute-start.3) | collective-permute-done | bytes 98336 | tf_op jit(solution)/shard_map/ppermute | solution.py:421
  21.7 0.0 copy-done.3
  21.7 0.0 copy-done.1
  21.7 0.0 copy-start.2
  21.7 0.6 %copy-done.2 = f32[192,128]{1,0:T(8,128)} copy-done((f32[192,128]{1,0:T(8,128)}, f32[192,128]{1,0:T(8,128)S(1)}, u32[]{:S(2)}) %copy-start.2) | copy-done | bytes 98328
  22.3 3.1 %apply.1 = (f32[4,4,16,16]{3,2,1,0:T(8,128)}, f32[4,4,16,16]{3,2,1,0:T(8,128)}) custom-call(f32[88,128]{1,0:T(8,128)} %get-tuple-element.4.refs_0_, f32[8,128]{1,0:T(8,128)} %copy-done.5, f32[88,128]{1,0:T(8,128)} %copy-done, f32[8,128]{1,0:T(8,128)} %copy-done.4, f32[192,128]{1,0:T(8,128)} %copy-done.2, f32[192,128]{1,0:T(8,128)} %copy-done.1, ...), custom_call_target="tpu_custom_call" | custom-call | tf_op jit(solution)/shard_map/apply/pallas_call | solution.py:436
  (6 shorter events, 0.0 us)
Async XLA Ops:
  3.7 7.3 %collective-permute-start.2 = (f32[8,128]{1,0:T(8,128)}, f32[8,128]{1,0:T(8,128)S(1)}, u32[]{:S(2)}, u32[]{:S(2)}) collective-permute-start(f32[8,128]{1,0:T(8,128)} %get-tuple-element.5), channel_id=1, source_target_pairs={{0,3},{1,2},{2,1},{3,0},{4,7},{5,6},{6,5},{7,4},{8,11},{9,10},{10,... | collective-permute-start | bytes 12296 | tf_op jit(solution)/shard_map/ppermute | solution.py:418
  6.1 2.9 %collective-permute-start = (f32[8,128]{1,0:T(8,128)}, f32[8,128]{1,0:T(8,128)S(1)}, u32[]{:S(2)}, u32[]{:S(2)}) collective-permute-start(f32[8,128]{1,0:T(8,128)} %get-tuple-element.5), channel_id=1, source_target_pairs={{0,1},{1,0},{2,3},{3,2},{4,5},{5,4},{6,7},{7,6},{8,9},{9,8},{10,11... | collective-permute-start | bytes 12296 | tf_op jit(solution)/shard_map/ppermute | solution.py:416
  6.8 4.3 %collective-permute-start.1 = (f32[88,128]{1,0:T(8,128)}, f32[88,128]{1,0:T(8,128)S(1)}, u32[]{:S(2)}, u32[]{:S(2)}) collective-permute-start(f32[88,128]{1,0:T(8,128)} %get-tuple-element.4.refs_0_), channel_id=1, source_target_pairs={{0,2},{2,0},{4,6},{6,4},{8,10},{10,8},{12,14},{14,12},{1,3},{3,1},... | collective-permute-start | bytes 135176 | tf_op jit(solution)/shard_map/ppermute | solution.py:417
  9.1 0.6 %copy-start.5 = (f32[8,128]{1,0:T(8,128)}, f32[8,128]{1,0:T(8,128)S(1)}, u32[]{:S(2)}) copy-start(f32[8,128]{1,0:T(8,128)S(1)} %collective-permute-done.refs_1_) | copy-start | bytes 12292
  11.1 4.2 %copy-start = (f32[88,128]{1,0:T(8,128)}, f32[88,128]{1,0:T(8,128)S(1)}, u32[]{:S(2)}) copy-start(f32[88,128]{1,0:T(8,128)S(1)} %collective-permute-done.1.refs_2_) | copy-start | bytes 135172
  11.1 0.6 %copy-start.4 = (f32[8,128]{1,0:T(8,128)}, f32[8,128]{1,0:T(8,128)S(1)}, u32[]{:S(2)}) copy-start(f32[8,128]{1,0:T(8,128)S(1)} %collective-permute-done.2.refs_3_) | copy-start | bytes 12292
  11.7 8.6 %collective-permute-start.4 = (f32[192,128]{1,0:T(8,128)S(1)}, f32[192,128]{1,0:T(8,128)S(1)}, u32[]{:S(2)}, u32[]{:S(2)}) collective-permute-start(f32[192,128]{1,0:T(8,128)S(1)} %constant_dynamic-update-slice_fusion), channel_id=1, source_target_pairs={{0,12},{2,14},{4,0},{6,2},{8,4},{10,6},{12,8},{14,10},{1,13},{3,15... | collective-permute-start | bytes 294920 | tf_op jit(solution)/shard_map/ppermute | solution.py:421
  15.3 6.4 %collective-permute-start.3 = (f32[192,128]{1,0:T(8,128)S(1)}, f32[192,128]{1,0:T(8,128)S(1)}, u32[]{:S(2)}, u32[]{:S(2)}) collective-permute-start(f32[192,128]{1,0:T(8,128)S(1)} %constant_dynamic-update-slice_fusion), channel_id=1, source_target_pairs={{0,4},{2,6},{4,8},{6,10},{8,12},{10,14},{12,0},{14,2},{1,5},{3,7},... | collective-permute-start | bytes 294920 | tf_op jit(solution)/shard_map/ppermute | solution.py:421
  15.3 5.0 %collective-permute-start.5 = (f32[80,128]{1,0:T(8,128)S(1)}, f32[80,128]{1,0:T(8,128)S(1)}, u32[]{:S(2)}, u32[]{:S(2)}) collective-permute-start(f32[80,128]{1,0:T(8,128)S(1)} %pad_maximum_fusion), channel_id=1, source_target_pairs={{0,8},{2,10},{4,12},{6,14},{8,0},{10,2},{12,4},{14,6},{1,9},{3,11}... | collective-permute-start | bytes 122888 | tf_op jit(solution)/shard_map/ppermute | solution.py:421
  20.3 1.4 %copy-start.3 = (f32[80,128]{1,0:T(8,128)}, f32[80,128]{1,0:T(8,128)S(1)}, u32[]{:S(2)}) copy-start(f32[80,128]{1,0:T(8,128)S(1)} %collective-permute-done.5.refs_6_) | copy-start | bytes 122884
  20.3 1.4 %copy-start.1 = (f32[192,128]{1,0:T(8,128)}, f32[192,128]{1,0:T(8,128)S(1)}, u32[]{:S(2)}) copy-start(f32[192,128]{1,0:T(8,128)S(1)} %collective-permute-done.4.refs_5_) | copy-start | bytes 294916
  21.7 0.6 %copy-start.2 = (f32[192,128]{1,0:T(8,128)}, f32[192,128]{1,0:T(8,128)S(1)}, u32[]{:S(2)}) copy-start(f32[192,128]{1,0:T(8,128)S(1)} %collective-permute-done.3.refs_4_) | copy-start | bytes 294916

commit v2 on v1

--- a/solution.py
+++ b/solution.py
@@ -184,6 +184,7 @@
 
 SUB = 8
 LANES = 128
+VMEM_BYTES = 4 * 2**20
 
 
 def dense_fits(mesh, shape, lats):
@@ -198,7 +199,7 @@
         and lons * lats + wins * (lats // tiles) <= LANES
         and mesh.shape["subwin"] == 2
         and tiles % 2 == 0
-        and tiles // 2 >= 3
+        and tiles // 2 >= 4
         and STEPS <= 2 * lons
     )
 
@@ -211,11 +212,20 @@
     return jnp.take_along_axis(values, index, axis=1)
 
 
-def pack_kernel(inc_ref, dual_ref, u_ref, v_ref, land_ref, len_ref, main_ref, extra_ref):
+def pack_kernel(*refs):
+    arrays, (main_ref, extra_ref), held, arrived = refs[:6], refs[6:8], refs[8:14], refs[14]
+    copies = [
+        pltpu.make_async_copy(source, target, arrived.at[k])
+        for k, (source, target) in enumerate(zip(arrays, held))
+    ]
+    for copy in copies:
+        copy.start()
+    for copy in copies:
+        copy.wait()
+    inc_ref, dual_ref, u_ref, v_ref, land_ref, len_ref = held
     lons, wins, levels, lats = inc_ref.shape
     halves = levels // SUB
-    own_lats = len_ref.shape[1]
-    lane = lane_index()
+    own_lats = len_ref.shape[0]
     first = lax.axis_index("subwin") == 0
 
     def put(ref, row, slot, value):
@@ -236,10 +246,10 @@
     for i in range(lons):
         mixing = 0.15 + 0.09 * land_ref[i : i + 1, :].astype(jnp.float32)
         main_ref[base : base + SUB, i * lats : (i + 1) * lats] = jnp.broadcast_to(mixing, (SUB, lats))
-    for s in range(wins):
-        at = lons * lats + s * own_lats
-        main_ref[base : base + SUB, at : at + own_lats] = jnp.broadcast_to(
-            len_ref[s : s + 1, :], (SUB, own_lats)
+    for j in range(own_lats):
+        at = lons * lats + j * wins
+        main_ref[base : base + SUB, at : at + wins] = jnp.broadcast_to(
+            len_ref[j : j + 1, :], (SUB, wins)
         )
 
 
@@ -284,7 +294,7 @@
     misc_row = 2 * lons + 2
 
     length = jnp.zeros((SUB, LANES), jnp.float32)
-    index = lons * lats + own_lats * (lane // group) + lane % own_lats
+    index = lons * lats + wins * (lane % own_lats) + lane // group
     owner = lane % lats // own_lats
     low = -(tiles // 2) + 1
     for offset in range(low, low + tiles):
@@ -397,16 +407,21 @@
     rings = tiles // 2
     main_rows = (2 * lons + 3) * SUB
     vmem = pl.BlockSpec(memory_space=pltpu.VMEM)
+    hbm = pl.BlockSpec(memory_space=pltpu.HBM)
+    arrays = (increment, dual_vector, wind_u, wind_v, land_sea, length_sq.T)
     main, extra = pl.pallas_call(
         pack_kernel,
         out_shape=(
             jax.ShapeDtypeStruct((main_rows, LANES), jnp.float32),
             jax.ShapeDtypeStruct((SUB, LANES), jnp.float32),
         ),
-        in_specs=[vmem] * 6,
+        in_specs=[hbm] * len(arrays),
         out_specs=(vmem, vmem),
+        scratch_shapes=[pltpu.VMEM(x.shape, x.dtype) for x in arrays]
+        + [pltpu.SemaphoreType.DMA((len(arrays),))],
+        compiler_params=pltpu.CompilerParams(vmem_limit_bytes=VMEM_BYTES),
         name="pack",
-    )(increment, dual_vector, wind_u, wind_v, land_sea, length_sq)
+    )(*[pltpu.with_memory_space_constraint(x, pltpu.HBM) for x in arrays])
 
     other = [(w, cores - 1 - w) for w in range(cores)]
     peer = [(t, t ^ 1) for t in range(tiles)]
@@ -443,6 +458,7 @@
             pltpu.VMEM((span, SUB, LANES), jnp.float32),
             pltpu.VMEM((span, SUB, LANES), jnp.float32),
         ],
+        compiler_params=pltpu.CompilerParams(vmem_limit_bytes=VMEM_BYTES),
         name="apply",
     )(*inputs)
 

time: 25.7 us -> 21.3 us (0.83)
  local copies, waits for them, and re-layouts: 5.38 us -> 0.02 us
  waiting for transfers between devices: 6.75 us -> 9.31 us
  Pallas kernels: 4.85 us -> 3.26 us
    unnamed x16 -> x5, local copies, waits for them, and re-layouts: 3.97 us -> 0.01 us
    ppermute x1, waiting for transfers between devices: 1.43 us -> 3.22 us  [dense_body(): peer_main = lax.ppermute(main, 'tiles', peer)]
    pallas_call x1, Pallas kernels: 3.08 us -> 2.08 us  [dense_body(): pl.pallas_call(functools.partial(apply_kernel, (lons, wins, levels, lats,...]
    ppermute x1, waiting for transfers between devices: 0.01 us -> 0.77 us  [dense_body(): swapped = lax.ppermute(extra, 'subwin', other)]
    slice x1, local copies, waits for them, and re-layouts: 0.72 us -> 0.01 us  [dense_body(): main[:held]]
    slice x1, local copies, waits for them, and re-layouts: 0.68 us -> 0.01 us  [dense_body(): main[misc:]]
    pallas_call x1, Pallas kernels: 1.77 us -> 1.18 us  [dense_body(): pl.pallas_call(pack_kernel, out_shape=(jax.ShapeDtypeStruct((main_rows, L...]
  transfers between devices with their start and end apart: 6 -> 6, of which waited for: 3 -> 4; matrix products, arithmetic and copies ran while one was open for 9% -> 0% of each run, Pallas kernels for 0% -> 0%
where the time goes in v2:
time: 21.3 us; the launch traced here: 21.2 us
  waiting for transfers between devices  9.31 us (44%)
  starting transfers between devices  7.91 us (37%)
  Pallas kernels  3.26 us (15%)
  between operations  0.68 us (3%)
    ppermute x3, waiting for transfers between devices, ring(): lax.ppermute(x, 'tiles', [(t, (t // 2 + by) % rings * 2 + t % 2) for t in...  5.32 us
    ppermute x3, starting transfers between devices, ring(): lax.ppermute(x, 'tiles', [(t, (t // 2 + by) % rings * 2 + t % 2) for t in...  4.72 us
    ppermute x1, waiting for transfers between devices, dense_body(): peer_main = lax.ppermute(main, 'tiles', peer)  3.22 us
    ppermute x1, starting transfers between devices, dense_body(): peer_extra = lax.ppermute(extra, ('tiles', 'subwin'), across)  2.47 us
    pallas_call x1, Pallas kernels, dense_body(): pl.pallas_call(functools.partial(apply_kernel, (lons, wins, levels, lats,...  2.08 us
    pallas_call x1, Pallas kernels, dense_body(): pl.pallas_call(pack_kernel, out_shape=(jax.ShapeDtypeStruct((main_rows, L...  1.18 us
    ppermute x1, waiting for transfers between devices, dense_body(): swapped = lax.ppermute(extra, 'subwin', other)  0.77 us
    ppermute x1, starting transfers between devices, dense_body(): swapped = lax.ppermute(extra, 'subwin', other)  0.68 us
  transfers between devices with their start and end apart: 6, of which 4 were waited for; matrix products, arithmetic and copies ran while one was open for 0% of the time, Pallas kernels for 0%

profile of v2, /device:TPU:0, one launch (start us, length us, event | category | flops | bytes accessed | tf_op | source)
XLA Modules:
  0.0 21.2 jit_solution(6639170455256901891)
XLA Ops:
  0.6 1.2 %pack.1 = (f32[88,128]{1,0:T(8,128)S(1)}, f32[8,128]{1,0:T(8,128)S(1)}) custom-call(f32[4,4,16,16]{3,2,1,0:T(8,128)} %refs_0_.1, f32[4,4,16,16]{3,2,1,0:T(8,128)} %refs_1_.1, f32[4,16,16]{2,1,0:T(8,128)} %refs_2_.1, f32[4,16,16]{2,1,0:T(8,128)} %refs_3_.1, s32[4,16]{1,0:T(4,128)} %refs_4_.1, f32[2,4]{1,0:T(2,128)} %bitcast.1), custom_call_target="tpu_custom_call" | custom-call | tf_op jit(solution)/shard_map/pack/pallas_call | solution.py:412
  1.8 2.5 %collective-permute-start.2 = (f32[8,128]{1,0:T(8,128)S(1)}, f32[8,128]{1,0:T(8,128)S(1)}, u32[]{:S(2)}, u32[]{:S(2)}) collective-permute-start(f32[8,128]{1,0:T(8,128)S(1)} %get-tuple-element.5), channel_id=1, source_target_pairs={{0,3},{1,2},{2,1},{3,0},{4,7},{5,6},{6,5},{7,4},{8,11},{9,10},{10,... | collective-permute-start | bytes 12296 | tf_op jit(solution)/shard_map/ppermute | solution.py:433
  4.3 0.7 %collective-permute-start = (f32[8,128]{1,0:T(8,128)S(1)}, f32[8,128]{1,0:T(8,128)S(1)}, u32[]{:S(2)}, u32[]{:S(2)}) collective-permute-start(f32[8,128]{1,0:T(8,128)S(1)} %get-tuple-element.5), channel_id=1, source_target_pairs={{0,1},{1,0},{2,3},{3,2},{4,5},{5,4},{6,7},{7,6},{8,9},{9,8},{10,11... | collective-permute-start | bytes 12296 | tf_op jit(solution)/shard_map/ppermute | solution.py:431
  5.0 0.0 collective-permute-start.1
  5.0 0.8 %collective-permute-done.refs_1_ = f32[8,128]{1,0:T(8,128)S(1)} collective-permute-done((f32[8,128]{1,0:T(8,128)S(1)}, f32[8,128]{1,0:T(8,128)S(1)}, u32[]{:S(2)}, u32[]{:S(2)}) %collective-permute-start) | collective-permute-done | bytes 4128 | tf_op jit(solution)/shard_map/ppermute | solution.py:431
  5.8 3.2 %collective-permute-done.1.refs_2_ = f32[88,128]{1,0:T(8,128)S(1)} collective-permute-done((f32[88,128]{1,0:T(8,128)S(1)}, f32[88,128]{1,0:T(8,128)S(1)}, u32[]{:S(2)}, u32[]{:S(2)}) %collective-permute-start.1) | collective-permute-done | bytes 45088 | tf_op jit(solution)/shard_map/ppermute | solution.py:432
  9.0 0.0 collective-permute-done.2.refs_3_
  9.0 3.7 %collective-permute-start.4 = (f32[192,128]{1,0:T(8,128)S(1)}, f32[192,128]{1,0:T(8,128)S(1)}, u32[]{:S(2)}, u32[]{:S(2)}) collective-permute-start(f32[192,128]{1,0:T(8,128)S(1)} %constant_dynamic-update-slice_fusion), channel_id=1, source_target_pairs={{0,12},{2,14},{4,0},{6,2},{8,4},{10,6},{12,8},{14,10},{1,13},{3,15... | collective-permute-start | bytes 294920 | tf_op jit(solution)/shard_map/ppermute | solution.py:436
  12.7 0.0 collective-permute-start.3
  12.7 0.0 copy-start
  12.7 1.1 %collective-permute-start.5 = (f32[80,128]{1,0:T(8,128)S(1)}, f32[80,128]{1,0:T(8,128)S(1)}, u32[]{:S(2)}, u32[]{:S(2)}) collective-permute-start(f32[80,128]{1,0:T(8,128)S(1)} %pad_maximum_fusion), channel_id=1, source_target_pairs={{0,8},{2,10},{4,12},{6,14},{8,0},{10,2},{12,4},{14,6},{1,9},{3,11}... | collective-permute-start | bytes 122888 | tf_op jit(solution)/shard_map/ppermute | solution.py:436
  13.8 3.9 %collective-permute-done.5.refs_6_ = f32[80,128]{1,0:T(8,128)S(1)} collective-permute-done((f32[80,128]{1,0:T(8,128)S(1)}, f32[80,128]{1,0:T(8,128)S(1)}, u32[]{:S(2)}, u32[]{:S(2)}) %collective-permute-start.5) | collective-permute-done | bytes 40992 | tf_op jit(solution)/shard_map/ppermute | solution.py:436
  17.7 0.0 collective-permute-done.4.refs_5_
  17.7 1.4 %collective-permute-done.3.refs_4_ = f32[192,128]{1,0:T(8,128)S(1)} collective-permute-done((f32[192,128]{1,0:T(8,128)S(1)}, f32[192,128]{1,0:T(8,128)S(1)}, u32[]{:S(2)}, u32[]{:S(2)}) %collective-permute-start.3) | collective-permute-done | bytes 98336 | tf_op jit(solution)/shard_map/ppermute | solution.py:436
  19.1 0.0 copy-done
  19.1 2.1 %apply.1 = (f32[4,4,16,16]{3,2,1,0:T(8,128)}, f32[4,4,16,16]{3,2,1,0:T(8,128)}) custom-call(f32[88,128]{1,0:T(8,128)S(1)} %get-tuple-element.4.refs_0_, f32[8,128]{1,0:T(8,128)S(1)} %collective-permute-done.refs_1_, f32[88,128]{1,0:T(8,128)S(1)} %collective-permute-done.1.refs_2_, f32[8,128]{1,0:T(8,128)S(1)} %collective-permute-done.2.refs_3_, ...), custom_call_target="tpu_custom_call" | custom-call | tf_op jit(solution)/shard_map/apply/pallas_call | solution.py:451
  (9 shorter events, 0.0 us)
Async XLA Ops:
  1.8 7.2 %collective-permute-start.2 = (f32[8,128]{1,0:T(8,128)S(1)}, f32[8,128]{1,0:T(8,128)S(1)}, u32[]{:S(2)}, u32[]{:S(2)}) collective-permute-start(f32[8,128]{1,0:T(8,128)S(1)} %get-tuple-element.5), channel_id=1, source_target_pairs={{0,3},{1,2},{2,1},{3,0},{4,7},{5,6},{6,5},{7,4},{8,11},{9,10},{10,... | collective-permute-start | bytes 12296 | tf_op jit(solution)/shard_map/ppermute | solution.py:433
  4.3 1.5 %collective-permute-start = (f32[8,128]{1,0:T(8,128)S(1)}, f32[8,128]{1,0:T(8,128)S(1)}, u32[]{:S(2)}, u32[]{:S(2)}) collective-permute-start(f32[8,128]{1,0:T(8,128)S(1)} %get-tuple-element.5), channel_id=1, source_target_pairs={{0,1},{1,0},{2,3},{3,2},{4,5},{5,4},{6,7},{7,6},{8,9},{9,8},{10,11... | collective-permute-start | bytes 12296 | tf_op jit(solution)/shard_map/ppermute | solution.py:431
  5.0 4.0 %collective-permute-start.1 = (f32[88,128]{1,0:T(8,128)S(1)}, f32[88,128]{1,0:T(8,128)S(1)}, u32[]{:S(2)}, u32[]{:S(2)}) collective-permute-start(f32[88,128]{1,0:T(8,128)S(1)} %get-tuple-element.4.refs_0_), channel_id=1, source_target_pairs={{0,2},{2,0},{4,6},{6,4},{8,10},{10,8},{12,14},{14,12},{1,3},{3,1},... | collective-permute-start | bytes 135176 | tf_op jit(solution)/shard_map/ppermute | solution.py:432
  9.0 8.7 %collective-permute-start.4 = (f32[192,128]{1,0:T(8,128)S(1)}, f32[192,128]{1,0:T(8,128)S(1)}, u32[]{:S(2)}, u32[]{:S(2)}) collective-permute-start(f32[192,128]{1,0:T(8,128)S(1)} %constant_dynamic-update-slice_fusion), channel_id=1, source_target_pairs={{0,12},{2,14},{4,0},{6,2},{8,4},{10,6},{12,8},{14,10},{1,13},{3,15... | collective-permute-start | bytes 294920 | tf_op jit(solution)/shard_map/ppermute | solution.py:436
  12.7 6.4 %collective-permute-start.3 = (f32[192,128]{1,0:T(8,128)S(1)}, f32[192,128]{1,0:T(8,128)S(1)}, u32[]{:S(2)}, u32[]{:S(2)}) collective-permute-start(f32[192,128]{1,0:T(8,128)S(1)} %constant_dynamic-update-slice_fusion), channel_id=1, source_target_pairs={{0,4},{2,6},{4,8},{6,10},{8,12},{10,14},{12,0},{14,2},{1,5},{3,7},... | collective-permute-start | bytes 294920 | tf_op jit(solution)/shard_map/ppermute | solution.py:436
  12.7 6.4 %copy-start = (f32[4,16]{1,0:T(4,128)S(1)}, f32[4,16]{1,0:T(4,128)}, u32[]{:S(2)}) copy-start(f32[4,16]{1,0:T(4,128)} %refs_7_.1) | copy-start | bytes 772
  12.7 5.0 %collective-permute-start.5 = (f32[80,128]{1,0:T(8,128)S(1)}, f32[80,128]{1,0:T(8,128)S(1)}, u32[]{:S(2)}, u32[]{:S(2)}) collective-permute-start(f32[80,128]{1,0:T(8,128)S(1)} %pad_maximum_fusion), channel_id=1, source_target_pairs={{0,8},{2,10},{4,12},{6,14},{8,0},{10,2},{12,4},{14,6},{1,9},{3,11}... | collective-permute-start | bytes 122888 | tf_op jit(solution)/shard_map/ppermute | solution.py:436

commit v3 on v0

--- a/solution.py
+++ b/solution.py
@@ -1,13 +1,18 @@
+import functools
 import math
 
 import jax
 import jax.numpy as jnp
 from jax import lax
+from jax.experimental import pallas as pl
+from jax.experimental.pallas import tpu as pltpu
 from jax.sharding import PartitionSpec as P
+
 
 STEPS = 8
 SWEEPS = 4
 LON_DEV = 4
+MODEL_FLOPS = 10**6
 
 
 def extended(x, sides, width):
@@ -80,9 +85,9 @@
 
 
 def run_tangent(fields, coeffs, margin):
-    for repeat in range(STEPS // margin):
+    for _ in range(STEPS // margin):
         grown = extended(fields, (("tiles", 0),), margin)
-        for inner_step in range(margin):
+        for _ in range(margin):
             offset = (coeffs[0].shape[0] - grown.shape[0]) // 2
             grown = tangent_step(grown, coeffs, offset)
         fields = grown
@@ -90,9 +95,9 @@
 
 
 def run_adjoint(fields, coeffs, margin):
-    for repeat in range(STEPS // margin):
+    for _ in range(STEPS // margin):
         grown = extended(fields, (("tiles", 0),), margin)
-        for inner_step in range(margin):
+        for _ in range(margin):
             offset = (coeffs[0].shape[0] - grown.shape[0]) // 2
             grown = adjoint_step(grown, coeffs, offset)
         fields = grown
@@ -179,6 +184,317 @@
     return (covar + increment - forward, dual_vector - backward)
 
 
+SUB = 8
+LANES = 128
+VMEM_BYTES = 4 * 2**20
+
+
+def dense_fits(mesh, shape):
+    lons, wins, levels, lats = shape
+    tiles = mesh.shape["tiles"]
+    halves = levels // SUB
+    return (
+        levels % SUB == 0
+        and wins * halves * lats == LANES
+        and lons * halves * lats == LANES
+        and LANES % levels == 0
+        and lats % tiles == 0
+        and lons * lats + wins * (lats // tiles) <= LANES
+        and mesh.shape["subwin"] == 2
+        and tiles % 2 == 0
+        and tiles // 2 >= 4
+        and STEPS <= 2 * lons
+    )
+
+
+def lane_index():
+    return lax.broadcasted_iota(jnp.int32, (SUB, LANES), 1)
+
+
+def picked(values, index):
+    return jnp.take_along_axis(values, index, axis=1)
+
+
+class Rows:
+    def __init__(self, lons, tiles, main, peer, left, right, far=()):
+        self.lons, self.tiles = lons, tiles
+        self.even = lax.axis_index("tiles") % 2 == 0
+        full = 2 * lons + 3
+        whole = {row: row for row in range(full)}
+        held = {row: row for row in range(lons)} | {full - 1: lons}
+        self.places = ({}, {})
+        for odd, sign in enumerate((1, -1)):
+            self.add(odd, 0, main, whole, 0)
+            self.add(odd, sign, peer, whole, 0)
+            for offset, ref in ((-2, left), (2, right)):
+                self.add(odd, offset, ref, whole, 0)
+                self.add(odd, offset + sign, ref, whole, full)
+            for k, ref in enumerate(far):
+                self.add(odd, 2 * (k + 2), ref, held, 0)
+                self.add(odd, 2 * (k + 2) + sign, ref, held, lons + 1)
+
+    def add(self, odd, offset, ref, rows, start):
+        for row, at in rows.items():
+            self.places[odd][offset % self.tiles, row] = (ref, (start + at) * SUB)
+
+    def __call__(self, offset, row):
+        key = (offset % self.tiles, row)
+        (one, at), (two, to) = self.places[0][key], self.places[1][key]
+        if one is two and at == to:
+            return one[at : at + SUB, :]
+        return jnp.where(self.even, one[at : at + SUB, :], two[to : to + SUB, :])
+
+
+def pack_kernel(*refs):
+    arrays, main_ref, held, arrived = refs[:6], refs[6], refs[7:13], refs[13]
+    copies = [
+        pltpu.make_async_copy(source, target, arrived.at[k])
+        for k, (source, target) in enumerate(zip(arrays, held))
+    ]
+    for copy in copies:
+        copy.start()
+    for copy in copies:
+        copy.wait()
+    inc_ref, dual_ref, u_ref, v_ref, land_ref, len_ref = held
+    lons, wins, levels, lats = inc_ref.shape
+    halves = levels // SUB
+    own_lats = len_ref.shape[0]
+
+    def put(row, slot, value):
+        main_ref[row * SUB : (row + 1) * SUB, slot * lats : (slot + 1) * lats] = value
+
+    for i in range(lons):
+        for half in range(halves):
+            rows = slice(half * SUB, (half + 1) * SUB)
+            for s in range(wins):
+                put(i, s * halves + half, dual_ref[i, s, rows, :])
+                put(lons + i, s * halves + half, inc_ref[i, s, rows, :])
+            put(2 * lons, i * halves + half, u_ref[i, rows, :])
+            put(2 * lons + 1, i * halves + half, v_ref[i, rows, :])
+    base = (2 * lons + 2) * SUB
+    main_ref[base : base + SUB, :] = jnp.zeros((SUB, LANES), jnp.float32)
+    for i in range(lons):
+        mixing = 0.15 + 0.09 * land_ref[i : i + 1, :].astype(jnp.float32)
+        main_ref[base : base + SUB, i * lats : (i + 1) * lats] = jnp.broadcast_to(mixing, (SUB, lats))
+    for j in range(own_lats):
+        at = lons * lats + j * wins
+        main_ref[base : base + SUB, at : at + wins] = jnp.broadcast_to(
+            len_ref[j : j + 1, :], (SUB, wins)
+        )
+
+
+def model_kernel(geometry, main, peer, left, right, forward_ref, backward_ref, edge_ref, coeff_ref):
+    lons, wins, _, lats, tiles = geometry
+    group = LANES // wins
+    rows = Rows(lons, tiles, main, peer, left, right)
+    lane = lane_index()
+    lat = lane % lats
+    span = lons + 2 * STEPS
+    forward, backward = [], []
+    for r in range(span):
+        offset, i = (r - STEPS) // lons, (r - STEPS) % lons
+        spot = i * group + lane % group
+        wind_u = 0.5 * picked(rows(offset, 2 * lons), spot)
+        wind_v = 0.5 * picked(rows(offset, 2 * lons + 1), spot)
+        mixing = picked(rows(offset, 2 * lons + 2), i * lats + lat)
+        coeff_ref[r, 0] = 1.0 - 4.0 * mixing
+        coeff_ref[r, 1] = mixing - wind_u
+        coeff_ref[r, 2] = mixing + wind_u
+        coeff_ref[r, 3] = jnp.where(lat == lats - 1, 0.0, mixing - wind_v)
+        coeff_ref[r, 4] = jnp.where(lat == 0, 0.0, mixing + wind_v)
+        forward.append(rows(offset, lons + i))
+        backward.append(rows(offset, i))
+
+    def north(values):
+        return pltpu.roll(values, LANES - 1, 1)
+
+    def south(values):
+        return pltpu.roll(values, 1, 1)
+
+    for step in range(STEPS):
+        ahead, behind = [], []
+        for p in range(1, len(forward) - 1):
+            r = p + step
+            middle = forward[p]
+            ahead.append(
+                coeff_ref[r, 0] * middle
+                + coeff_ref[r, 1] * forward[p + 1]
+                + coeff_ref[r, 2] * forward[p - 1]
+                + coeff_ref[r, 3] * north(middle)
+                + coeff_ref[r, 4] * south(middle)
+            )
+            middle = backward[p]
+            behind.append(
+                coeff_ref[r, 0] * middle
+                + coeff_ref[r - 1, 1] * backward[p - 1]
+                + coeff_ref[r + 1, 2] * backward[p + 1]
+                + south(coeff_ref[r, 3] * middle)
+                + north(coeff_ref[r, 4] * middle)
+            )
+        forward, backward = ahead, behind
+    first = lax.axis_index("subwin") == 0
+    for i in range(lons):
+        at = slice(i * SUB, (i + 1) * SUB)
+        forward_ref[at, :] = forward[i]
+        backward_ref[at, :] = backward[i]
+        edge_ref[at, :] = jnp.where(first, forward[i], backward[i])
+
+
+def unpack(ref, i, value, wins, halves, lats):
+    for s in range(wins):
+        for half in range(halves):
+            at = (s * halves + half) * lats
+            ref[i, s, half * SUB : (half + 1) * SUB, :] = value[:, at : at + lats]
+
+
+def finish_kernel(geometry, *refs):
+    lons, wins, levels, lats, tiles = geometry
+    group = LANES // wins
+    own_lats = lats // tiles
+    count = lons * tiles
+    main, peer, left, right = refs[:4]
+    far, (forward_ref, backward_ref, edge_ref, spread_ref) = refs[4:-9], refs[-9:-5]
+    model_ref, dual_out_ref, model_held, dual_held, sent = refs[-5:]
+    first = lax.axis_index("subwin") == 0
+    rows = Rows(lons, tiles, main, peer, left, right, far)
+    lane = lane_index()
+    tile = lax.axis_index("tiles")
+
+    rest = []
+    for i in range(lons):
+        at = slice(i * SUB, (i + 1) * SUB)
+        edge = edge_ref[at, :]
+        ahead = jnp.where(lane < LANES - group, forward_ref[at, :], jnp.where(first, 0.0, edge))
+        behind = jnp.where(lane >= group, backward_ref[at, :], jnp.where(first, edge, 0.0))
+        rest.append(rows(0, lons + i) - pltpu.roll(ahead, group, 1))
+        dual_side = rows(0, i) - pltpu.roll(behind, LANES - group, 1)
+        unpack(dual_held, i, dual_side, wins, levels // SUB, lats)
+    dual_copy = pltpu.make_async_copy(dual_held, dual_out_ref, sent.at[0])
+    dual_copy.start()
+
+    length = jnp.zeros((SUB, LANES), jnp.float32)
+    index = lons * lats + wins * (lane % own_lats) + lane // group
+    owner = lane % lats // own_lats
+    for offset in range(tiles):
+        here = picked(rows(offset, 2 * lons + 2), index)
+        length = jnp.where(owner == (tile + offset) % tiles, here, length)
+    half = count // 2
+    damped = []
+    for wave in range(half + 1):
+        basic = 1.0 - math.cos(2.0 * math.pi * wave / count)
+        inverse = 1.0 / (1.0 + (2.0 * basic) * length)
+        squared = inverse * inverse
+        weight = (1.0 if wave in (0, half) else 2.0) / count
+        damped.append(squared * (squared * weight))
+
+    def waves(gap, start):
+        total = None
+        for wave in range(start, half + 1, 2):
+            factor = math.cos(2.0 * math.pi * (wave * gap % count) / count)
+            term = damped[wave] if factor == 1.0 else damped[wave] * factor
+            total = term if total is None else total + term
+        return total
+
+    weights = [None] * (half + 1)
+    for gap in range(half // 2 + 1):
+        even, odd = waves(gap, 0), waves(gap, 1)
+        weights[gap] = even + odd
+        weights[half - gap] = even - odd if half % 2 == 0 else None
+    for gap in range(half + 1):
+        if weights[gap] is None:
+            weights[gap] = waves(gap, 0) + waves(gap, 1)
+
+    smooth = [None] * lons
+    for offset in range(tiles):
+        for j in range(lons):
+            value = rows(offset, j)
+            for i in range(lons):
+                gap = (i - (offset * lons + j)) % count
+                term = weights[min(gap, count - gap)] * value
+                smooth[i] = term if smooth[i] is None else smooth[i] + term
+
+    level = lax.broadcasted_iota(jnp.int32, (SUB, LANES), 0) + SUB * (lane % group // lats)
+    scale = jnp.zeros((SUB, LANES), jnp.float32)
+    for s in range(wins):
+        row = jnp.concatenate(
+            [jnp.broadcast_to(spread_ref[s : s + 1, :], (SUB, levels))] * (LANES // levels), axis=1
+        )
+        scale = jnp.where(lane // group == s, picked(row, level), scale)
+    square = scale * scale
+    for i in range(lons):
+        unpack(model_held, i, square * smooth[i] + rest[i], wins, levels // SUB, lats)
+    model_copy = pltpu.make_async_copy(model_held, model_ref, sent.at[1])
+    model_copy.start()
+    dual_copy.wait()
+    model_copy.wait()
+
+
+def kernel_call(kernel, inputs, outputs, scratch=(), flops=0, space=pltpu.VMEM):
+    vmem = pl.BlockSpec(memory_space=pltpu.VMEM)
+    return pl.pallas_call(
+        kernel,
+        out_shape=outputs,
+        in_specs=[vmem] * len(inputs),
+        out_specs=(pl.BlockSpec(memory_space=space),) * len(outputs),
+        scratch_shapes=list(scratch),
+        compiler_params=pltpu.CompilerParams(vmem_limit_bytes=VMEM_BYTES),
+        cost_estimate=pl.CostEstimate(flops=flops, bytes_accessed=2**18, transcendentals=0),
+    )(*inputs)
+
+
+def dense_body(increment, dual_vector, wind_u, wind_v, land_sea, length_sq, spread):
+    lons, wins, levels, lats = increment.shape
+    tiles = lax.axis_size("tiles")
+    rings = tiles // 2
+    geometry = (lons, wins, levels, lats, tiles)
+
+    def rows(count):
+        return jax.ShapeDtypeStruct((count * SUB, LANES), jnp.float32)
+
+    full = jax.ShapeDtypeStruct(increment.shape, jnp.float32)
+    arrays = (increment, dual_vector, wind_u, wind_v, land_sea, length_sq.T)
+    main = pl.pallas_call(
+        pack_kernel,
+        out_shape=rows(2 * lons + 3),
+        in_specs=[pl.BlockSpec(memory_space=pltpu.HBM)] * len(arrays),
+        out_specs=pl.BlockSpec(memory_space=pltpu.VMEM),
+        scratch_shapes=[pltpu.VMEM(x.shape, x.dtype) for x in arrays]
+        + [pltpu.SemaphoreType.DMA((len(arrays),))],
+        compiler_params=pltpu.CompilerParams(vmem_limit_bytes=VMEM_BYTES),
+        name="pack",
+    )(*[pltpu.with_memory_space_constraint(x, pltpu.HBM) for x in arrays])
+
+    def moved(x, by):
+        pairs = [(t, (t // 2 + by) % rings * 2 + t % 2) for t in range(tiles)]
+        return lax.ppermute(x, "tiles", pairs)
+
+    peer = lax.ppermute(main, "tiles", [(t, t ^ 1) for t in range(tiles)])
+    held, misc = lons * SUB, (2 * lons + 2) * SUB
+    pair = jnp.concatenate([main, peer])
+    left = moved(pair, 1)
+    right = moved(pair, -1)
+    short = jnp.concatenate([main[:held], main[misc:], peer[:held], peer[misc:]])
+    far = [moved(short, -d) for d in range(2, rings - 1)]
+    near = (main, peer, left, right)
+    forward, backward, edge = kernel_call(
+        functools.partial(model_kernel, geometry),
+        near,
+        (rows(lons), rows(lons), rows(lons)),
+        [pltpu.VMEM((lons + 2 * STEPS, 5, SUB, LANES), jnp.float32)],
+        flops=MODEL_FLOPS,
+    )
+    edge = lax.ppermute(edge, "subwin", [(0, 1), (1, 0)])
+    model_side, dual_side = kernel_call(
+        functools.partial(finish_kernel, geometry),
+        (*near, *far, forward, backward, edge, spread),
+        (full, full),
+        [pltpu.VMEM(full.shape, full.dtype)] * 2 + [pltpu.SemaphoreType.DMA((2,))],
+        flops=MODEL_FLOPS,
+        space=pltpu.HBM,
+    )
+    return model_side, dual_side
+
+
 def solution(mesh):
     placed = (
         P(("groups", "tiles"), "subwin", None, None),
@@ -189,8 +505,14 @@
         P("subwin", "tiles"),
         P("subwin", None),
     )
+
+    def local(*arrays):
+        if dense_fits(mesh, arrays[0].shape):
+            return dense_body(*arrays)
+        return body(*arrays)
+
     return jax.shard_map(
-        body,
+        local,
         mesh=mesh,
         in_specs=placed,
         out_specs=(

time: 89.4 us -> 20.6 us (0.23)
  starting transfers between devices: 43.3 us -> 8.36 us
  waiting for transfers between devices: 22.6 us -> 8.42 us
  local copies, waits for them, and re-layouts: 12.8 us -> 0.01 us
  other arithmetic: 5.55 us -> 0.01 us
  matrix products: 3.17 us -> 0 us
  Pallas kernels: 0 us -> 2.96 us
    ppermute x16 -> x5, starting transfers between devices: 36.1 us -> 8.36 us  [the longest x3 5.25 us: moved(): return lax.ppermute(x, 'tiles', pairs)]
    all_to_all x2 -> x0, waiting for transfers between devices: 12.1 us -> none  [the longest x1 6.35 us: body(): lax.all_to_all(weighted, 'tiles', split_axis=3, concat_axis=0, tiled=True)]
    unnamed x24 -> x2, local copies, waits for them, and re-layouts: 8.26 us -> 0.01 us
    all_to_all x2 -> x0, starting transfers between devices: 7.17 us -> none  [the longest x1 3.83 us: body(): lax.all_to_all(weighted, 'tiles', split_axis=3, concat_axis=0, tiled=True)]
    dot_general x12 -> x0, matrix products: 3.17 us -> none  [contract(): return jnp.einsum(form, first, second, precision=lax.Precision.HIGHEST)]
    pallas_call x0 -> x3, Pallas kernels: none -> 2.96 us  [the longest x2 1.79 us: kernel_call(): pl.pallas_call(kernel, out_shape=outputs, in_specs=[vmem] * len(inputs),...]
    slice x62 -> x4, local copies, waits for them, and re-layouts: 2.7 us -> 0.01 us  [the longest x1 0.01 us: dense_body(): main[:held]]
    add x7 -> x0, other arithmetic: 2.53 us -> none  [adjoint_step(): centre * middle + (eastward * fields)[:-2] + (westward * fields)[2:]]
  transfers between devices with their start and end apart: 18 -> 5, of which waited for: 9 -> 4; matrix products, arithmetic and copies ran while one was open for 5% -> 0% of each run, Pallas kernels for 0% -> 4%
where the time goes in v3:
time: 20.6 us; the launch traced here: 20.4 us
  waiting for transfers between devices  8.42 us (41%)
  starting transfers between devices  8.36 us (41%)
  Pallas kernels  2.96 us (14%)
  between operations  0.68 us (3%)
    ppermute x3, starting transfers between devices, moved(): return lax.ppermute(x, 'tiles', pairs)  5.25 us
    ppermute x3, waiting for transfers between devices, moved(): return lax.ppermute(x, 'tiles', pairs)  5.24 us
    ppermute x1, starting transfers between devices, dense_body(): peer = lax.ppermute(main, 'tiles', [(t, t ^ 1) for t in range(tiles)])  3.03 us
    ppermute x1, waiting for transfers between devices, dense_body(): peer = lax.ppermute(main, 'tiles', [(t, t ^ 1) for t in range(tiles)])  2.02 us
    pallas_call x2, Pallas kernels, kernel_call(): pl.pallas_call(kernel, out_shape=outputs, in_specs=[vmem] * len(inputs),...  1.79 us
    pallas_call x1, Pallas kernels, dense_body(): pl.pallas_call(pack_kernel, out_shape=rows(2 * lons + 3), in_specs=[pl.Bl...  1.17 us
    ppermute x1, waiting for transfers between devices, dense_body(): edge = lax.ppermute(edge, 'subwin', [(0, 1), (1, 0)])  1.16 us
  transfers between devices with their start and end apart: 5, of which 4 were waited for; matrix products, arithmetic and copies ran while one was open for 0% of the time, Pallas kernels for 4%

profile of v3, /device:TPU:0, one launch (start us, length us, event | category | flops | bytes accessed | tf_op | source)
XLA Modules:
  0.0 20.4 jit_solution(4643927753874482432)
XLA Ops:
  0.6 1.2 %pack.1.main.refs_0_ = f32[88,128]{1,0:T(8,128)S(1)} custom-call(f32[4,4,16,16]{3,2,1,0:T(8,128)} %refs_0_.1, f32[4,4,16,16]{3,2,1,0:T(8,128)} %refs_1_.1, f32[4,16,16]{2,1,0:T(8,128)} %refs_2_.1, f32[4,16,16]{2,1,0:T(8,128)} %refs_3_.1, s32[4,16]{1,0:T(4,128)} %refs_4_.1, f32[2,4]{1,0:T(2,128)} %bitcast.1), custom_call_target="tpu_custom_call" | custom-call | tf_op jit(solution)/shard_map/pack/pallas_call | solution.py:456
  1.8 3.0 %collective-permute-start = (f32[88,128]{1,0:T(8,128)S(1)}, f32[88,128]{1,0:T(8,128)S(1)}, u32[]{:S(2)}, u32[]{:S(2)}) collective-permute-start(f32[88,128]{1,0:T(8,128)S(1)} %pack.1.main.refs_0_), channel_id=1, source_target_pairs={{0,2},{2,0},{4,6},{6,4},{8,10},{10,8},{12,14},{14,12},{1,3},{3,1},... | collective-permute-start | bytes 135176 | tf_op jit(solution)/shard_map/ppermute | solution.py:471
  4.8 2.0 %collective-permute-done.peer.refs_1_ = f32[88,128]{1,0:T(8,128)S(1)} collective-permute-done((f32[88,128]{1,0:T(8,128)S(1)}, f32[88,128]{1,0:T(8,128)S(1)}, u32[]{:S(2)}, u32[]{:S(2)}) %collective-permute-start) | collective-permute-done | bytes 45088 | tf_op jit(solution)/shard_map/ppermute | solution.py:471
  6.9 4.2 %collective-permute-start.2 = (f32[176,128]{1,0:T(8,128)S(1)}, f32[176,128]{1,0:T(8,128)S(1)}, u32[]{:S(2)}, u32[]{:S(2)}) collective-permute-start(f32[176,128]{1,0:T(8,128)S(1)} %pad_maximum_fusion), channel_id=1, source_target_pairs={{0,12},{2,14},{4,0},{6,2},{8,4},{10,6},{12,8},{14,10},{1,13},{3,15... | collective-permute-start | bytes 270344 | tf_op jit(solution)/shard_map/ppermute | solution.py:469
  11.1 0.0 collective-permute-start.1
  11.1 1.1 %collective-permute-start.3 = (f32[80,128]{1,0:T(8,128)S(1)}, f32[80,128]{1,0:T(8,128)S(1)}, u32[]{:S(2)}, u32[]{:S(2)}) collective-permute-start(f32[80,128]{1,0:T(8,128)S(1)} %pad_maximum_fusion.1), channel_id=1, source_target_pairs={{0,8},{2,10},{4,12},{6,14},{8,0},{10,2},{12,4},{14,6},{1,9},{3,11}... | collective-permute-start | bytes 122888 | tf_op jit(solution)/shard_map/ppermute | solution.py:469
  12.1 1.0 %collective-permute-done.2.right.refs_3_ = f32[176,128]{1,0:T(8,128)S(1)} collective-permute-done((f32[176,128]{1,0:T(8,128)S(1)}, f32[176,128]{1,0:T(8,128)S(1)}, u32[]{:S(2)}, u32[]{:S(2)}) %collective-permute-start.2) | collective-permute-done | bytes 90144 | tf_op jit(solution)/shard_map/ppermute | solution.py:469
  13.2 4.2 %collective-permute-done.1.left.refs_2_ = f32[176,128]{1,0:T(8,128)S(1)} collective-permute-done((f32[176,128]{1,0:T(8,128)S(1)}, f32[176,128]{1,0:T(8,128)S(1)}, u32[]{:S(2)}, u32[]{:S(2)}) %collective-permute-start.1) | collective-permute-done | bytes 90144 | tf_op jit(solution)/shard_map/ppermute | solution.py:469
  17.4 0.8 %shard_map.86 = (f32[32,128]{1,0:T(8,128)S(1)}, f32[32,128]{1,0:T(8,128)S(1)}, f32[32,128]{1,0:T(8,128)S(1)}) custom-call(f32[88,128]{1,0:T(8,128)S(1)} %pack.1.main.refs_0_, f32[88,128]{1,0:T(8,128)S(1)} %collective-permute-done.peer.refs_1_, f32[176,128]{1,0:T(8,128)S(1)} %collective-permute-done.1.left.refs_2_, ...), custom_call_target="tpu_custom_call" | custom-call | flops 1000000 | bytes 262144 | tf_op jit(solution)/shard_map/pallas_call | solution.py:434
  18.2 0.0 copy-start
  18.2 0.1 collective-permute-start.4
  18.3 0.0 collective-permute-done.3.refs_4_
  18.3 1.2 %collective-permute-done.4.refs_7_ = f32[32,128]{1,0:T(8,128)S(1)} collective-permute-done((f32[32,128]{1,0:T(8,128)S(1)}, f32[32,128]{1,0:T(8,128)S(1)}, u32[]{:S(2)}, u32[]{:S(2)}) %collective-permute-start.4) | collective-permute-done | bytes 16416 | tf_op jit(solution)/shard_map/ppermute | solution.py:486
  19.5 0.0 copy-done
  19.5 1.0 %shard_map.87 = (f32[4,4,16,16]{3,2,1,0:T(8,128)}, f32[4,4,16,16]{3,2,1,0:T(8,128)}) custom-call(f32[88,128]{1,0:T(8,128)S(1)} %pack.1.main.refs_0_, f32[88,128]{1,0:T(8,128)S(1)} %collective-permute-done.peer.refs_1_, f32[176,128]{1,0:T(8,128)S(1)} %collective-permute-done.1.left.refs_2_, f32[176,128]{1,0:T(8,128)S(1)} %collective-permute-done.2.right.refs_3_, ...), custom_call_target="tpu_custom_call" | custom-call | flops 1000000 | bytes 262144 | tf_op jit(solution)/shard_map/pallas_call | solution.py:434
  (6 shorter events, 0.0 us)
Async XLA Ops:
  1.8 5.1 %collective-permute-start = (f32[88,128]{1,0:T(8,128)S(1)}, f32[88,128]{1,0:T(8,128)S(1)}, u32[]{:S(2)}, u32[]{:S(2)}) collective-permute-start(f32[88,128]{1,0:T(8,128)S(1)} %pack.1.main.refs_0_), channel_id=1, source_target_pairs={{0,2},{2,0},{4,6},{6,4},{8,10},{10,8},{12,14},{14,12},{1,3},{3,1},... | collective-permute-start | bytes 135176 | tf_op jit(solution)/shard_map/ppermute | solution.py:471
  6.9 6.3 %collective-permute-start.2 = (f32[176,128]{1,0:T(8,128)S(1)}, f32[176,128]{1,0:T(8,128)S(1)}, u32[]{:S(2)}, u32[]{:S(2)}) collective-permute-start(f32[176,128]{1,0:T(8,128)S(1)} %pad_maximum_fusion), channel_id=1, source_target_pairs={{0,12},{2,14},{4,0},{6,2},{8,4},{10,6},{12,8},{14,10},{1,13},{3,15... | collective-permute-start | bytes 270344 | tf_op jit(solution)/shard_map/ppermute | solution.py:469
  11.1 6.3 %collective-permute-start.1 = (f32[176,128]{1,0:T(8,128)S(1)}, f32[176,128]{1,0:T(8,128)S(1)}, u32[]{:S(2)}, u32[]{:S(2)}) collective-permute-start(f32[176,128]{1,0:T(8,128)S(1)} %pad_maximum_fusion), channel_id=1, source_target_pairs={{0,4},{2,6},{4,8},{6,10},{8,12},{10,14},{12,0},{14,2},{1,5},{3,7},... | collective-permute-start | bytes 270344 | tf_op jit(solution)/shard_map/ppermute | solution.py:469
  11.1 7.2 %collective-permute-start.3 = (f32[80,128]{1,0:T(8,128)S(1)}, f32[80,128]{1,0:T(8,128)S(1)}, u32[]{:S(2)}, u32[]{:S(2)}) collective-permute-start(f32[80,128]{1,0:T(8,128)S(1)} %pad_maximum_fusion.1), channel_id=1, source_target_pairs={{0,8},{2,10},{4,12},{6,14},{8,0},{10,2},{12,4},{14,6},{1,9},{3,11}... | collective-permute-start | bytes 122888 | tf_op jit(solution)/shard_map/ppermute | solution.py:469
  18.2 1.3 %copy-start = (f32[4,16]{1,0:T(4,128)S(1)}, f32[4,16]{1,0:T(4,128)}, u32[]{:S(2)}) copy-start(f32[4,16]{1,0:T(4,128)} %refs_8_.1) | copy-start | bytes 772
  18.2 1.2 %collective-permute-start.4 = (f32[32,128]{1,0:T(8,128)S(1)}, f32[32,128]{1,0:T(8,128)S(1)}, u32[]{:S(2)}, u32[]{:S(2)}) collective-permute-start(f32[32,128]{1,0:T(8,128)S(1)} %get-tuple-element.7), channel_id=1, source_target_pairs={{0,1},{1,0},{2,3},{3,2},{4,5},{5,4},{6,7},{7,6},{8,9},{9,8},{10,11... | collective-permute-start | bytes 49160 | tf_op jit(solution)/shard_map/ppermute | solution.py:486

commit v4 on v3

--- a/solution.py
+++ b/solution.py
@@ -216,33 +216,38 @@
 
 
 class Rows:
-    def __init__(self, lons, tiles, main, peer, left, right, far=()):
-        self.lons, self.tiles = lons, tiles
+    def __init__(self, lons, tiles, main, peer, left=None, right=None, far=()):
+        self.tiles = tiles
         self.even = lax.axis_index("tiles") % 2 == 0
         full = 2 * lons + 3
-        whole = {row: row for row in range(full)}
-        held = {row: row for row in range(lons)} | {full - 1: lons}
+        whole = {row - 1: row * SUB for row in range(full)}
+        held = {row - 1: row * SUB for row in range(lons + 1)}
         self.places = ({}, {})
         for odd, sign in enumerate((1, -1)):
-            self.add(odd, 0, main, whole, 0)
-            self.add(odd, sign, peer, whole, 0)
+            self.add(odd, 0, main, whole, 0, 0)
+            self.add(odd, sign, peer, whole, 0, 0)
             for offset, ref in ((-2, left), (2, right)):
-                self.add(odd, offset, ref, whole, 0)
-                self.add(odd, offset + sign, ref, whole, full)
+                self.add(odd, offset, ref, whole, 0, 0)
+                self.add(odd, offset + sign, ref, whole, full - 1, SUB // 2)
             for k, ref in enumerate(far):
-                self.add(odd, 2 * (k + 2), ref, held, 0)
-                self.add(odd, 2 * (k + 2) + sign, ref, held, lons + 1)
-
-    def add(self, odd, offset, ref, rows, start):
+                self.add(odd, 2 * (k + 2), ref, held, 0, 0)
+                self.add(odd, 2 * (k + 2) + sign, ref, held, lons, SUB // 2)
+
+    def add(self, odd, offset, ref, rows, start, misc):
         for row, at in rows.items():
-            self.places[odd][offset % self.tiles, row] = (ref, (start + at) * SUB)
+            at = misc if row < 0 else start * SUB + at
+            self.places[odd][offset % self.tiles, row] = (ref, at)
 
     def __call__(self, offset, row):
         key = (offset % self.tiles, row)
-        (one, at), (two, to) = self.places[0][key], self.places[1][key]
-        if one is two and at == to:
-            return one[at : at + SUB, :]
-        return jnp.where(self.even, one[at : at + SUB, :], two[to : to + SUB, :])
+        places = [self.places[odd][key] for odd in (0, 1)]
+        if row < 0:
+            values = [jnp.broadcast_to(ref[at : at + 1, :], (SUB, LANES)) for ref, at in places]
+        else:
+            values = [ref[at : at + SUB, :] for ref, at in places]
+        if places[0][0] is places[1][0] and places[0][1] == places[1][1]:
+            return values[0]
+        return jnp.where(self.even, values[0], values[1])
 
 
 def pack_kernel(*refs):
@@ -261,7 +266,8 @@
     own_lats = len_ref.shape[0]
 
     def put(row, slot, value):
-        main_ref[row * SUB : (row + 1) * SUB, slot * lats : (slot + 1) * lats] = value
+        at = (row + 1) * SUB
+        main_ref[at : at + SUB, slot * lats : (slot + 1) * lats] = value
 
     for i in range(lons):
         for half in range(halves):
@@ -271,32 +277,39 @@
                 put(lons + i, s * halves + half, inc_ref[i, s, rows, :])
             put(2 * lons, i * halves + half, u_ref[i, rows, :])
             put(2 * lons + 1, i * halves + half, v_ref[i, rows, :])
-    base = (2 * lons + 2) * SUB
-    main_ref[base : base + SUB, :] = jnp.zeros((SUB, LANES), jnp.float32)
+    main_ref[:SUB, :] = jnp.zeros((SUB, LANES), jnp.float32)
     for i in range(lons):
         mixing = 0.15 + 0.09 * land_ref[i : i + 1, :].astype(jnp.float32)
-        main_ref[base : base + SUB, i * lats : (i + 1) * lats] = jnp.broadcast_to(mixing, (SUB, lats))
+        main_ref[:SUB, i * lats : (i + 1) * lats] = jnp.broadcast_to(mixing, (SUB, lats))
     for j in range(own_lats):
         at = lons * lats + j * wins
-        main_ref[base : base + SUB, at : at + wins] = jnp.broadcast_to(
+        main_ref[:SUB, at : at + wins] = jnp.broadcast_to(
             len_ref[j : j + 1, :], (SUB, wins)
         )
 
 
-def model_kernel(geometry, main, peer, left, right, forward_ref, backward_ref, edge_ref, coeff_ref):
+def north(values):
+    return pltpu.roll(values, LANES - 1, 1)
+
+
+def south(values):
+    return pltpu.roll(values, 1, 1)
+
+
+def model_kernel(geometry, *refs):
     lons, wins, _, lats, tiles = geometry
+    near, (forward_ref, backward_ref, edge_ref, coeff_ref) = refs[:-4], refs[-4:]
     group = LANES // wins
-    rows = Rows(lons, tiles, main, peer, left, right)
+    rows = Rows(lons, tiles, *near)
     lane = lane_index()
     lat = lane % lats
-    span = lons + 2 * STEPS
     forward, backward = [], []
-    for r in range(span):
+    for r in range(lons + 2 * STEPS):
         offset, i = (r - STEPS) // lons, (r - STEPS) % lons
         spot = i * group + lane % group
         wind_u = 0.5 * picked(rows(offset, 2 * lons), spot)
         wind_v = 0.5 * picked(rows(offset, 2 * lons + 1), spot)
-        mixing = picked(rows(offset, 2 * lons + 2), i * lats + lat)
+        mixing = picked(rows(offset, -1), i * lats + lat)
         coeff_ref[r, 0] = 1.0 - 4.0 * mixing
         coeff_ref[r, 1] = mixing - wind_u
         coeff_ref[r, 2] = mixing + wind_u
@@ -304,13 +317,6 @@
         coeff_ref[r, 4] = jnp.where(lat == 0, 0.0, mixing + wind_v)
         forward.append(rows(offset, lons + i))
         backward.append(rows(offset, i))
-
-    def north(values):
-        return pltpu.roll(values, LANES - 1, 1)
-
-    def south(values):
-        return pltpu.roll(values, 1, 1)
-
     for step in range(STEPS):
         ahead, behind = [], []
         for p in range(1, len(forward) - 1):
@@ -347,36 +353,22 @@
             ref[i, s, half * SUB : (half + 1) * SUB, :] = value[:, at : at + lats]
 
 
-def finish_kernel(geometry, *refs):
+def filter_kernel(geometry, *refs):
     lons, wins, levels, lats, tiles = geometry
     group = LANES // wins
     own_lats = lats // tiles
     count = lons * tiles
     main, peer, left, right = refs[:4]
-    far, (forward_ref, backward_ref, edge_ref, spread_ref) = refs[4:-9], refs[-9:-5]
-    model_ref, dual_out_ref, model_held, dual_held, sent = refs[-5:]
-    first = lax.axis_index("subwin") == 0
+    far, (spread_ref, covar_ref) = refs[4:-2], refs[-2:]
     rows = Rows(lons, tiles, main, peer, left, right, far)
     lane = lane_index()
     tile = lax.axis_index("tiles")
-
-    rest = []
-    for i in range(lons):
-        at = slice(i * SUB, (i + 1) * SUB)
-        edge = edge_ref[at, :]
-        ahead = jnp.where(lane < LANES - group, forward_ref[at, :], jnp.where(first, 0.0, edge))
-        behind = jnp.where(lane >= group, backward_ref[at, :], jnp.where(first, edge, 0.0))
-        rest.append(rows(0, lons + i) - pltpu.roll(ahead, group, 1))
-        dual_side = rows(0, i) - pltpu.roll(behind, LANES - group, 1)
-        unpack(dual_held, i, dual_side, wins, levels // SUB, lats)
-    dual_copy = pltpu.make_async_copy(dual_held, dual_out_ref, sent.at[0])
-    dual_copy.start()
 
     length = jnp.zeros((SUB, LANES), jnp.float32)
     index = lons * lats + wins * (lane % own_lats) + lane // group
     owner = lane % lats // own_lats
     for offset in range(tiles):
-        here = picked(rows(offset, 2 * lons + 2), index)
+        here = picked(rows(offset, -1), index)
         length = jnp.where(owner == (tile + offset) % tiles, here, length)
     half = count // 2
     damped = []
@@ -422,11 +414,34 @@
         scale = jnp.where(lane // group == s, picked(row, level), scale)
     square = scale * scale
     for i in range(lons):
-        unpack(model_held, i, square * smooth[i] + rest[i], wins, levels // SUB, lats)
-    model_copy = pltpu.make_async_copy(model_held, model_ref, sent.at[1])
-    model_copy.start()
-    dual_copy.wait()
-    model_copy.wait()
+        covar_ref[i * SUB : (i + 1) * SUB, :] = square * smooth[i]
+
+
+def finish_kernel(geometry, *refs):
+    lons, wins, levels, lats, _ = geometry
+    main, forward_ref, backward_ref, swapped_ref, covar_ref = refs[:5]
+    outs, held, sent = refs[5:7], refs[7:9], refs[9]
+    group = LANES // wins
+    lane = lane_index()
+    first = lax.axis_index("subwin") == 0
+    copies = [pltpu.make_async_copy(held[k], outs[k], sent.at[k]) for k in (0, 1)]
+    for i in range(lons):
+        at = slice(i * SUB, (i + 1) * SUB)
+        edge = jnp.where(first, swapped_ref[at, :], 0.0)
+        behind = jnp.where(lane >= group, backward_ref[at, :], edge)
+        value = main[(i + 1) * SUB : (i + 2) * SUB, :] - pltpu.roll(behind, LANES - group, 1)
+        unpack(held[1], i, value, wins, levels // SUB, lats)
+    copies[1].start()
+    for i in range(lons):
+        at = slice(i * SUB, (i + 1) * SUB)
+        edge = jnp.where(first, 0.0, swapped_ref[at, :])
+        ahead = jnp.where(lane < LANES - group, forward_ref[at, :], edge)
+        increment = main[(lons + i + 1) * SUB : (lons + i + 2) * SUB, :]
+        value = covar_ref[at, :] + increment - pltpu.roll(ahead, group, 1)
+        unpack(held[0], i, value, wins, levels // SUB, lats)
+    copies[0].start()
+    for copy in copies:
+        copy.wait()
 
 
 def kernel_call(kernel, inputs, outputs, scratch=(), flops=0, space=pltpu.VMEM):
@@ -469,24 +484,33 @@
         return lax.ppermute(x, "tiles", pairs)
 
     peer = lax.ppermute(main, "tiles", [(t, t ^ 1) for t in range(tiles)])
-    held, misc = lons * SUB, (2 * lons + 2) * SUB
-    pair = jnp.concatenate([main, peer])
+    row = lax.broadcasted_iota(jnp.int32, (SUB, LANES), 0)
+    misc = jnp.where(row < SUB // 2, main[:SUB], peer[:SUB])
+    held = (lons + 1) * SUB
+    pair = jnp.concatenate([misc, main[SUB:], peer[SUB:]])
     left = moved(pair, 1)
     right = moved(pair, -1)
-    short = jnp.concatenate([main[:held], main[misc:], peer[:held], peer[misc:]])
+    short = jnp.concatenate([misc, main[SUB:held], peer[SUB:held]])
     far = [moved(short, -d) for d in range(2, rings - 1)]
     near = (main, peer, left, right)
+    span = lons + 2 * STEPS
     forward, backward, edge = kernel_call(
         functools.partial(model_kernel, geometry),
         near,
-        (rows(lons), rows(lons), rows(lons)),
-        [pltpu.VMEM((lons + 2 * STEPS, 5, SUB, LANES), jnp.float32)],
+        (rows(lons),) * 3,
+        [pltpu.VMEM((span, 5, SUB, LANES), jnp.float32)],
         flops=MODEL_FLOPS,
     )
-    edge = lax.ppermute(edge, "subwin", [(0, 1), (1, 0)])
+    swapped = lax.ppermute(edge, "subwin", [(0, 1), (1, 0)])
+    (covar,) = kernel_call(
+        functools.partial(filter_kernel, geometry),
+        (*near, *far, spread),
+        (rows(lons),),
+        flops=MODEL_FLOPS,
+    )
     model_side, dual_side = kernel_call(
         functools.partial(finish_kernel, geometry),
-        (*near, *far, forward, backward, edge, spread),
+        (main, forward, backward, swapped, covar),
         (full, full),
         [pltpu.VMEM(full.shape, full.dtype)] * 2 + [pltpu.SemaphoreType.DMA((2,))],
         flops=MODEL_FLOPS,

time: 20.6 us -> 20.5 us (level)
    pallas_call x2 -> x3, Pallas kernels: 1.79 us -> 1.91 us  [kernel_call(): pl.pallas_call(kernel, out_shape=outputs, in_specs=[vmem] * len(inputs),...]
  transfers between devices with their start and end apart: 5 -> 5, of which waited for: 4 -> 4; matrix products, arithmetic and copies ran while one was open for 0% -> 0% of each run, Pallas kernels for 4% -> 5%
where the time goes in v4:
time: 20.5 us; the launch traced here: 20.4 us
  starting transfers between devices  8.29 us (40%)
  waiting for transfers between devices  8.23 us (40%)
  Pallas kernels  3.08 us (15%)
  between operations  0.68 us (3%)
    ppermute x3, waiting for transfers between devices, moved(): return lax.ppermute(x, 'tiles', pairs)  5.26 us
    ppermute x3, starting transfers between devices, moved(): return lax.ppermute(x, 'tiles', pairs)  5.19 us
    ppermute x1, starting transfers between devices, dense_body(): peer = lax.ppermute(main, 'tiles', [(t, t ^ 1) for t in range(tiles)])  3.03 us
    ppermute x1, waiting for transfers between devices, dense_body(): peer = lax.ppermute(main, 'tiles', [(t, t ^ 1) for t in range(tiles)])  2.01 us
    pallas_call x3, Pallas kernels, kernel_call(): pl.pallas_call(kernel, out_shape=outputs, in_specs=[vmem] * len(inputs),...  1.91 us
    pallas_call x1, Pallas kernels, dense_body(): pl.pallas_call(pack_kernel, out_shape=rows(2 * lons + 3), in_specs=[pl.Bl...  1.17 us
    ppermute x1, waiting for transfers between devices, dense_body(): swapped = lax.ppermute(edge, 'subwin', [(0, 1), (1, 0)])  0.96 us
  transfers between devices with their start and end apart: 5, of which 4 were waited for; matrix products, arithmetic and copies ran while one was open for 0% of the time, Pallas kernels for 5%

profile of v4, /device:TPU:0, one launch (start us, length us, event | category | flops | bytes accessed | tf_op | source)
XLA Modules:
  0.0 20.4 jit_solution(17168041314294839732)
XLA Ops:
  0.6 1.2 %pack.1.refs_0_ = f32[88,128]{1,0:T(8,128)S(1)} custom-call(f32[4,4,16,16]{3,2,1,0:T(8,128)} %refs_0_.1, f32[4,4,16,16]{3,2,1,0:T(8,128)} %refs_1_.1, f32[4,16,16]{2,1,0:T(8,128)} %refs_2_.1, f32[4,16,16]{2,1,0:T(8,128)} %refs_3_.1, s32[4,16]{1,0:T(4,128)} %refs_4_.1, f32[2,4]{1,0:T(2,128)} %bitcast.1), custom_call_target="tpu_custom_call" | custom-call | tf_op jit(solution)/shard_map/pack/pallas_call | solution.py:471
  1.8 3.0 %collective-permute-start = (f32[88,128]{1,0:T(8,128)S(1)}, f32[88,128]{1,0:T(8,128)S(1)}, u32[]{:S(2)}, u32[]{:S(2)}) collective-permute-start(f32[88,128]{1,0:T(8,128)S(1)} %pack.1.refs_0_), channel_id=1, source_target_pairs={{0,2},{2,0},{4,6},{6,4},{8,10},{10,8},{12,14},{14,12},{1,3},{3,1},... | collective-permute-start | bytes 135176 | tf_op jit(solution)/shard_map/ppermute | solution.py:486
  4.9 2.0 %collective-permute-done.refs_1_ = f32[88,128]{1,0:T(8,128)S(1)} collective-permute-done((f32[88,128]{1,0:T(8,128)S(1)}, f32[88,128]{1,0:T(8,128)S(1)}, u32[]{:S(2)}, u32[]{:S(2)}) %collective-permute-start) | collective-permute-done | bytes 45088 | tf_op jit(solution)/shard_map/ppermute | solution.py:486
  6.9 0.1 slice_select_fusion
  7.0 4.2 %collective-permute-start.2 = (f32[168,128]{1,0:T(8,128)S(1)}, f32[168,128]{1,0:T(8,128)S(1)}, u32[]{:S(2)}, u32[]{:S(2)}) collective-permute-start(f32[168,128]{1,0:T(8,128)S(1)} %pad_maximum_fusion), channel_id=1, source_target_pairs={{0,12},{2,14},{4,0},{6,2},{8,4},{10,6},{12,8},{14,10},{1,13},{3,15... | collective-permute-start | bytes 258056 | tf_op jit(solution)/shard_map/ppermute | solution.py:484
  11.1 0.0 collective-permute-start.1
  11.1 1.0 %collective-permute-start.4 = (f32[72,128]{1,0:T(8,128)S(1)}, f32[72,128]{1,0:T(8,128)S(1)}, u32[]{:S(2)}, u32[]{:S(2)}) collective-permute-start(f32[72,128]{1,0:T(8,128)S(1)} %pad_maximum_fusion.1), channel_id=1, source_target_pairs={{0,8},{2,10},{4,12},{6,14},{8,0},{10,2},{12,4},{14,6},{1,9},{3,11}... | collective-permute-start | bytes 110600 | tf_op jit(solution)/shard_map/ppermute | solution.py:484
  12.2 1.1 %collective-permute-done.2.refs_3_ = f32[168,128]{1,0:T(8,128)S(1)} collective-permute-done((f32[168,128]{1,0:T(8,128)S(1)}, f32[168,128]{1,0:T(8,128)S(1)}, u32[]{:S(2)}, u32[]{:S(2)}) %collective-permute-start.2) | collective-permute-done | bytes 86048 | tf_op jit(solution)/shard_map/ppermute | solution.py:484
  13.2 4.2 %collective-permute-done.1.refs_2_ = f32[168,128]{1,0:T(8,128)S(1)} collective-permute-done((f32[168,128]{1,0:T(8,128)S(1)}, f32[168,128]{1,0:T(8,128)S(1)}, u32[]{:S(2)}, u32[]{:S(2)}) %collective-permute-start.1) | collective-permute-done | bytes 86048 | tf_op jit(solution)/shard_map/ppermute | solution.py:484
  17.4 0.0 copy-start
  17.4 0.8 %shard_map.86 = (f32[32,128]{1,0:T(8,128)S(1)}, f32[32,128]{1,0:T(8,128)S(1)}, f32[32,128]{1,0:T(8,128)S(1)}) custom-call(f32[88,128]{1,0:T(8,128)S(1)} %pack.1.refs_0_, f32[88,128]{1,0:T(8,128)S(1)} %collective-permute-done.refs_1_, f32[168,128]{1,0:T(8,128)S(1)} %collective-permute-done.1.refs_2_, f32[168,128]{1,0:T(8,128)S(1)} %collective-permute-done.2.refs_3_), custom_call_target="tpu_custom_call" | custom-call | flops 1000000 | bytes 262144 | tf_op jit(solution)/shard_map/pallas_call | solution.py:449
  18.3 0.1 collective-permute-start.3
  18.3 0.0 collective-permute-done.4.refs_4_
  18.3 0.0 copy-done
  18.4 0.2 shard_map.87.refs_4_
  18.5 1.0 %collective-permute-done.3.refs_3_ = f32[32,128]{1,0:T(8,128)S(1)} collective-permute-done((f32[32,128]{1,0:T(8,128)S(1)}, f32[32,128]{1,0:T(8,128)S(1)}, u32[]{:S(2)}, u32[]{:S(2)}) %collective-permute-start.3) | collective-permute-done | bytes 16416 | tf_op jit(solution)/shard_map/ppermute | solution.py:504
  19.5 0.9 %shard_map.88 = (f32[4,4,16,16]{3,2,1,0:T(8,128)}, f32[4,4,16,16]{3,2,1,0:T(8,128)}) custom-call(f32[88,128]{1,0:T(8,128)S(1)} %pack.1.refs_0_, f32[32,128]{1,0:T(8,128)S(1)} %get-tuple-element.5.refs_1_, f32[32,128]{1,0:T(8,128)S(1)} %get-tuple-element.6.refs_2_, f32[32,128]{1,0:T(8,128)S(1)} %collective-permute-done.3.refs_3_, f32[32,128]{1,0:T(8,128)S(1)} %shard_map.87.refs_4_), custom_call_target="tpu_custom_call" | custom-call | flops 1000000 | bytes 262144 | tf_op jit(solution)/shard_map/pallas_call | solution.py:449
  (7 shorter events, 0.0 us)
Async XLA Ops:
  1.8 5.1 %collective-permute-start = (f32[88,128]{1,0:T(8,128)S(1)}, f32[88,128]{1,0:T(8,128)S(1)}, u32[]{:S(2)}, u32[]{:S(2)}) collective-permute-start(f32[88,128]{1,0:T(8,128)S(1)} %pack.1.refs_0_), channel_id=1, source_target_pairs={{0,2},{2,0},{4,6},{6,4},{8,10},{10,8},{12,14},{14,12},{1,3},{3,1},... | collective-permute-start | bytes 135176 | tf_op jit(solution)/shard_map/ppermute | solution.py:486
  7.0 6.3 %collective-permute-start.2 = (f32[168,128]{1,0:T(8,128)S(1)}, f32[168,128]{1,0:T(8,128)S(1)}, u32[]{:S(2)}, u32[]{:S(2)}) collective-permute-start(f32[168,128]{1,0:T(8,128)S(1)} %pad_maximum_fusion), channel_id=1, source_target_pairs={{0,12},{2,14},{4,0},{6,2},{8,4},{10,6},{12,8},{14,10},{1,13},{3,15... | collective-permute-start | bytes 258056 | tf_op jit(solution)/shard_map/ppermute | solution.py:484
  11.1 6.3 %collective-permute-start.1 = (f32[168,128]{1,0:T(8,128)S(1)}, f32[168,128]{1,0:T(8,128)S(1)}, u32[]{:S(2)}, u32[]{:S(2)}) collective-permute-start(f32[168,128]{1,0:T(8,128)S(1)} %pad_maximum_fusion), channel_id=1, source_target_pairs={{0,4},{2,6},{4,8},{6,10},{8,12},{10,14},{12,0},{14,2},{1,5},{3,7},... | collective-permute-start | bytes 258056 | tf_op jit(solution)/shard_map/ppermute | solution.py:484
  11.1 7.2 %collective-permute-start.4 = (f32[72,128]{1,0:T(8,128)S(1)}, f32[72,128]{1,0:T(8,128)S(1)}, u32[]{:S(2)}, u32[]{:S(2)}) collective-permute-start(f32[72,128]{1,0:T(8,128)S(1)} %pad_maximum_fusion.1), channel_id=1, source_target_pairs={{0,8},{2,10},{4,12},{6,14},{8,0},{10,2},{12,4},{14,6},{1,9},{3,11}... | collective-permute-start | bytes 110600 | tf_op jit(solution)/shard_map/ppermute | solution.py:484
  17.4 0.9 %copy-start = (f32[4,16]{1,0:T(4,128)S(1)}, f32[4,16]{1,0:T(4,128)}, u32[]{:S(2)}) copy-start(f32[4,16]{1,0:T(4,128)} %refs_5_.1) | copy-start | bytes 772
  18.3 1.2 %collective-permute-start.3 = (f32[32,128]{1,0:T(8,128)S(1)}, f32[32,128]{1,0:T(8,128)S(1)}, u32[]{:S(2)}, u32[]{:S(2)}) collective-permute-start(f32[32,128]{1,0:T(8,128)S(1)} %get-tuple-element.7), channel_id=1, source_target_pairs={{0,1},{1,0},{2,3},{3,2},{4,5},{5,4},{6,7},{7,6},{8,9},{9,8},{10,11... | collective-permute-start | bytes 49160 | tf_op jit(solution)/shard_map/ppermute | solution.py:504

commit v5 on v4

--- a/solution.py
+++ b/solution.py
@@ -216,7 +216,7 @@
 
 
 class Rows:
-    def __init__(self, lons, tiles, main, peer, left=None, right=None, far=()):
+    def __init__(self, lons, tiles, main, peer, left, right, *far):
         self.tiles = tiles
         self.even = lax.axis_index("tiles") % 2 == 0
         full = 2 * lons + 3
@@ -226,9 +226,12 @@
         for odd, sign in enumerate((1, -1)):
             self.add(odd, 0, main, whole, 0, 0)
             self.add(odd, sign, peer, whole, 0, 0)
-            for offset, ref in ((-2, left), (2, right)):
-                self.add(odd, offset, ref, whole, 0, 0)
-                self.add(odd, offset + sign, ref, whole, full - 1, SUB // 2)
+            for offset, refs in ((-2, left), (2, right)):
+                self.add(odd, offset, refs[0], whole, 0, 0)
+                if len(refs) == 2:
+                    self.add(odd, offset + sign, refs[1], whole, 0, 0)
+                else:
+                    self.add(odd, offset + sign, refs[0], whole, full - 1, SUB // 2)
             for k, ref in enumerate(far):
                 self.add(odd, 2 * (k + 2), ref, held, 0, 0)
                 self.add(odd, 2 * (k + 2) + sign, ref, held, lons, SUB // 2)
@@ -300,7 +303,7 @@
     lons, wins, _, lats, tiles = geometry
     near, (forward_ref, backward_ref, edge_ref, coeff_ref) = refs[:-4], refs[-4:]
     group = LANES // wins
-    rows = Rows(lons, tiles, *near)
+    rows = Rows(lons, tiles, near[0], near[1], near[2:4], near[4:5], *near[5:])
     lane = lane_index()
     lat = lane % lats
     forward, backward = [], []
@@ -358,9 +361,8 @@
     group = LANES // wins
     own_lats = lats // tiles
     count = lons * tiles
-    main, peer, left, right = refs[:4]
-    far, (spread_ref, covar_ref) = refs[4:-2], refs[-2:]
-    rows = Rows(lons, tiles, main, peer, left, right, far)
+    near, (spread_ref, covar_ref) = refs[:-2], refs[-2:]
+    rows = Rows(lons, tiles, near[0], near[1], near[2:4], near[4:5], *near[5:])
     lane = lane_index()
     tile = lax.axis_index("tiles")
 
@@ -488,11 +490,13 @@
     misc = jnp.where(row < SUB // 2, main[:SUB], peer[:SUB])
     held = (lons + 1) * SUB
     pair = jnp.concatenate([misc, main[SUB:], peer[SUB:]])
-    left = moved(pair, 1)
-    right = moved(pair, -1)
+    left_own = moved(main, 1)
+    left_peer = moved(peer, 1)
+    left = (left_own, left_peer)
+    right = (moved(pair, -1),)
     short = jnp.concatenate([misc, main[SUB:held], peer[SUB:held]])
     far = [moved(short, -d) for d in range(2, rings - 1)]
-    near = (main, peer, left, right)
+    near = (main, peer, *left, *right)
     span = lons + 2 * STEPS
     forward, backward, edge = kernel_call(
         functools.partial(model_kernel, geometry),

time: 20.5 us -> 20.1 us (0.980)
  waiting for transfers between devices: 8.23 us -> 6.21 us
  starting transfers between devices: 8.29 us -> 9.87 us
    ppermute x1, waiting for transfers between devices: 2.01 us -> 0.43 us  [dense_body(): peer = lax.ppermute(main, 'tiles', [(t, t ^ 1) for t in range(tiles)])]
    ppermute x3 -> x4, starting transfers between devices: 5.19 us -> 6.76 us  [moved(): return lax.ppermute(x, 'tiles', pairs)]
    ppermute x3 -> x4, waiting for transfers between devices: 5.26 us -> 4.83 us  [moved(): return lax.ppermute(x, 'tiles', pairs)]
  transfers between devices with their start and end apart: 5 -> 6, of which waited for: 4 -> 3; matrix products, arithmetic and copies ran while one was open for 0% -> 1% of each run, Pallas kernels for 5% -> 5%
where the time goes in v5:
time: 20.1 us; the launch traced here: 20 us
  starting transfers between devices  9.87 us (49%)
  waiting for transfers between devices  6.21 us (31%)
  Pallas kernels  3.08 us (15%)
  between operations  0.69 us (3%)
    ppermute x4, starting transfers between devices, moved(): return lax.ppermute(x, 'tiles', pairs)  6.76 us
    ppermute x4, waiting for transfers between devices, moved(): return lax.ppermute(x, 'tiles', pairs)  4.83 us
    ppermute x1, starting transfers between devices, dense_body(): peer = lax.ppermute(main, 'tiles', [(t, t ^ 1) for t in range(tiles)])  3.03 us
    pallas_call x3, Pallas kernels, kernel_call(): pl.pallas_call(kernel, out_shape=outputs, in_specs=[vmem] * len(inputs),...  1.9 us
    pallas_call x1, Pallas kernels, dense_body(): pl.pallas_call(pack_kernel, out_shape=rows(2 * lons + 3), in_specs=[pl.Bl...  1.17 us
    ppermute x1, waiting for transfers between devices, dense_body(): swapped = lax.ppermute(edge, 'subwin', [(0, 1), (1, 0)])  0.96 us
    ppermute x1, waiting for transfers between devices, dense_body(): peer = lax.ppermute(main, 'tiles', [(t, t ^ 1) for t in range(tiles)])  0.43 us
  transfers between devices with their start and end apart: 6, of which 3 were waited for; matrix products, arithmetic and copies ran while one was open for 1% of the time, Pallas kernels for 5%

profile of v5, /device:TPU:0, one launch (start us, length us, event | category | flops | bytes accessed | tf_op | source)
XLA Modules:
  0.0 20.0 jit_solution(16182734419774758735)
XLA Ops:
  0.6 1.2 %pack.1.refs_0_ = f32[88,128]{1,0:T(8,128)S(1)} custom-call(f32[4,4,16,16]{3,2,1,0:T(8,128)} %refs_0_.1, f32[4,4,16,16]{3,2,1,0:T(8,128)} %refs_1_.1, f32[4,16,16]{2,1,0:T(8,128)} %refs_2_.1, f32[4,16,16]{2,1,0:T(8,128)} %refs_3_.1, s32[4,16]{1,0:T(4,128)} %refs_4_.1, f32[2,4]{1,0:T(2,128)} %bitcast.1), custom_call_target="tpu_custom_call" | custom-call | tf_op jit(solution)/shard_map/pack/pallas_call | solution.py:473
  1.8 3.0 %collective-permute-start = (f32[88,128]{1,0:T(8,128)S(1)}, f32[88,128]{1,0:T(8,128)S(1)}, u32[]{:S(2)}, u32[]{:S(2)}) collective-permute-start(f32[88,128]{1,0:T(8,128)S(1)} %pack.1.refs_0_), channel_id=1, source_target_pairs={{0,2},{2,0},{4,6},{6,4},{8,10},{10,8},{12,14},{14,12},{1,3},{3,1},... | collective-permute-start | bytes 135176 | tf_op jit(solution)/shard_map/ppermute | solution.py:488
  4.8 1.6 %collective-permute-start.1 = (f32[88,128]{1,0:T(8,128)S(1)}, f32[88,128]{1,0:T(8,128)S(1)}, u32[]{:S(2)}, u32[]{:S(2)}) collective-permute-start(f32[88,128]{1,0:T(8,128)S(1)} %pack.1.refs_0_), channel_id=1, source_target_pairs={{0,4},{2,6},{4,8},{6,10},{8,12},{10,14},{12,0},{14,2},{1,5},{3,7},... | collective-permute-start | bytes 135176 | tf_op jit(solution)/shard_map/ppermute | solution.py:486
  6.4 0.4 %collective-permute-done.refs_1_ = f32[88,128]{1,0:T(8,128)S(1)} collective-permute-done((f32[88,128]{1,0:T(8,128)S(1)}, f32[88,128]{1,0:T(8,128)S(1)}, u32[]{:S(2)}, u32[]{:S(2)}) %collective-permute-start) | collective-permute-done | bytes 45088 | tf_op jit(solution)/shard_map/ppermute | solution.py:488
  6.9 0.1 slice_select_fusion
  7.0 4.2 %collective-permute-start.3 = (f32[168,128]{1,0:T(8,128)S(1)}, f32[168,128]{1,0:T(8,128)S(1)}, u32[]{:S(2)}, u32[]{:S(2)}) collective-permute-start(f32[168,128]{1,0:T(8,128)S(1)} %pad_maximum_fusion), channel_id=1, source_target_pairs={{0,12},{2,14},{4,0},{6,2},{8,4},{10,6},{12,8},{14,10},{1,13},{3,15... | collective-permute-start | bytes 258056 | tf_op jit(solution)/shard_map/ppermute | solution.py:486
  11.1 0.0 collective-permute-start.2
  11.1 1.0 %collective-permute-start.5 = (f32[72,128]{1,0:T(8,128)S(1)}, f32[72,128]{1,0:T(8,128)S(1)}, u32[]{:S(2)}, u32[]{:S(2)}) collective-permute-start(f32[72,128]{1,0:T(8,128)S(1)} %pad_maximum_fusion.1), channel_id=1, source_target_pairs={{0,8},{2,10},{4,12},{6,14},{8,0},{10,2},{12,4},{14,6},{1,9},{3,11}... | collective-permute-start | bytes 110600 | tf_op jit(solution)/shard_map/ppermute | solution.py:486
  12.2 0.0 collective-permute-done.1.refs_2_
  12.2 4.8 %collective-permute-done.2.refs_3_ = f32[88,128]{1,0:T(8,128)S(1)} collective-permute-done((f32[88,128]{1,0:T(8,128)S(1)}, f32[88,128]{1,0:T(8,128)S(1)}, u32[]{:S(2)}, u32[]{:S(2)}) %collective-permute-start.2) | collective-permute-done | bytes 45088 | tf_op jit(solution)/shard_map/ppermute | solution.py:486
  17.0 0.0 collective-permute-done.3.refs_4_
  17.0 0.0 copy-start
  17.0 0.8 %shard_map.86 = (f32[32,128]{1,0:T(8,128)S(1)}, f32[32,128]{1,0:T(8,128)S(1)}, f32[32,128]{1,0:T(8,128)S(1)}) custom-call(f32[88,128]{1,0:T(8,128)S(1)} %pack.1.refs_0_, f32[88,128]{1,0:T(8,128)S(1)} %collective-permute-done.refs_1_, f32[88,128]{1,0:T(8,128)S(1)} %collective-permute-done.1.refs_2_, f32[88,128]{1,0:T(8,128)S(1)} %collective-permute-done.2.refs_3_, ...), custom_call_target="tpu_custom_call" | custom-call | flops 1000000 | bytes 262144 | tf_op jit(solution)/shard_map/pallas_call | solution.py:451
  17.8 0.1 collective-permute-start.4
  17.9 0.0 collective-permute-done.5.refs_5_
  17.9 0.0 copy-done
  17.9 0.2 shard_map.87.refs_4_
  18.1 1.0 %collective-permute-done.4.refs_3_ = f32[32,128]{1,0:T(8,128)S(1)} collective-permute-done((f32[32,128]{1,0:T(8,128)S(1)}, f32[32,128]{1,0:T(8,128)S(1)}, u32[]{:S(2)}, u32[]{:S(2)}) %collective-permute-start.4) | collective-permute-done | bytes 16416 | tf_op jit(solution)/shard_map/ppermute | solution.py:508
  19.1 0.9 %shard_map.88 = (f32[4,4,16,16]{3,2,1,0:T(8,128)}, f32[4,4,16,16]{3,2,1,0:T(8,128)}) custom-call(f32[88,128]{1,0:T(8,128)S(1)} %pack.1.refs_0_, f32[32,128]{1,0:T(8,128)S(1)} %get-tuple-element.5.refs_1_, f32[32,128]{1,0:T(8,128)S(1)} %get-tuple-element.6.refs_2_, f32[32,128]{1,0:T(8,128)S(1)} %collective-permute-done.4.refs_3_, f32[32,128]{1,0:T(8,128)S(1)} %shard_map.87.refs_4_), custom_call_target="tpu_custom_call" | custom-call | flops 1000000 | bytes 262144 | tf_op jit(solution)/shard_map/pallas_call | solution.py:451
  (7 shorter events, 0.0 us)
Async XLA Ops:
  1.8 5.1 %collective-permute-start = (f32[88,128]{1,0:T(8,128)S(1)}, f32[88,128]{1,0:T(8,128)S(1)}, u32[]{:S(2)}, u32[]{:S(2)}) collective-permute-start(f32[88,128]{1,0:T(8,128)S(1)} %pack.1.refs_0_), channel_id=1, source_target_pairs={{0,2},{2,0},{4,6},{6,4},{8,10},{10,8},{12,14},{14,12},{1,3},{3,1},... | collective-permute-start | bytes 135176 | tf_op jit(solution)/shard_map/ppermute | solution.py:488
  4.8 7.3 %collective-permute-start.1 = (f32[88,128]{1,0:T(8,128)S(1)}, f32[88,128]{1,0:T(8,128)S(1)}, u32[]{:S(2)}, u32[]{:S(2)}) collective-permute-start(f32[88,128]{1,0:T(8,128)S(1)} %pack.1.refs_0_), channel_id=1, source_target_pairs={{0,4},{2,6},{4,8},{6,10},{8,12},{10,14},{12,0},{14,2},{1,5},{3,7},... | collective-permute-start | bytes 135176 | tf_op jit(solution)/shard_map/ppermute | solution.py:486
  7.0 10.0 %collective-permute-start.3 = (f32[168,128]{1,0:T(8,128)S(1)}, f32[168,128]{1,0:T(8,128)S(1)}, u32[]{:S(2)}, u32[]{:S(2)}) collective-permute-start(f32[168,128]{1,0:T(8,128)S(1)} %pad_maximum_fusion), channel_id=1, source_target_pairs={{0,12},{2,14},{4,0},{6,2},{8,4},{10,6},{12,8},{14,10},{1,13},{3,15... | collective-permute-start | bytes 258056 | tf_op jit(solution)/shard_map/ppermute | solution.py:486
  11.1 5.8 %collective-permute-start.2 = (f32[88,128]{1,0:T(8,128)S(1)}, f32[88,128]{1,0:T(8,128)S(1)}, u32[]{:S(2)}, u32[]{:S(2)}) collective-permute-start(f32[88,128]{1,0:T(8,128)S(1)} %collective-permute-done.refs_1_), channel_id=1, source_target_pairs={{0,4},{2,6},{4,8},{6,10},{8,12},{10,14},{12,0},{14,2},{1,5},{3,7},... | collective-permute-start | bytes 135176 | tf_op jit(solution)/shard_map/ppermute | solution.py:486
  11.1 6.8 %collective-permute-start.5 = (f32[72,128]{1,0:T(8,128)S(1)}, f32[72,128]{1,0:T(8,128)S(1)}, u32[]{:S(2)}, u32[]{:S(2)}) collective-permute-start(f32[72,128]{1,0:T(8,128)S(1)} %pad_maximum_fusion.1), channel_id=1, source_target_pairs={{0,8},{2,10},{4,12},{6,14},{8,0},{10,2},{12,4},{14,6},{1,9},{3,11}... | collective-permute-start | bytes 110600 | tf_op jit(solution)/shard_map/ppermute | solution.py:486
  17.0 0.9 %copy-start = (f32[4,16]{1,0:T(4,128)S(1)}, f32[4,16]{1,0:T(4,128)}, u32[]{:S(2)}) copy-start(f32[4,16]{1,0:T(4,128)} %refs_6_.1) | copy-start | bytes 772
  17.8 1.2 %collective-permute-start.4 = (f32[32,128]{1,0:T(8,128)S(1)}, f32[32,128]{1,0:T(8,128)S(1)}, u32[]{:S(2)}, u32[]{:S(2)}) collective-permute-start(f32[32,128]{1,0:T(8,128)S(1)} %get-tuple-element.7), channel_id=1, source_target_pairs={{0,1},{1,0},{2,3},{3,2},{4,5},{5,4},{6,7},{7,6},{8,9},{9,8},{10,11... | collective-permute-start | bytes 49160 | tf_op jit(solution)/shard_map/ppermute | solution.py:508

commit v6 on v4

--- a/solution.py
+++ b/solution.py
@@ -216,19 +216,19 @@
 
 
 class Rows:
-    def __init__(self, lons, tiles, main, peer, left=None, right=None, far=()):
+    def __init__(self, lons, tiles, main, peer, left, right, wide, narrow=None, *far):
         self.tiles = tiles
         self.even = lax.axis_index("tiles") % 2 == 0
-        full = 2 * lons + 3
-        whole = {row - 1: row * SUB for row in range(full)}
+        whole = {row - 1: row * SUB for row in range(2 * lons + 3)}
         held = {row - 1: row * SUB for row in range(lons + 1)}
         self.places = ({}, {})
         for odd, sign in enumerate((1, -1)):
             self.add(odd, 0, main, whole, 0, 0)
             self.add(odd, sign, peer, whole, 0, 0)
-            for offset, ref in ((-2, left), (2, right)):
-                self.add(odd, offset, ref, whole, 0, 0)
-                self.add(odd, offset + sign, ref, whole, full - 1, SUB // 2)
+            self.add(odd, -2, left, whole, 0, 0)
+            self.add(odd, 2, right, whole, 0, 0)
+            self.add(odd, -sign, wide, whole, 0, 0)
+            self.add(odd, 3 * sign, narrow, held, 0, 0)
             for k, ref in enumerate(far):
                 self.add(odd, 2 * (k + 2), ref, held, 0, 0)
                 self.add(odd, 2 * (k + 2) + sign, ref, held, lons, SUB // 2)
@@ -358,9 +358,8 @@
     group = LANES // wins
     own_lats = lats // tiles
     count = lons * tiles
-    main, peer, left, right = refs[:4]
-    far, (spread_ref, covar_ref) = refs[4:-2], refs[-2:]
-    rows = Rows(lons, tiles, main, peer, left, right, far)
+    spread_ref, covar_ref = refs[-2:]
+    rows = Rows(lons, tiles, *refs[:-2])
     lane = lane_index()
     tile = lax.axis_index("tiles")
 
@@ -480,19 +479,24 @@
     )(*[pltpu.with_memory_space_constraint(x, pltpu.HBM) for x in arrays])
 
     def moved(x, by):
-        pairs = [(t, (t // 2 + by) % rings * 2 + t % 2) for t in range(tiles)]
+        pairs = [(t, (t // 2 + by(t % 2)) % rings * 2 + t % 2) for t in range(tiles)]
         return lax.ppermute(x, "tiles", pairs)
 
     peer = lax.ppermute(main, "tiles", [(t, t ^ 1) for t in range(tiles)])
     row = lax.broadcasted_iota(jnp.int32, (SUB, LANES), 0)
     misc = jnp.where(row < SUB // 2, main[:SUB], peer[:SUB])
     held = (lons + 1) * SUB
-    pair = jnp.concatenate([misc, main[SUB:], peer[SUB:]])
-    left = moved(pair, 1)
-    right = moved(pair, -1)
+    left = moved(main, lambda odd: 1)
+    right = moved(main, lambda odd: -1)
+    wide = lax.ppermute(
+        main,
+        "tiles",
+        [(t, (t + 1 if t % 2 else t - 1) % tiles) for t in range(tiles)],
+    )
+    narrow = moved(peer[:held], lambda odd: 1 if odd else -1)
     short = jnp.concatenate([misc, main[SUB:held], peer[SUB:held]])
-    far = [moved(short, -d) for d in range(2, rings - 1)]
-    near = (main, peer, left, right)
+    far = [moved(short, lambda odd, d=d: -d) for d in range(2, rings - 1)]
+    near = (main, peer, left, right, wide)
     span = lons + 2 * STEPS
     forward, backward, edge = kernel_call(
         functools.partial(model_kernel, geometry),
@@ -504,7 +508,7 @@
     swapped = lax.ppermute(edge, "subwin", [(0, 1), (1, 0)])
     (covar,) = kernel_call(
         functools.partial(filter_kernel, geometry),
-        (*near, *far, spread),
+        (*near, narrow, *far, spread),
         (rows(lons),),
         flops=MODEL_FLOPS,
     )

time: 20.5 us -> 20.3 us (level)
  waiting for transfers between devices: 8.23 us -> 5.71 us
  starting transfers between devices: 8.29 us -> 10.5 us
    ppermute x0 -> x1, starting transfers between devices: none -> 6.07 us  [dense_body(): lax.ppermute(main, 'tiles', [(t, (t + 1 if t % 2 else t - 1) % tiles) for...]
    ppermute x3 -> x4, waiting for transfers between devices: 5.26 us -> 1.67 us  [moved(): return lax.ppermute(x, 'tiles', pairs)]
    ppermute x1, starting transfers between devices: 3.03 us -> 0.01 us  [dense_body(): peer = lax.ppermute(main, 'tiles', [(t, t ^ 1) for t in range(tiles)])]
    ppermute x1, waiting for transfers between devices: 2.01 us -> 4.03 us  [dense_body(): peer = lax.ppermute(main, 'tiles', [(t, t ^ 1) for t in range(tiles)])]
    ppermute x1, waiting for transfers between devices: 0.96 us -> 0.01 us  [dense_body(): swapped = lax.ppermute(edge, 'subwin', [(0, 1), (1, 0)])]
    ppermute x3 -> x4, starting transfers between devices: 5.19 us -> 4.38 us  [moved(): return lax.ppermute(x, 'tiles', pairs)]
  transfers between devices with their start and end apart: 5 -> 7, of which waited for: 4 -> 2; matrix products, arithmetic and copies ran while one was open for 0% -> 0% of each run, Pallas kernels for 5% -> 5%
where the time goes in v6:
time: 20.3 us; the launch traced here: 20.1 us
  starting transfers between devices  10.5 us (52%)
  waiting for transfers between devices  5.71 us (28%)
  Pallas kernels  3.08 us (15%)
  between operations  0.7 us (3%)
    ppermute x1, starting transfers between devices, dense_body(): lax.ppermute(main, 'tiles', [(t, (t + 1 if t % 2 else t - 1) % tiles) for...  6.07 us
    ppermute x4, starting transfers between devices, moved(): return lax.ppermute(x, 'tiles', pairs)  4.38 us
    ppermute x1, waiting for transfers between devices, dense_body(): peer = lax.ppermute(main, 'tiles', [(t, t ^ 1) for t in range(tiles)])  4.03 us
    pallas_call x3, Pallas kernels, kernel_call(): pl.pallas_call(kernel, out_shape=outputs, in_specs=[vmem] * len(inputs),...  1.91 us
    ppermute x4, waiting for transfers between devices, moved(): return lax.ppermute(x, 'tiles', pairs)  1.67 us
    pallas_call x1, Pallas kernels, dense_body(): pl.pallas_call(pack_kernel, out_shape=rows(2 * lons + 3), in_specs=[pl.Bl...  1.17 us
  transfers between devices with their start and end apart: 7, of which 2 were waited for; matrix products, arithmetic and copies ran while one was open for 0% of the time, Pallas kernels for 5%

profile of v6, /device:TPU:0, one launch (start us, length us, event | category | flops | bytes accessed | tf_op | source)
XLA Modules:
  0.0 20.1 jit_solution(3900419247910111962)
XLA Ops:
  0.6 1.2 %pack.1.refs_0_ = f32[88,128]{1,0:T(8,128)S(1)} custom-call(f32[4,4,16,16]{3,2,1,0:T(8,128)} %refs_0_.1, f32[4,4,16,16]{3,2,1,0:T(8,128)} %refs_1_.1, f32[4,16,16]{2,1,0:T(8,128)} %refs_2_.1, f32[4,16,16]{2,1,0:T(8,128)} %refs_3_.1, s32[4,16]{1,0:T(4,128)} %refs_4_.1, f32[2,4]{1,0:T(2,128)} %bitcast.1), custom_call_target="tpu_custom_call" | custom-call | tf_op jit(solution)/shard_map/pack/pallas_call | solution.py:470
  1.8 6.1 %collective-permute-start.3 = (f32[88,128]{1,0:T(8,128)S(1)}, f32[88,128]{1,0:T(8,128)S(1)}, u32[]{:S(2)}, u32[]{:S(2)}) collective-permute-start(f32[88,128]{1,0:T(8,128)S(1)} %pack.1.refs_0_), channel_id=1, source_target_pairs={{0,14},{2,4},{4,2},{6,8},{8,6},{10,12},{12,10},{14,0},{1,15},{3,5}... | collective-permute-start | bytes 135176 | tf_op jit(solution)/shard_map/ppermute | solution.py:491
  7.9 0.4 %collective-permute-start.2 = (f32[88,128]{1,0:T(8,128)S(1)}, f32[88,128]{1,0:T(8,128)S(1)}, u32[]{:S(2)}, u32[]{:S(2)}) collective-permute-start(f32[88,128]{1,0:T(8,128)S(1)} %pack.1.refs_0_), channel_id=1, source_target_pairs={{0,12},{2,14},{4,0},{6,2},{8,4},{10,6},{12,8},{14,10},{1,13},{3,15... | collective-permute-start | bytes 135176 | tf_op jit(solution)/shard_map/ppermute | solution.py:483
  8.3 1.6 %collective-permute-start.1 = (f32[88,128]{1,0:T(8,128)S(1)}, f32[88,128]{1,0:T(8,128)S(1)}, u32[]{:S(2)}, u32[]{:S(2)}) collective-permute-start(f32[88,128]{1,0:T(8,128)S(1)} %pack.1.refs_0_), channel_id=1, source_target_pairs={{0,4},{2,6},{4,8},{6,10},{8,12},{10,14},{12,0},{14,2},{1,5},{3,7},... | collective-permute-start | bytes 135176 | tf_op jit(solution)/shard_map/ppermute | solution.py:483
  9.9 0.0 collective-permute-start
  9.9 4.0 %collective-permute-done.refs_1_ = f32[88,128]{1,0:T(8,128)S(1)} collective-permute-done((f32[88,128]{1,0:T(8,128)S(1)}, f32[88,128]{1,0:T(8,128)S(1)}, u32[]{:S(2)}, u32[]{:S(2)}) %collective-permute-start) | collective-permute-done | bytes 45088 | tf_op jit(solution)/shard_map/ppermute | solution.py:485
  14.0 0.1 slice_select_fusion
  14.0 0.0 collective-permute-start.6
  14.1 2.3 %collective-permute-start.5 = (f32[40,128]{1,0:T(8,128)S(1)}, f32[40,128]{1,0:T(8,128)S(1)}, u32[]{:S(2)}, u32[]{:S(2)}) collective-permute-start(f32[40,128]{1,0:T(8,128)S(1)} %slice.20), channel_id=1, source_target_pairs={{0,12},{2,6},{4,0},{6,10},{8,4},{10,14},{12,8},{14,2},{1,13},{3,7}... | collective-permute-start | bytes 61448 | tf_op jit(solution)/shard_map/ppermute | solution.py:483
  16.4 0.0 collective-permute-done.3.refs_4_
  16.4 0.0 collective-permute-done.2.refs_3_
  16.4 0.0 collective-permute-done.1.refs_2_
  16.4 0.0 copy-start
  16.4 0.8 %shard_map.86 = (f32[32,128]{1,0:T(8,128)S(1)}, f32[32,128]{1,0:T(8,128)S(1)}, f32[32,128]{1,0:T(8,128)S(1)}) custom-call(f32[88,128]{1,0:T(8,128)S(1)} %pack.1.refs_0_, f32[88,128]{1,0:T(8,128)S(1)} %collective-permute-done.refs_1_, f32[88,128]{1,0:T(8,128)S(1)} %collective-permute-done.1.refs_2_, f32[88,128]{1,0:T(8,128)S(1)} %collective-permute-done.2.refs_3_, ...), custom_call_target="tpu_custom_call" | custom-call | flops 1000000 | bytes 262144 | tf_op jit(solution)/shard_map/pallas_call | solution.py:448
  17.3 0.1 collective-permute-start.4
  17.4 1.7 %collective-permute-done.5.refs_5_ = f32[40,128]{1,0:T(8,128)S(1)} collective-permute-done((f32[40,128]{1,0:T(8,128)S(1)}, f32[40,128]{1,0:T(8,128)S(1)}, u32[]{:S(2)}, u32[]{:S(2)}) %collective-permute-start.5) | collective-permute-done | bytes 20512 | tf_op jit(solution)/shard_map/ppermute | solution.py:483
  19.0 0.0 collective-permute-done.6.refs_6_
  19.0 0.0 copy-done
  19.0 0.2 shard_map.87.refs_4_
  19.2 0.0 collective-permute-done.4.refs_3_
  19.2 0.9 %shard_map.88 = (f32[4,4,16,16]{3,2,1,0:T(8,128)}, f32[4,4,16,16]{3,2,1,0:T(8,128)}) custom-call(f32[88,128]{1,0:T(8,128)S(1)} %pack.1.refs_0_, f32[32,128]{1,0:T(8,128)S(1)} %get-tuple-element.5.refs_1_, f32[32,128]{1,0:T(8,128)S(1)} %get-tuple-element.6.refs_2_, f32[32,128]{1,0:T(8,128)S(1)} %collective-permute-done.4.refs_3_, f32[32,128]{1,0:T(8,128)S(1)} %shard_map.87.refs_4_), custom_call_target="tpu_custom_call" | custom-call | flops 1000000 | bytes 262144 | tf_op jit(solution)/shard_map/pallas_call | solution.py:448
  (5 shorter events, 0.0 us)
Async XLA Ops:
  1.8 14.6 %collective-permute-start.3 = (f32[88,128]{1,0:T(8,128)S(1)}, f32[88,128]{1,0:T(8,128)S(1)}, u32[]{:S(2)}, u32[]{:S(2)}) collective-permute-start(f32[88,128]{1,0:T(8,128)S(1)} %pack.1.refs_0_), channel_id=1, source_target_pairs={{0,14},{2,4},{4,2},{6,8},{8,6},{10,12},{12,10},{14,0},{1,15},{3,5}... | collective-permute-start | bytes 135176 | tf_op jit(solution)/shard_map/ppermute | solution.py:491
  7.9 8.5 %collective-permute-start.2 = (f32[88,128]{1,0:T(8,128)S(1)}, f32[88,128]{1,0:T(8,128)S(1)}, u32[]{:S(2)}, u32[]{:S(2)}) collective-permute-start(f32[88,128]{1,0:T(8,128)S(1)} %pack.1.refs_0_), channel_id=1, source_target_pairs={{0,12},{2,14},{4,0},{6,2},{8,4},{10,6},{12,8},{14,10},{1,13},{3,15... | collective-permute-start | bytes 135176 | tf_op jit(solution)/shard_map/ppermute | solution.py:483
  8.3 8.1 %collective-permute-start.1 = (f32[88,128]{1,0:T(8,128)S(1)}, f32[88,128]{1,0:T(8,128)S(1)}, u32[]{:S(2)}, u32[]{:S(2)}) collective-permute-start(f32[88,128]{1,0:T(8,128)S(1)} %pack.1.refs_0_), channel_id=1, source_target_pairs={{0,4},{2,6},{4,8},{6,10},{8,12},{10,14},{12,0},{14,2},{1,5},{3,7},... | collective-permute-start | bytes 135176 | tf_op jit(solution)/shard_map/ppermute | solution.py:483
  9.9 4.0 %collective-permute-start = (f32[88,128]{1,0:T(8,128)S(1)}, f32[88,128]{1,0:T(8,128)S(1)}, u32[]{:S(2)}, u32[]{:S(2)}) collective-permute-start(f32[88,128]{1,0:T(8,128)S(1)} %pack.1.refs_0_), channel_id=1, source_target_pairs={{0,2},{2,0},{4,6},{6,4},{8,10},{10,8},{12,14},{14,12},{1,3},{3,1},... | collective-permute-start | bytes 135176 | tf_op jit(solution)/shard_map/ppermute | solution.py:485
  14.0 5.0 %collective-permute-start.6 = (f32[72,128]{1,0:T(8,128)S(1)}, f32[72,128]{1,0:T(8,128)S(1)}, u32[]{:S(2)}, u32[]{:S(2)}) collective-permute-start(f32[72,128]{1,0:T(8,128)S(1)} %pad_maximum_fusion), channel_id=1, source_target_pairs={{0,8},{2,10},{4,12},{6,14},{8,0},{10,2},{12,4},{14,6},{1,9},{3,11}... | collective-permute-start | bytes 110600 | tf_op jit(solution)/shard_map/ppermute | solution.py:483
  14.1 4.9 %collective-permute-start.5 = (f32[40,128]{1,0:T(8,128)S(1)}, f32[40,128]{1,0:T(8,128)S(1)}, u32[]{:S(2)}, u32[]{:S(2)}) collective-permute-start(f32[40,128]{1,0:T(8,128)S(1)} %slice.20), channel_id=1, source_target_pairs={{0,12},{2,6},{4,0},{6,10},{8,4},{10,14},{12,8},{14,2},{1,13},{3,7}... | collective-permute-start | bytes 61448 | tf_op jit(solution)/shard_map/ppermute | solution.py:483
  16.4 2.6 %copy-start = (f32[4,16]{1,0:T(4,128)S(1)}, f32[4,16]{1,0:T(4,128)}, u32[]{:S(2)}) copy-start(f32[4,16]{1,0:T(4,128)} %refs_7_.1) | copy-start | bytes 772
  17.3 1.9 %collective-permute-start.4 = (f32[32,128]{1,0:T(8,128)S(1)}, f32[32,128]{1,0:T(8,128)S(1)}, u32[]{:S(2)}, u32[]{:S(2)}) collective-permute-start(f32[32,128]{1,0:T(8,128)S(1)} %get-tuple-element.7), channel_id=1, source_target_pairs={{0,1},{1,0},{2,3},{3,2},{4,5},{5,4},{6,7},{7,6},{8,9},{9,8},{10,11... | collective-permute-start | bytes 49160 | tf_op jit(solution)/shard_map/ppermute | solution.py:508

commit v7 on v6

--- a/solution.py
+++ b/solution.py
@@ -353,13 +353,12 @@
             ref[i, s, half * SUB : (half + 1) * SUB, :] = value[:, at : at + lats]
 
 
-def filter_kernel(geometry, *refs):
+def filtered(geometry, spread_ref, *refs):
     lons, wins, levels, lats, tiles = geometry
     group = LANES // wins
     own_lats = lats // tiles
     count = lons * tiles
-    spread_ref, covar_ref = refs[-2:]
-    rows = Rows(lons, tiles, *refs[:-2])
+    rows = Rows(lons, tiles, *refs)
     lane = lane_index()
     tile = lax.axis_index("tiles")
 
@@ -413,13 +412,14 @@
         scale = jnp.where(lane // group == s, picked(row, level), scale)
     square = scale * scale
     for i in range(lons):
-        covar_ref[i * SUB : (i + 1) * SUB, :] = square * smooth[i]
+        smooth[i] = square * smooth[i]
+    return smooth
 
 
 def finish_kernel(geometry, *refs):
     lons, wins, levels, lats, _ = geometry
-    main, forward_ref, backward_ref, swapped_ref, covar_ref = refs[:5]
-    outs, held, sent = refs[5:7], refs[7:9], refs[9]
+    main, forward_ref, backward_ref, swapped_ref, spread_ref = refs[0], *refs[-9:-5]
+    outs, held, sent = refs[-5:-3], refs[-3:-1], refs[-1]
     group = LANES // wins
     lane = lane_index()
     first = lax.axis_index("subwin") == 0
@@ -431,12 +431,13 @@
         value = main[(i + 1) * SUB : (i + 2) * SUB, :] - pltpu.roll(behind, LANES - group, 1)
         unpack(held[1], i, value, wins, levels // SUB, lats)
     copies[1].start()
+    covar = filtered(geometry, spread_ref, *refs[:-9])
     for i in range(lons):
         at = slice(i * SUB, (i + 1) * SUB)
         edge = jnp.where(first, 0.0, swapped_ref[at, :])
         ahead = jnp.where(lane < LANES - group, forward_ref[at, :], edge)
         increment = main[(lons + i + 1) * SUB : (lons + i + 2) * SUB, :]
-        value = covar_ref[at, :] + increment - pltpu.roll(ahead, group, 1)
+        value = covar[i] + increment - pltpu.roll(ahead, group, 1)
         unpack(held[0], i, value, wins, levels // SUB, lats)
     copies[0].start()
     for copy in copies:
@@ -506,15 +507,9 @@
         flops=MODEL_FLOPS,
     )
     swapped = lax.ppermute(edge, "subwin", [(0, 1), (1, 0)])
-    (covar,) = kernel_call(
-        functools.partial(filter_kernel, geometry),
-        (*near, narrow, *far, spread),
-        (rows(lons),),
-        flops=MODEL_FLOPS,
-    )
     model_side, dual_side = kernel_call(
         functools.partial(finish_kernel, geometry),
-        (main, forward, backward, swapped, covar),
+        (*near, narrow, *far, forward, backward, swapped, spread),
         (full, full),
         [pltpu.VMEM(full.shape, full.dtype)] * 2 + [pltpu.SemaphoreType.DMA((2,))],
         flops=MODEL_FLOPS,

time: 20.3 us -> 20.1 us (level)
    ppermute x4, waiting for transfers between devices: 1.67 us -> 0.5 us  [moved(): return lax.ppermute(x, 'tiles', pairs)]
    ppermute x1, waiting for transfers between devices: 0.01 us -> 1.17 us  [dense_body(): swapped = lax.ppermute(edge, 'subwin', [(0, 1), (1, 0)])]
    pallas_call x3 -> x2, Pallas kernels: 1.91 us -> 1.79 us  [kernel_call(): pl.pallas_call(kernel, out_shape=outputs, in_specs=[vmem] * len(inputs),...]
  transfers between devices with their start and end apart: 7 -> 7, of which waited for: 2 -> 3; matrix products, arithmetic and copies ran while one was open for 0% -> 0% of each run, Pallas kernels for 5% -> 4%
where the time goes in v7:
time: 20.1 us; the launch traced here: 20 us
  starting transfers between devices  10.5 us (52%)
  waiting for transfers between devices  5.71 us (28%)
  Pallas kernels  2.96 us (15%)
  between operations  0.69 us (3%)
    ppermute x1, starting transfers between devices, dense_body(): lax.ppermute(main, 'tiles', [(t, (t + 1 if t % 2 else t - 1) % tiles) for...  6.07 us
    ppermute x4, starting transfers between devices, moved(): return lax.ppermute(x, 'tiles', pairs)  4.38 us
    ppermute x1, waiting for transfers between devices, dense_body(): peer = lax.ppermute(main, 'tiles', [(t, t ^ 1) for t in range(tiles)])  4.03 us
    pallas_call x2, Pallas kernels, kernel_call(): pl.pallas_call(kernel, out_shape=outputs, in_specs=[vmem] * len(inputs),...  1.79 us
    pallas_call x1, Pallas kernels, dense_body(): pl.pallas_call(pack_kernel, out_shape=rows(2 * lons + 3), in_specs=[pl.Bl...  1.17 us
    ppermute x1, waiting for transfers between devices, dense_body(): swapped = lax.ppermute(edge, 'subwin', [(0, 1), (1, 0)])  1.17 us
    ppermute x4, waiting for transfers between devices, moved(): return lax.ppermute(x, 'tiles', pairs)  0.5 us
  transfers between devices with their start and end apart: 7, of which 3 were waited for; matrix products, arithmetic and copies ran while one was open for 0% of the time, Pallas kernels for 4%

profile of v7, /device:TPU:0, one launch (start us, length us, event | category | flops | bytes accessed | tf_op | source)
XLA Modules:
  0.0 20.0 jit_solution(8679580020730891650)
XLA Ops:
  0.6 1.2 %pack.1.refs_0_ = f32[88,128]{1,0:T(8,128)S(1)} custom-call(f32[4,4,16,16]{3,2,1,0:T(8,128)} %refs_0_.1, f32[4,4,16,16]{3,2,1,0:T(8,128)} %refs_1_.1, f32[4,16,16]{2,1,0:T(8,128)} %refs_2_.1, f32[4,16,16]{2,1,0:T(8,128)} %refs_3_.1, s32[4,16]{1,0:T(4,128)} %refs_4_.1, f32[2,4]{1,0:T(2,128)} %bitcast.1), custom_call_target="tpu_custom_call" | custom-call | tf_op jit(solution)/shard_map/pack/pallas_call | solution.py:471
  1.8 6.1 %collective-permute-start.3 = (f32[88,128]{1,0:T(8,128)S(1)}, f32[88,128]{1,0:T(8,128)S(1)}, u32[]{:S(2)}, u32[]{:S(2)}) collective-permute-start(f32[88,128]{1,0:T(8,128)S(1)} %pack.1.refs_0_), channel_id=1, source_target_pairs={{0,14},{2,4},{4,2},{6,8},{8,6},{10,12},{12,10},{14,0},{1,15},{3,5}... | collective-permute-start | bytes 135176 | tf_op jit(solution)/shard_map/ppermute | solution.py:492
  7.9 0.4 %collective-permute-start.2 = (f32[88,128]{1,0:T(8,128)S(1)}, f32[88,128]{1,0:T(8,128)S(1)}, u32[]{:S(2)}, u32[]{:S(2)}) collective-permute-start(f32[88,128]{1,0:T(8,128)S(1)} %pack.1.refs_0_), channel_id=1, source_target_pairs={{0,12},{2,14},{4,0},{6,2},{8,4},{10,6},{12,8},{14,10},{1,13},{3,15... | collective-permute-start | bytes 135176 | tf_op jit(solution)/shard_map/ppermute | solution.py:484
  8.3 1.6 %collective-permute-start.1 = (f32[88,128]{1,0:T(8,128)S(1)}, f32[88,128]{1,0:T(8,128)S(1)}, u32[]{:S(2)}, u32[]{:S(2)}) collective-permute-start(f32[88,128]{1,0:T(8,128)S(1)} %pack.1.refs_0_), channel_id=1, source_target_pairs={{0,4},{2,6},{4,8},{6,10},{8,12},{10,14},{12,0},{14,2},{1,5},{3,7},... | collective-permute-start | bytes 135176 | tf_op jit(solution)/shard_map/ppermute | solution.py:484
  9.9 0.0 collective-permute-start
  9.9 4.0 %collective-permute-done.refs_1_ = f32[88,128]{1,0:T(8,128)S(1)} collective-permute-done((f32[88,128]{1,0:T(8,128)S(1)}, f32[88,128]{1,0:T(8,128)S(1)}, u32[]{:S(2)}, u32[]{:S(2)}) %collective-permute-start) | collective-permute-done | bytes 45088 | tf_op jit(solution)/shard_map/ppermute | solution.py:486
  14.0 0.1 slice_select_fusion
  14.0 0.0 collective-permute-start.5
  14.1 2.3 %collective-permute-start.4 = (f32[40,128]{1,0:T(8,128)S(1)}, f32[40,128]{1,0:T(8,128)S(1)}, u32[]{:S(2)}, u32[]{:S(2)}) collective-permute-start(f32[40,128]{1,0:T(8,128)S(1)} %slice.20), channel_id=1, source_target_pairs={{0,12},{2,6},{4,0},{6,10},{8,4},{10,14},{12,8},{14,2},{1,13},{3,7}... | collective-permute-start | bytes 61448 | tf_op jit(solution)/shard_map/ppermute | solution.py:484
  16.4 0.0 collective-permute-done.3.refs_4_
  16.4 0.0 collective-permute-done.2.refs_3_
  16.4 0.0 collective-permute-done.1.refs_2_
  16.4 0.8 %shard_map.86 = (f32[32,128]{1,0:T(8,128)S(1)}, f32[32,128]{1,0:T(8,128)S(1)}, f32[32,128]{1,0:T(8,128)S(1)}) custom-call(f32[88,128]{1,0:T(8,128)S(1)} %pack.1.refs_0_, f32[88,128]{1,0:T(8,128)S(1)} %collective-permute-done.refs_1_, f32[88,128]{1,0:T(8,128)S(1)} %collective-permute-done.1.refs_2_, f32[88,128]{1,0:T(8,128)S(1)} %collective-permute-done.2.refs_3_, ...), custom_call_target="tpu_custom_call" | custom-call | flops 1000000 | bytes 262144 | tf_op jit(solution)/shard_map/pallas_call | solution.py:449
  17.3 0.0 copy-start
  17.3 0.1 collective-permute-start.6
  17.4 1.2 %collective-permute-done.6.refs_9_ = f32[32,128]{1,0:T(8,128)S(1)} collective-permute-done((f32[32,128]{1,0:T(8,128)S(1)}, f32[32,128]{1,0:T(8,128)S(1)}, u32[]{:S(2)}, u32[]{:S(2)}) %collective-permute-start.6) | collective-permute-done | bytes 16416 | tf_op jit(solution)/shard_map/ppermute | solution.py:509
  18.5 0.5 %collective-permute-done.4.refs_5_ = f32[40,128]{1,0:T(8,128)S(1)} collective-permute-done((f32[40,128]{1,0:T(8,128)S(1)}, f32[40,128]{1,0:T(8,128)S(1)}, u32[]{:S(2)}, u32[]{:S(2)}) %collective-permute-start.4) | collective-permute-done | bytes 20512 | tf_op jit(solution)/shard_map/ppermute | solution.py:484
  19.0 0.0 collective-permute-done.5.refs_6_
  19.0 0.0 copy-done
  19.0 1.0 %shard_map.87 = (f32[4,4,16,16]{3,2,1,0:T(8,128)}, f32[4,4,16,16]{3,2,1,0:T(8,128)}) custom-call(f32[88,128]{1,0:T(8,128)S(1)} %pack.1.refs_0_, f32[88,128]{1,0:T(8,128)S(1)} %collective-permute-done.refs_1_, f32[88,128]{1,0:T(8,128)S(1)} %collective-permute-done.1.refs_2_, f32[88,128]{1,0:T(8,128)S(1)} %collective-permute-done.2.refs_3_, ...), custom_call_target="tpu_custom_call" | custom-call | flops 1000000 | bytes 262144 | tf_op jit(solution)/shard_map/pallas_call | solution.py:449
  (5 shorter events, 0.0 us)
Async XLA Ops:
  1.8 14.6 %collective-permute-start.3 = (f32[88,128]{1,0:T(8,128)S(1)}, f32[88,128]{1,0:T(8,128)S(1)}, u32[]{:S(2)}, u32[]{:S(2)}) collective-permute-start(f32[88,128]{1,0:T(8,128)S(1)} %pack.1.refs_0_), channel_id=1, source_target_pairs={{0,14},{2,4},{4,2},{6,8},{8,6},{10,12},{12,10},{14,0},{1,15},{3,5}... | collective-permute-start | bytes 135176 | tf_op jit(solution)/shard_map/ppermute | solution.py:492
  7.9 8.5 %collective-permute-start.2 = (f32[88,128]{1,0:T(8,128)S(1)}, f32[88,128]{1,0:T(8,128)S(1)}, u32[]{:S(2)}, u32[]{:S(2)}) collective-permute-start(f32[88,128]{1,0:T(8,128)S(1)} %pack.1.refs_0_), channel_id=1, source_target_pairs={{0,12},{2,14},{4,0},{6,2},{8,4},{10,6},{12,8},{14,10},{1,13},{3,15... | collective-permute-start | bytes 135176 | tf_op jit(solution)/shard_map/ppermute | solution.py:484
  8.3 8.1 %collective-permute-start.1 = (f32[88,128]{1,0:T(8,128)S(1)}, f32[88,128]{1,0:T(8,128)S(1)}, u32[]{:S(2)}, u32[]{:S(2)}) collective-permute-start(f32[88,128]{1,0:T(8,128)S(1)} %pack.1.refs_0_), channel_id=1, source_target_pairs={{0,4},{2,6},{4,8},{6,10},{8,12},{10,14},{12,0},{14,2},{1,5},{3,7},... | collective-permute-start | bytes 135176 | tf_op jit(solution)/shard_map/ppermute | solution.py:484
  9.9 4.0 %collective-permute-start = (f32[88,128]{1,0:T(8,128)S(1)}, f32[88,128]{1,0:T(8,128)S(1)}, u32[]{:S(2)}, u32[]{:S(2)}) collective-permute-start(f32[88,128]{1,0:T(8,128)S(1)} %pack.1.refs_0_), channel_id=1, source_target_pairs={{0,2},{2,0},{4,6},{6,4},{8,10},{10,8},{12,14},{14,12},{1,3},{3,1},... | collective-permute-start | bytes 135176 | tf_op jit(solution)/shard_map/ppermute | solution.py:486
  14.0 5.0 %collective-permute-start.5 = (f32[72,128]{1,0:T(8,128)S(1)}, f32[72,128]{1,0:T(8,128)S(1)}, u32[]{:S(2)}, u32[]{:S(2)}) collective-permute-start(f32[72,128]{1,0:T(8,128)S(1)} %pad_maximum_fusion), channel_id=1, source_target_pairs={{0,8},{2,10},{4,12},{6,14},{8,0},{10,2},{12,4},{14,6},{1,9},{3,11}... | collective-permute-start | bytes 110600 | tf_op jit(solution)/shard_map/ppermute | solution.py:484
  14.1 4.9 %collective-permute-start.4 = (f32[40,128]{1,0:T(8,128)S(1)}, f32[40,128]{1,0:T(8,128)S(1)}, u32[]{:S(2)}, u32[]{:S(2)}) collective-permute-start(f32[40,128]{1,0:T(8,128)S(1)} %slice.20), channel_id=1, source_target_pairs={{0,12},{2,6},{4,0},{6,10},{8,4},{10,14},{12,8},{14,2},{1,13},{3,7}... | collective-permute-start | bytes 61448 | tf_op jit(solution)/shard_map/ppermute | solution.py:484
  17.3 1.8 %copy-start = (f32[4,16]{1,0:T(4,128)S(1)}, f32[4,16]{1,0:T(4,128)}, u32[]{:S(2)}) copy-start(f32[4,16]{1,0:T(4,128)} %refs_10_.1) | copy-start | bytes 772
  17.3 1.2 %collective-permute-start.6 = (f32[32,128]{1,0:T(8,128)S(1)}, f32[32,128]{1,0:T(8,128)S(1)}, u32[]{:S(2)}, u32[]{:S(2)}) collective-permute-start(f32[32,128]{1,0:T(8,128)S(1)} %get-tuple-element.7), channel_id=1, source_target_pairs={{0,1},{1,0},{2,3},{3,2},{4,5},{5,4},{6,7},{7,6},{8,9},{9,8},{10,11... | collective-permute-start | bytes 49160 | tf_op jit(solution)/shard_map/ppermute | solution.py:509

commit v8 on v6

--- a/solution.py
+++ b/solution.py
@@ -275,8 +275,8 @@
             for s in range(wins):
                 put(i, s * halves + half, dual_ref[i, s, rows, :])
                 put(lons + i, s * halves + half, inc_ref[i, s, rows, :])
-            put(2 * lons, i * halves + half, u_ref[i, rows, :])
-            put(2 * lons + 1, i * halves + half, v_ref[i, rows, :])
+            put(2 * lons, i * halves + half, 0.5 * u_ref[i, rows, :])
+            put(2 * lons + 1, i * halves + half, 0.5 * v_ref[i, rows, :])
     main_ref[:SUB, :] = jnp.zeros((SUB, LANES), jnp.float32)
     for i in range(lons):
         mixing = 0.15 + 0.09 * land_ref[i : i + 1, :].astype(jnp.float32)
@@ -307,8 +307,8 @@
     for r in range(lons + 2 * STEPS):
         offset, i = (r - STEPS) // lons, (r - STEPS) % lons
         spot = i * group + lane % group
-        wind_u = 0.5 * picked(rows(offset, 2 * lons), spot)
-        wind_v = 0.5 * picked(rows(offset, 2 * lons + 1), spot)
+        wind_u = picked(rows(offset, 2 * lons), spot)
+        wind_v = picked(rows(offset, 2 * lons + 1), spot)
         mixing = picked(rows(offset, -1), i * lats + lat)
         coeff_ref[r, 0] = 1.0 - 4.0 * mixing
         coeff_ref[r, 1] = mixing - wind_u

time: 20.3 us -> 20.3 us (level)
  no operation moved by 1% of the time
where the time goes in v8:
time: 20.3 us; the launch traced here: 20.1 us
  starting transfers between devices  10.5 us (52%)
  waiting for transfers between devices  5.71 us (28%)
  Pallas kernels  3.08 us (15%)
  between operations  0.7 us (3%)
    ppermute x1, starting transfers between devices, dense_body(): lax.ppermute(main, 'tiles', [(t, (t + 1 if t % 2 else t - 1) % tiles) for...  6.07 us
    ppermute x4, starting transfers between devices, moved(): return lax.ppermute(x, 'tiles', pairs)  4.38 us
    ppermute x1, waiting for transfers between devices, dense_body(): peer = lax.ppermute(main, 'tiles', [(t, t ^ 1) for t in range(tiles)])  4.03 us
    pallas_call x3, Pallas kernels, kernel_call(): pl.pallas_call(kernel, out_shape=outputs, in_specs=[vmem] * len(inputs),...  1.91 us
    ppermute x4, waiting for transfers between devices, moved(): return lax.ppermute(x, 'tiles', pairs)  1.67 us
    pallas_call x1, Pallas kernels, dense_body(): pl.pallas_call(pack_kernel, out_shape=rows(2 * lons + 3), in_specs=[pl.Bl...  1.17 us
  transfers between devices with their start and end apart: 7, of which 2 were waited for; matrix products, arithmetic and copies ran while one was open for 0% of the time, Pallas kernels for 5%

profile of v8, /device:TPU:0, one launch (start us, length us, event | category | flops | bytes accessed | tf_op | source)
XLA Modules:
  0.0 20.1 jit_solution(11021153482249315787)
XLA Ops:
  0.6 1.2 %pack.1.refs_0_ = f32[88,128]{1,0:T(8,128)S(1)} custom-call(f32[4,4,16,16]{3,2,1,0:T(8,128)} %refs_0_.1, f32[4,4,16,16]{3,2,1,0:T(8,128)} %refs_1_.1, f32[4,16,16]{2,1,0:T(8,128)} %refs_2_.1, f32[4,16,16]{2,1,0:T(8,128)} %refs_3_.1, s32[4,16]{1,0:T(4,128)} %refs_4_.1, f32[2,4]{1,0:T(2,128)} %bitcast.1), custom_call_target="tpu_custom_call" | custom-call | tf_op jit(solution)/shard_map/pack/pallas_call | solution.py:470
  1.8 6.1 %collective-permute-start.3 = (f32[88,128]{1,0:T(8,128)S(1)}, f32[88,128]{1,0:T(8,128)S(1)}, u32[]{:S(2)}, u32[]{:S(2)}) collective-permute-start(f32[88,128]{1,0:T(8,128)S(1)} %pack.1.refs_0_), channel_id=1, source_target_pairs={{0,14},{2,4},{4,2},{6,8},{8,6},{10,12},{12,10},{14,0},{1,15},{3,5}... | collective-permute-start | bytes 135176 | tf_op jit(solution)/shard_map/ppermute | solution.py:491
  7.9 0.4 %collective-permute-start.2 = (f32[88,128]{1,0:T(8,128)S(1)}, f32[88,128]{1,0:T(8,128)S(1)}, u32[]{:S(2)}, u32[]{:S(2)}) collective-permute-start(f32[88,128]{1,0:T(8,128)S(1)} %pack.1.refs_0_), channel_id=1, source_target_pairs={{0,12},{2,14},{4,0},{6,2},{8,4},{10,6},{12,8},{14,10},{1,13},{3,15... | collective-permute-start | bytes 135176 | tf_op jit(solution)/shard_map/ppermute | solution.py:483
  8.3 1.6 %collective-permute-start.1 = (f32[88,128]{1,0:T(8,128)S(1)}, f32[88,128]{1,0:T(8,128)S(1)}, u32[]{:S(2)}, u32[]{:S(2)}) collective-permute-start(f32[88,128]{1,0:T(8,128)S(1)} %pack.1.refs_0_), channel_id=1, source_target_pairs={{0,4},{2,6},{4,8},{6,10},{8,12},{10,14},{12,0},{14,2},{1,5},{3,7},... | collective-permute-start | bytes 135176 | tf_op jit(solution)/shard_map/ppermute | solution.py:483
  9.9 0.0 collective-permute-start
  9.9 4.0 %collective-permute-done.refs_1_ = f32[88,128]{1,0:T(8,128)S(1)} collective-permute-done((f32[88,128]{1,0:T(8,128)S(1)}, f32[88,128]{1,0:T(8,128)S(1)}, u32[]{:S(2)}, u32[]{:S(2)}) %collective-permute-start) | collective-permute-done | bytes 45088 | tf_op jit(solution)/shard_map/ppermute | solution.py:485
  14.0 0.1 slice_select_fusion
  14.0 0.0 collective-permute-start.6
  14.1 2.3 %collective-permute-start.5 = (f32[40,128]{1,0:T(8,128)S(1)}, f32[40,128]{1,0:T(8,128)S(1)}, u32[]{:S(2)}, u32[]{:S(2)}) collective-permute-start(f32[40,128]{1,0:T(8,128)S(1)} %slice.20), channel_id=1, source_target_pairs={{0,12},{2,6},{4,0},{6,10},{8,4},{10,14},{12,8},{14,2},{1,13},{3,7}... | collective-permute-start | bytes 61448 | tf_op jit(solution)/shard_map/ppermute | solution.py:483
  16.4 0.0 collective-permute-done.3.refs_4_
  16.4 0.0 collective-permute-done.2.refs_3_
  16.4 0.0 collective-permute-done.1.refs_2_
  16.4 0.0 copy-start
  16.4 0.8 %shard_map.86 = (f32[32,128]{1,0:T(8,128)S(1)}, f32[32,128]{1,0:T(8,128)S(1)}, f32[32,128]{1,0:T(8,128)S(1)}) custom-call(f32[88,128]{1,0:T(8,128)S(1)} %pack.1.refs_0_, f32[88,128]{1,0:T(8,128)S(1)} %collective-permute-done.refs_1_, f32[88,128]{1,0:T(8,128)S(1)} %collective-permute-done.1.refs_2_, f32[88,128]{1,0:T(8,128)S(1)} %collective-permute-done.2.refs_3_, ...), custom_call_target="tpu_custom_call" | custom-call | flops 1000000 | bytes 262144 | tf_op jit(solution)/shard_map/pallas_call | solution.py:448
  17.3 0.1 collective-permute-start.4
  17.4 1.7 %collective-permute-done.5.refs_5_ = f32[40,128]{1,0:T(8,128)S(1)} collective-permute-done((f32[40,128]{1,0:T(8,128)S(1)}, f32[40,128]{1,0:T(8,128)S(1)}, u32[]{:S(2)}, u32[]{:S(2)}) %collective-permute-start.5) | collective-permute-done | bytes 20512 | tf_op jit(solution)/shard_map/ppermute | solution.py:483
  19.0 0.0 collective-permute-done.6.refs_6_
  19.0 0.0 copy-done
  19.0 0.2 shard_map.87.refs_4_
  19.2 0.0 collective-permute-done.4.refs_3_
  19.2 0.9 %shard_map.88 = (f32[4,4,16,16]{3,2,1,0:T(8,128)}, f32[4,4,16,16]{3,2,1,0:T(8,128)}) custom-call(f32[88,128]{1,0:T(8,128)S(1)} %pack.1.refs_0_, f32[32,128]{1,0:T(8,128)S(1)} %get-tuple-element.5.refs_1_, f32[32,128]{1,0:T(8,128)S(1)} %get-tuple-element.6.refs_2_, f32[32,128]{1,0:T(8,128)S(1)} %collective-permute-done.4.refs_3_, f32[32,128]{1,0:T(8,128)S(1)} %shard_map.87.refs_4_), custom_call_target="tpu_custom_call" | custom-call | flops 1000000 | bytes 262144 | tf_op jit(solution)/shard_map/pallas_call | solution.py:448
  (5 shorter events, 0.0 us)
Async XLA Ops:
  1.8 14.6 %collective-permute-start.3 = (f32[88,128]{1,0:T(8,128)S(1)}, f32[88,128]{1,0:T(8,128)S(1)}, u32[]{:S(2)}, u32[]{:S(2)}) collective-permute-start(f32[88,128]{1,0:T(8,128)S(1)} %pack.1.refs_0_), channel_id=1, source_target_pairs={{0,14},{2,4},{4,2},{6,8},{8,6},{10,12},{12,10},{14,0},{1,15},{3,5}... | collective-permute-start | bytes 135176 | tf_op jit(solution)/shard_map/ppermute | solution.py:491
  7.9 8.5 %collective-permute-start.2 = (f32[88,128]{1,0:T(8,128)S(1)}, f32[88,128]{1,0:T(8,128)S(1)}, u32[]{:S(2)}, u32[]{:S(2)}) collective-permute-start(f32[88,128]{1,0:T(8,128)S(1)} %pack.1.refs_0_), channel_id=1, source_target_pairs={{0,12},{2,14},{4,0},{6,2},{8,4},{10,6},{12,8},{14,10},{1,13},{3,15... | collective-permute-start | bytes 135176 | tf_op jit(solution)/shard_map/ppermute | solution.py:483
  8.3 8.1 %collective-permute-start.1 = (f32[88,128]{1,0:T(8,128)S(1)}, f32[88,128]{1,0:T(8,128)S(1)}, u32[]{:S(2)}, u32[]{:S(2)}) collective-permute-start(f32[88,128]{1,0:T(8,128)S(1)} %pack.1.refs_0_), channel_id=1, source_target_pairs={{0,4},{2,6},{4,8},{6,10},{8,12},{10,14},{12,0},{14,2},{1,5},{3,7},... | collective-permute-start | bytes 135176 | tf_op jit(solution)/shard_map/ppermute | solution.py:483
  9.9 4.0 %collective-permute-start = (f32[88,128]{1,0:T(8,128)S(1)}, f32[88,128]{1,0:T(8,128)S(1)}, u32[]{:S(2)}, u32[]{:S(2)}) collective-permute-start(f32[88,128]{1,0:T(8,128)S(1)} %pack.1.refs_0_), channel_id=1, source_target_pairs={{0,2},{2,0},{4,6},{6,4},{8,10},{10,8},{12,14},{14,12},{1,3},{3,1},... | collective-permute-start | bytes 135176 | tf_op jit(solution)/shard_map/ppermute | solution.py:485
  14.0 5.0 %collective-permute-start.6 = (f32[72,128]{1,0:T(8,128)S(1)}, f32[72,128]{1,0:T(8,128)S(1)}, u32[]{:S(2)}, u32[]{:S(2)}) collective-permute-start(f32[72,128]{1,0:T(8,128)S(1)} %pad_maximum_fusion), channel_id=1, source_target_pairs={{0,8},{2,10},{4,12},{6,14},{8,0},{10,2},{12,4},{14,6},{1,9},{3,11}... | collective-permute-start | bytes 110600 | tf_op jit(solution)/shard_map/ppermute | solution.py:483
  14.1 4.9 %collective-permute-start.5 = (f32[40,128]{1,0:T(8,128)S(1)}, f32[40,128]{1,0:T(8,128)S(1)}, u32[]{:S(2)}, u32[]{:S(2)}) collective-permute-start(f32[40,128]{1,0:T(8,128)S(1)} %slice.20), channel_id=1, source_target_pairs={{0,12},{2,6},{4,0},{6,10},{8,4},{10,14},{12,8},{14,2},{1,13},{3,7}... | collective-permute-start | bytes 61448 | tf_op jit(solution)/shard_map/ppermute | solution.py:483
  16.4 2.6 %copy-start = (f32[4,16]{1,0:T(4,128)S(1)}, f32[4,16]{1,0:T(4,128)}, u32[]{:S(2)}) copy-start(f32[4,16]{1,0:T(4,128)} %refs_7_.1) | copy-start | bytes 772
  17.3 1.9 %collective-permute-start.4 = (f32[32,128]{1,0:T(8,128)S(1)}, f32[32,128]{1,0:T(8,128)S(1)}, u32[]{:S(2)}, u32[]{:S(2)}) collective-permute-start(f32[32,128]{1,0:T(8,128)S(1)} %get-tuple-element.7), channel_id=1, source_target_pairs={{0,1},{1,0},{2,3},{3,2},{4,5},{5,4},{6,7},{7,6},{8,9},{9,8},{10,11... | collective-permute-start | bytes 49160 | tf_op jit(solution)/shard_map/ppermute | solution.py:508

commit v9 on v7

--- a/solution.py
+++ b/solution.py
@@ -275,8 +275,8 @@
             for s in range(wins):
                 put(i, s * halves + half, dual_ref[i, s, rows, :])
                 put(lons + i, s * halves + half, inc_ref[i, s, rows, :])
-            put(2 * lons, i * halves + half, u_ref[i, rows, :])
-            put(2 * lons + 1, i * halves + half, v_ref[i, rows, :])
+            put(2 * lons, i * halves + half, 0.5 * u_ref[i, rows, :])
+            put(2 * lons + 1, i * halves + half, 0.5 * v_ref[i, rows, :])
     main_ref[:SUB, :] = jnp.zeros((SUB, LANES), jnp.float32)
     for i in range(lons):
         mixing = 0.15 + 0.09 * land_ref[i : i + 1, :].astype(jnp.float32)
@@ -307,8 +307,8 @@
     for r in range(lons + 2 * STEPS):
         offset, i = (r - STEPS) // lons, (r - STEPS) % lons
         spot = i * group + lane % group
-        wind_u = 0.5 * picked(rows(offset, 2 * lons), spot)
-        wind_v = 0.5 * picked(rows(offset, 2 * lons + 1), spot)
+        wind_u = picked(rows(offset, 2 * lons), spot)
+        wind_v = picked(rows(offset, 2 * lons + 1), spot)
         mixing = picked(rows(offset, -1), i * lats + lat)
         coeff_ref[r, 0] = 1.0 - 4.0 * mixing
         coeff_ref[r, 1] = mixing - wind_u

time: 20.1 us -> 20.1 us (level)
  no operation moved by 1% of the time
where the time goes in v9:
time: 20.1 us; the launch traced here: 20 us
  starting transfers between devices  10.5 us (52%)
  waiting for transfers between devices  5.71 us (28%)
  Pallas kernels  2.96 us (15%)
  between operations  0.69 us (3%)
    ppermute x1, starting transfers between devices, dense_body(): lax.ppermute(main, 'tiles', [(t, (t + 1 if t % 2 else t - 1) % tiles) for...  6.07 us
    ppermute x4, starting transfers between devices, moved(): return lax.ppermute(x, 'tiles', pairs)  4.38 us
    ppermute x1, waiting for transfers between devices, dense_body(): peer = lax.ppermute(main, 'tiles', [(t, t ^ 1) for t in range(tiles)])  4.03 us
    pallas_call x2, Pallas kernels, kernel_call(): pl.pallas_call(kernel, out_shape=outputs, in_specs=[vmem] * len(inputs),...  1.79 us
    pallas_call x1, Pallas kernels, dense_body(): pl.pallas_call(pack_kernel, out_shape=rows(2 * lons + 3), in_specs=[pl.Bl...  1.17 us
    ppermute x1, waiting for transfers between devices, dense_body(): swapped = lax.ppermute(edge, 'subwin', [(0, 1), (1, 0)])  1.17 us
    ppermute x4, waiting for transfers between devices, moved(): return lax.ppermute(x, 'tiles', pairs)  0.5 us
  transfers between devices with their start and end apart: 7, of which 3 were waited for; matrix products, arithmetic and copies ran while one was open for 0% of the time, Pallas kernels for 4%

profile of v9, /device:TPU:0, one launch (start us, length us, event | category | flops | bytes accessed | tf_op | source)
XLA Modules:
  0.0 20.0 jit_solution(15967380008151779989)
XLA Ops:
  0.6 1.2 %pack.1.refs_0_ = f32[88,128]{1,0:T(8,128)S(1)} custom-call(f32[4,4,16,16]{3,2,1,0:T(8,128)} %refs_0_.1, f32[4,4,16,16]{3,2,1,0:T(8,128)} %refs_1_.1, f32[4,16,16]{2,1,0:T(8,128)} %refs_2_.1, f32[4,16,16]{2,1,0:T(8,128)} %refs_3_.1, s32[4,16]{1,0:T(4,128)} %refs_4_.1, f32[2,4]{1,0:T(2,128)} %bitcast.1), custom_call_target="tpu_custom_call" | custom-call | tf_op jit(solution)/shard_map/pack/pallas_call | solution.py:471
  1.8 6.1 %collective-permute-start.3 = (f32[88,128]{1,0:T(8,128)S(1)}, f32[88,128]{1,0:T(8,128)S(1)}, u32[]{:S(2)}, u32[]{:S(2)}) collective-permute-start(f32[88,128]{1,0:T(8,128)S(1)} %pack.1.refs_0_), channel_id=1, source_target_pairs={{0,14},{2,4},{4,2},{6,8},{8,6},{10,12},{12,10},{14,0},{1,15},{3,5}... | collective-permute-start | bytes 135176 | tf_op jit(solution)/shard_map/ppermute | solution.py:492
  7.9 0.4 %collective-permute-start.2 = (f32[88,128]{1,0:T(8,128)S(1)}, f32[88,128]{1,0:T(8,128)S(1)}, u32[]{:S(2)}, u32[]{:S(2)}) collective-permute-start(f32[88,128]{1,0:T(8,128)S(1)} %pack.1.refs_0_), channel_id=1, source_target_pairs={{0,12},{2,14},{4,0},{6,2},{8,4},{10,6},{12,8},{14,10},{1,13},{3,15... | collective-permute-start | bytes 135176 | tf_op jit(solution)/shard_map/ppermute | solution.py:484
  8.3 1.6 %collective-permute-start.1 = (f32[88,128]{1,0:T(8,128)S(1)}, f32[88,128]{1,0:T(8,128)S(1)}, u32[]{:S(2)}, u32[]{:S(2)}) collective-permute-start(f32[88,128]{1,0:T(8,128)S(1)} %pack.1.refs_0_), channel_id=1, source_target_pairs={{0,4},{2,6},{4,8},{6,10},{8,12},{10,14},{12,0},{14,2},{1,5},{3,7},... | collective-permute-start | bytes 135176 | tf_op jit(solution)/shard_map/ppermute | solution.py:484
  9.9 0.0 collective-permute-start
  9.9 4.0 %collective-permute-done.refs_1_ = f32[88,128]{1,0:T(8,128)S(1)} collective-permute-done((f32[88,128]{1,0:T(8,128)S(1)}, f32[88,128]{1,0:T(8,128)S(1)}, u32[]{:S(2)}, u32[]{:S(2)}) %collective-permute-start) | collective-permute-done | bytes 45088 | tf_op jit(solution)/shard_map/ppermute | solution.py:486
  14.0 0.1 slice_select_fusion
  14.0 0.0 collective-permute-start.5
  14.1 2.3 %collective-permute-start.4 = (f32[40,128]{1,0:T(8,128)S(1)}, f32[40,128]{1,0:T(8,128)S(1)}, u32[]{:S(2)}, u32[]{:S(2)}) collective-permute-start(f32[40,128]{1,0:T(8,128)S(1)} %slice.20), channel_id=1, source_target_pairs={{0,12},{2,6},{4,0},{6,10},{8,4},{10,14},{12,8},{14,2},{1,13},{3,7}... | collective-permute-start | bytes 61448 | tf_op jit(solution)/shard_map/ppermute | solution.py:484
  16.4 0.0 collective-permute-done.3.refs_4_
  16.4 0.0 collective-permute-done.2.refs_3_
  16.4 0.0 collective-permute-done.1.refs_2_
  16.4 0.8 %shard_map.86 = (f32[32,128]{1,0:T(8,128)S(1)}, f32[32,128]{1,0:T(8,128)S(1)}, f32[32,128]{1,0:T(8,128)S(1)}) custom-call(f32[88,128]{1,0:T(8,128)S(1)} %pack.1.refs_0_, f32[88,128]{1,0:T(8,128)S(1)} %collective-permute-done.refs_1_, f32[88,128]{1,0:T(8,128)S(1)} %collective-permute-done.1.refs_2_, f32[88,128]{1,0:T(8,128)S(1)} %collective-permute-done.2.refs_3_, ...), custom_call_target="tpu_custom_call" | custom-call | flops 1000000 | bytes 262144 | tf_op jit(solution)/shard_map/pallas_call | solution.py:449
  17.3 0.0 copy-start
  17.3 0.1 collective-permute-start.6
  17.4 1.2 %collective-permute-done.6.refs_9_ = f32[32,128]{1,0:T(8,128)S(1)} collective-permute-done((f32[32,128]{1,0:T(8,128)S(1)}, f32[32,128]{1,0:T(8,128)S(1)}, u32[]{:S(2)}, u32[]{:S(2)}) %collective-permute-start.6) | collective-permute-done | bytes 16416 | tf_op jit(solution)/shard_map/ppermute | solution.py:509
  18.5 0.5 %collective-permute-done.4.refs_5_ = f32[40,128]{1,0:T(8,128)S(1)} collective-permute-done((f32[40,128]{1,0:T(8,128)S(1)}, f32[40,128]{1,0:T(8,128)S(1)}, u32[]{:S(2)}, u32[]{:S(2)}) %collective-permute-start.4) | collective-permute-done | bytes 20512 | tf_op jit(solution)/shard_map/ppermute | solution.py:484
  19.0 0.0 collective-permute-done.5.refs_6_
  19.0 0.0 copy-done
  19.0 1.0 %shard_map.87 = (f32[4,4,16,16]{3,2,1,0:T(8,128)}, f32[4,4,16,16]{3,2,1,0:T(8,128)}) custom-call(f32[88,128]{1,0:T(8,128)S(1)} %pack.1.refs_0_, f32[88,128]{1,0:T(8,128)S(1)} %collective-permute-done.refs_1_, f32[88,128]{1,0:T(8,128)S(1)} %collective-permute-done.1.refs_2_, f32[88,128]{1,0:T(8,128)S(1)} %collective-permute-done.2.refs_3_, ...), custom_call_target="tpu_custom_call" | custom-call | flops 1000000 | bytes 262144 | tf_op jit(solution)/shard_map/pallas_call | solution.py:449
  (5 shorter events, 0.0 us)
Async XLA Ops:
  1.8 14.6 %collective-permute-start.3 = (f32[88,128]{1,0:T(8,128)S(1)}, f32[88,128]{1,0:T(8,128)S(1)}, u32[]{:S(2)}, u32[]{:S(2)}) collective-permute-start(f32[88,128]{1,0:T(8,128)S(1)} %pack.1.refs_0_), channel_id=1, source_target_pairs={{0,14},{2,4},{4,2},{6,8},{8,6},{10,12},{12,10},{14,0},{1,15},{3,5}... | collective-permute-start | bytes 135176 | tf_op jit(solution)/shard_map/ppermute | solution.py:492
  7.9 8.5 %collective-permute-start.2 = (f32[88,128]{1,0:T(8,128)S(1)}, f32[88,128]{1,0:T(8,128)S(1)}, u32[]{:S(2)}, u32[]{:S(2)}) collective-permute-start(f32[88,128]{1,0:T(8,128)S(1)} %pack.1.refs_0_), channel_id=1, source_target_pairs={{0,12},{2,14},{4,0},{6,2},{8,4},{10,6},{12,8},{14,10},{1,13},{3,15... | collective-permute-start | bytes 135176 | tf_op jit(solution)/shard_map/ppermute | solution.py:484
  8.3 8.1 %collective-permute-start.1 = (f32[88,128]{1,0:T(8,128)S(1)}, f32[88,128]{1,0:T(8,128)S(1)}, u32[]{:S(2)}, u32[]{:S(2)}) collective-permute-start(f32[88,128]{1,0:T(8,128)S(1)} %pack.1.refs_0_), channel_id=1, source_target_pairs={{0,4},{2,6},{4,8},{6,10},{8,12},{10,14},{12,0},{14,2},{1,5},{3,7},... | collective-permute-start | bytes 135176 | tf_op jit(solution)/shard_map/ppermute | solution.py:484
  9.9 4.0 %collective-permute-start = (f32[88,128]{1,0:T(8,128)S(1)}, f32[88,128]{1,0:T(8,128)S(1)}, u32[]{:S(2)}, u32[]{:S(2)}) collective-permute-start(f32[88,128]{1,0:T(8,128)S(1)} %pack.1.refs_0_), channel_id=1, source_target_pairs={{0,2},{2,0},{4,6},{6,4},{8,10},{10,8},{12,14},{14,12},{1,3},{3,1},... | collective-permute-start | bytes 135176 | tf_op jit(solution)/shard_map/ppermute | solution.py:486
  14.0 5.0 %collective-permute-start.5 = (f32[72,128]{1,0:T(8,128)S(1)}, f32[72,128]{1,0:T(8,128)S(1)}, u32[]{:S(2)}, u32[]{:S(2)}) collective-permute-start(f32[72,128]{1,0:T(8,128)S(1)} %pad_maximum_fusion), channel_id=1, source_target_pairs={{0,8},{2,10},{4,12},{6,14},{8,0},{10,2},{12,4},{14,6},{1,9},{3,11}... | collective-permute-start | bytes 110600 | tf_op jit(solution)/shard_map/ppermute | solution.py:484
  14.1 4.9 %collective-permute-start.4 = (f32[40,128]{1,0:T(8,128)S(1)}, f32[40,128]{1,0:T(8,128)S(1)}, u32[]{:S(2)}, u32[]{:S(2)}) collective-permute-start(f32[40,128]{1,0:T(8,128)S(1)} %slice.20), channel_id=1, source_target_pairs={{0,12},{2,6},{4,0},{6,10},{8,4},{10,14},{12,8},{14,2},{1,13},{3,7}... | collective-permute-start | bytes 61448 | tf_op jit(solution)/shard_map/ppermute | solution.py:484
  17.3 1.8 %copy-start = (f32[4,16]{1,0:T(4,128)S(1)}, f32[4,16]{1,0:T(4,128)}, u32[]{:S(2)}) copy-start(f32[4,16]{1,0:T(4,128)} %refs_10_.1) | copy-start | bytes 772
  17.3 1.2 %collective-permute-start.6 = (f32[32,128]{1,0:T(8,128)S(1)}, f32[32,128]{1,0:T(8,128)S(1)}, u32[]{:S(2)}, u32[]{:S(2)}) collective-permute-start(f32[32,128]{1,0:T(8,128)S(1)} %get-tuple-element.7), channel_id=1, source_target_pairs={{0,1},{1,0},{2,3},{3,2},{4,5},{5,4},{6,7},{7,6},{8,9},{9,8},{10,11... | collective-permute-start | bytes 49160 | tf_op jit(solution)/shard_map/ppermute | solution.py:509
